TPU v7x, 256 devices: a whole 4x4x8 slice. The times are simulated.
256 devices in a mesh: ep: 256 (over z, y, x, core).
Axes of the slice: x: 4, y: 4, z: 8, core: 2. Of those that a mesh axis runs over, the one named last changes fastest.
Arguments:
- tokens: bfloat16 [8192, 256], P('ep')
- grad_out: bfloat16 [8192, 256], P('ep')
- expert_ids: int32 [8192, 2], P('ep')
- w_gate: bfloat16 [256, 256], replicated
- w_in: bfloat16 [256, 256, 1024], P('ep')
- w_out: bfloat16 [256, 1024, 256], P('ep')
Outputs:
- output 1: bfloat16 [8192, 256], P('ep')
- output 2: bfloat16 [8192, 256], P('ep')
- output 3: float32 [256, 256, 1024], P('ep')
- output 4: float32 [256, 1024, 256], P('ep')
- output 5: float32 [256, 256], replicated
All inputs are finite; a program needn't handle non-finite values.
Results may differ from a plain program's by a relative error of at most 0.00483969.
Values are sent between devices in bfloat16 or wider.
A program may use at most 768 MiB of HBM per device.

v0:
```python
import jax
import jax.numpy as jnp
from jax import lax
from jax.sharding import PartitionSpec as P


def route_slots(expert_ids, n_exp):
    flat_ids = expert_ids.reshape(-1)
    one_hot = (flat_ids[:, None] == jnp.arange(n_exp)[None, :]).astype(jnp.int32)
    rank_in = jnp.sum((jnp.cumsum(one_hot, axis=0) - one_hot) * one_hot, axis=1)
    return flat_ids, one_hot, rank_in


def slot_owner(dest_slot, n_slots):
    n_choice = dest_slot.shape[0]
    return jnp.full((n_slots,), n_choice, jnp.int32).at[dest_slot].set(jnp.arange(n_choice, dtype=jnp.int32), mode='drop')


def local_block(tokens, grad_out, expert_ids, w_gate, w_in, w_out):
    n_exp = w_gate.shape[1]
    tok_dev, d_model = tokens.shape
    cap_rows = tok_dev // 4
    n_choice = 2 * tok_dev
    n_slots = n_exp * cap_rows
    w_one = w_in[0]
    w_two = w_out[0]
    flat_ids, one_hot, rank_in = route_slots(expert_ids, n_exp)
    dest_slot = flat_ids * cap_rows + rank_in
    src_choice = slot_owner(dest_slot, n_slots)
    zero_row = jnp.zeros((1, d_model), jnp.bfloat16)
    x_table = jnp.concatenate([tokens, zero_row], axis=0)
    send_x = jnp.take(x_table, jnp.where(src_choice < n_choice, src_choice // 2, tok_dev), axis=0)
    recv_x = lax.all_to_all(send_x.reshape(n_exp, cap_rows, d_model), 'ep', 0, 0, tiled=True).reshape(n_slots, d_model)
    a_pre = jnp.dot(recv_x, w_one, preferred_element_type=jnp.float32)
    hidden, gelu_vjp = jax.vjp(jax.nn.gelu, a_pre)
    hid_b = hidden.astype(jnp.bfloat16)
    y_rows = jnp.dot(hid_b, w_two, preferred_element_type=jnp.float32).astype(jnp.bfloat16)
    y_back = lax.all_to_all(y_rows.reshape(n_exp, cap_rows, d_model), 'ep', 0, 0, tiled=True).reshape(n_slots, d_model)
    y_pair = jnp.take(y_back, dest_slot, axis=0).reshape(tok_dev, 2, d_model)
    logits = jnp.dot(tokens, w_gate, preferred_element_type=jnp.float32)
    choice_hot = one_hot.reshape(tok_dev, 2, n_exp) > 0
    sel_logit = jnp.sum(jnp.where(choice_hot, logits[:, None, :], 0.0), axis=-1)
    gate_val = jax.nn.softmax(sel_logit, axis=1)
    y_out = jnp.sum(gate_val[:, :, None] * y_pair.astype(jnp.float32), axis=1).astype(jnp.bfloat16)
    d_gate = jnp.einsum('tm,tkm->tk', grad_out, y_pair, preferred_element_type=jnp.float32)
    dy_flat = (gate_val[:, :, None] * grad_out[:, None, :].astype(jnp.float32)).astype(jnp.bfloat16).reshape(n_choice, d_model)
    send_dy = jnp.take(jnp.concatenate([dy_flat, zero_row], axis=0), src_choice, axis=0)
    recv_dy = lax.all_to_all(send_dy.reshape(n_exp, cap_rows, d_model), 'ep', 0, 0, tiled=True).reshape(n_slots, d_model)
    g_w_out = jnp.einsum('rh,rm->hm', hid_b, recv_dy, preferred_element_type=jnp.float32)
    d_hid = jnp.einsum('rm,hm->rh', recv_dy, w_two, preferred_element_type=jnp.float32)
    d_pre = gelu_vjp(d_hid)[0].astype(jnp.bfloat16)
    g_w_in = jnp.einsum('rm,rh->mh', recv_x, d_pre, preferred_element_type=jnp.float32)
    dx_rows = jnp.einsum('rh,mh->rm', d_pre, w_one, preferred_element_type=jnp.float32).astype(jnp.bfloat16)
    dx_back = lax.all_to_all(dx_rows.reshape(n_exp, cap_rows, d_model), 'ep', 0, 0, tiled=True).reshape(n_slots, d_model)
    dx_pair = jnp.take(dx_back, dest_slot, axis=0).reshape(tok_dev, 2, d_model)
    d_sel = gate_val * (d_gate - jnp.sum(gate_val * d_gate, axis=1, keepdims=True))
    d_logits = jnp.sum(jnp.where(choice_hot, d_sel[:, :, None], 0.0), axis=1).astype(jnp.bfloat16)
    grad_x = (jnp.sum(dx_pair.astype(jnp.float32), axis=1) + jnp.einsum('te,me->tm', d_logits, w_gate, preferred_element_type=jnp.float32)).astype(jnp.bfloat16)
    grad_w_gate = lax.psum(jnp.einsum('tm,te->me', tokens, d_logits, preferred_element_type=jnp.float32), 'ep')
    return y_out, grad_x, g_w_in[None], g_w_out[None], grad_w_gate


def solution(mesh):
    return jax.shard_map(local_block, mesh=mesh, in_specs=(P('ep'), P('ep'), P('ep'), P(), P('ep'), P('ep')), out_specs=(P('ep'), P('ep'), P('ep'), P('ep'), P()), check_vma=False)
```

profile of v0, /device:TPU:1, one launch (start us, length us, event | category | flops | bytes accessed | tf_op | source)
XLA Modules:
  0.0 465.7 jit_solution(2786856806860483553)
XLA Ops:
  7.2 0.0 copy-start
  7.2 0.7 broadcast_multiply_fusion
  7.9 0.8 copy.20
  8.7 0.1 copy.21
  8.8 0.1 mul.100
  8.9 0.1 eq.25
  9.0 0.1 fusion.19
  9.1 0.1 reduce_window_sum.11
  9.2 0.2 select_reduce_fusion.1
  9.4 0.8 scatter_custom_fusion
  10.2 0.1 broadcast_in_dim.81
  10.3 0.7 concatenate.6
  11.1 7.5 %gather_fusion = bf16[2048,256]{1,0:T(8,128)(2,1)S(1)} fusion(bf16[33,256]{1,0:T(8,128)(2,1)S(1)} %concatenate.6, s32[2048]{0:T(1024)S(1)} %get-tuple-element.28), kind=kCustom, calls=%fused_computation.2 | custom fusion | bytes 2105344 | tf_op jit(solution)/shard_map/jit(_take)/gather | solution.py:32
  18.6 0.4 bitcast_select_fusion.1
  19.0 45.7 %all_to_all.20 = bf16[256,8,256]{2,1,0:T(8,128)(2,1)S(1)} all-to-all(bf16[256,8,256]{2,1,0:T(8,128)(2,1)S(1)} %bitcast_select_fusion.1), channel_id=1, replica_groups=mesh['ep'=256] {'ep'}, dimensions={0} | all-to-all | bytes 2097152 | tf_op jit(solution)/shard_map/all_to_all | solution.py:33
  64.7 0.0 copy-done
  64.7 0.0 copy-start.6
  64.7 5.0 %multiply_convert_fusion = (bf16[2048,1024]{1,0:T(8,128)(2,1)S(1)}, f32[2048,1024]{1,0:T(8,128)}) fusion(bf16[1,256,1024]{2,1,0:T(8,128)(2,1)S(1)} %copy-done, bf16[256,8,256]{2,1,0:T(8,128)(2,1)S(1)} %all_to_all.20), kind=kOutput, calls=%fused_computation.14 | convolution fusion | flops 1092616192 | bytes 14155776 | tf_op jit(solution)/shard_map/dot_general | solution.py:34
  69.7 0.0 copy-start.8
  69.7 0.0 copy-start.4
  69.7 0.0 copy-start.2
  69.7 0.0 copy-start.5
  69.7 2.0 copy-done.8
  71.7 0.0 copy-done.6
  71.7 2.3 fusion.7
  73.9 6.7 %all-to-all-start.1 = ((bf16[256,8,256]{2,1,0:T(8,128)(2,1)}), bf16[256,8,256]{2,1,0:T(8,128)(2,1)S(1)}, u32[]{:S(2)}, u32[]{:S(2)}) async-start(bf16[256,8,256]{2,1,0:T(8,128)(2,1)} %fusion.7), calls=%async_computation.1 | async-start | bytes 2097152 | tf_op jit(solution)/shard_map/all_to_all | solution.py:38
  80.7 0.0 copy-done.4
  80.8 0.1 broadcast_in_dim.85
  80.9 0.0 copy-done.2
  80.9 0.0 copy-done.3
  80.9 0.1 fusion.36
  81.0 0.0 copy-done.5
  81.0 0.2 select_reduce_fusion.2
  81.3 29.5 %all-to-all-done.1 = bf16[256,8,256]{2,1,0:T(8,128)(2,1)S(1)} async-done(((bf16[256,8,256]{2,1,0:T(8,128)(2,1)}), bf16[256,8,256]{2,1,0:T(8,128)(2,1)S(1)}, u32[]{:S(2)}, u32[]{:S(2)}) %all-to-all-start.1) | async-done | bytes 1048608 | tf_op jit(solution)/shard_map/all_to_all | solution.py:38
  110.8 0.7 gather_fusion.2
  111.5 0.1 broadcast_select_fusion
  111.6 0.1 fusion.20
  111.8 0.1 copy.25
  111.9 0.1 copy.19
  112.0 0.1 div.31
  112.1 0.1 multiply_convert_fusion.1
  112.2 7.5 %gather_fusion.1 = bf16[2048,256]{1,0:T(8,128)(2,1)S(1)} fusion(bf16[65,256]{1,0:T(8,128)(2,1)S(1)} %concatenate.7, s32[2048]{0:T(1024)S(1)} %get-tuple-element.27), kind=kCustom, calls=%fused_computation.3 | custom fusion | bytes 2105344 | tf_op jit(solution)/shard_map/jit(_take)/gather | solution.py:47
  119.7 0.4 bitcast_select_fusion
  120.1 36.7 %all_to_all.21 = bf16[256,8,256]{2,1,0:T(8,128)(2,1)S(1)} all-to-all(bf16[256,8,256]{2,1,0:T(8,128)(2,1)S(1)} %bitcast_select_fusion), channel_id=1, replica_groups=mesh['ep'=256] {'ep'}, dimensions={0} | all-to-all | bytes 2097152 | tf_op jit(solution)/shard_map/all_to_all | solution.py:48
  156.9 8.5 %fusion.6 = bf16[2048,1024]{1,0:T(8,128)(2,1)S(1)} fusion(f32[2048,1024]{1,0:T(8,128)} %get-tuple-element.30, bf16[256,8,256]{2,1,0:T(8,128)(2,1)S(1)} %all_to_all.21, bf16[1,1024,256]{2,1,0:T(8,128)(2,1)S(1)} %copy-done.6), kind=kOutput, calls=%fused_computation.13 | convolution fusion | flops 1115684864 | bytes 14155776 | tf_op jit(solution)/shard_map/rm,hm->rh/dot_general | solution.py:50
  165.4 0.0 copy-done.1
  165.4 0.0 copy-start.7
  165.4 1.9 copy-done.7
  167.3 2.3 fusion.8
  169.6 6.7 %all-to-all-start.3 = ((bf16[256,8,256]{2,1,0:T(8,128)(2,1)}), bf16[256,8,256]{2,1,0:T(8,128)(2,1)S(1)}, u32[]{:S(2)}, u32[]{:S(2)}) async-start(bf16[256,8,256]{2,1,0:T(8,128)(2,1)} %fusion.8), calls=%async_computation.3 | async-start | bytes 2097152 | tf_op jit(solution)/shard_map/all_to_all | solution.py:54
  176.4 0.0 all-reduce.4.cloned.1.call-start
  176.5 0.1 select_reduce_fusion
  176.5 0.9 convolution_bitcast_fusion.2
  177.5 0.0 all-reduce.4.cloned.1.call-update
  177.5 0.8 multiply_reduce_fusion
  178.2 267.9 %all-reduce.4.cloned.1.call-done = f32[256,256]{0,1:T(8,128)} async-done(((f32[256,256]{0,1:T(8,128)}), f32[256,256]{0,1:T(8,128)}) %all-reduce.4.cloned.1.call-update) | async-done | bytes 262160 | tf_op jit(solution)/shard_map/psum | solution.py:59
  446.2 1.8 copy.23
  447.9 4.4 convolution_bitcast_fusion.1
  452.4 4.7 %convolution_bitcast_fusion = f32[1,1024,256]{2,1,0:T(8,128)} fusion(bf16[2048,1024]{1,0:T(8,128)(2,1)} %copy-done.8, bf16[256,8,256]{2,1,0:T(8,128)(2,1)} %copy-done.1), kind=kOutput, calls=%fused_computation.19 | convolution fusion | flops 1073741824 | bytes 6291456 | tf_op jit(solution)/shard_map/rh,rm->hm/dot_general | solution.py:49
  457.1 0.0 all-to-all-done.3
  457.1 0.7 gather_fusion.3
  457.8 0.1 select_convert_fusion
  457.9 0.1 reduce_sum.70
  458.0 0.8 fusion.9
  (17 shorter events, 0.3 us)
Async XLA Ops:
  7.2 57.6 %copy-start = (bf16[1,256,1024]{2,1,0:T(8,128)(2,1)S(1)}, bf16[1,256,1024]{2,1,0:T(8,128)(2,1)}, u32[]{:S(2)}) copy-start(bf16[1,256,1024]{2,1,0:T(8,128)(2,1)} %param.12) | copy-start | bytes 1572868
  64.7 7.0 %copy-start.6 = (bf16[1,1024,256]{2,1,0:T(8,128)(2,1)S(1)}, bf16[1,1024,256]{2,1,0:T(8,128)(2,1)}, u32[]{:S(2)}) copy-start(bf16[1,1024,256]{2,1,0:T(8,128)(2,1)} %param.13) | copy-start | bytes 1572868
  69.7 2.0 copy-start.8
  69.7 11.0 %copy-start.4 = (bf16[32,256]{1,0:T(8,128)(2,1)S(1)}, bf16[32,256]{1,0:T(8,128)(2,1)}, u32[]{:S(2)}) copy-start(bf16[32,256]{1,0:T(8,128)(2,1)} %param.9) | copy-start | bytes 49156
  69.7 11.2 %copy-start.2 = (bf16[256,256]{1,0:T(8,128)(2,1)S(1)}, bf16[256,256]{1,0:T(8,128)(2,1)}, u32[]{:S(2)}) copy-start(bf16[256,256]{1,0:T(8,128)(2,1)} %param.11) | copy-start | bytes 393220
  69.7 11.2 %copy-start.3 = (bf16[32,256]{1,0:T(8,128)(2,1)S(1)}, bf16[32,256]{1,0:T(8,128)(2,1)}, u32[]{:S(2)}) copy-start(bf16[32,256]{1,0:T(8,128)(2,1)} %param.8) | copy-start | bytes 49156
  69.7 11.3 %copy-start.5 = (s32[32,2]{0,1:T(2,128)S(1)}, s32[32,2]{0,1:T(2,128)}, u32[]{:S(2)}) copy-start(s32[32,2]{0,1:T(2,128)} %param.10) | copy-start | bytes 772
  73.9 36.9 %all-to-all-start.1 = ((bf16[256,8,256]{2,1,0:T(8,128)(2,1)}), bf16[256,8,256]{2,1,0:T(8,128)(2,1)S(1)}, u32[]{:S(2)}, u32[]{:S(2)}) async-start(bf16[256,8,256]{2,1,0:T(8,128)(2,1)} %fusion.7), calls=%async_computation.1 | async-start | bytes 2097152 | tf_op jit(solution)/shard_map/all_to_all | solution.py:38
  156.9 8.5 %copy-start.1 = (bf16[256,8,256]{2,1,0:T(8,128)(2,1)}, bf16[256,8,256]{2,1,0:T(8,128)(2,1)S(1)}, u32[]{:S(2)}) copy-start(bf16[256,8,256]{2,1,0:T(8,128)(2,1)S(1)} %all_to_all.21) | copy-start | bytes 3145732
  165.4 1.9 copy-start.7
  169.6 287.5 %all-to-all-start.3 = ((bf16[256,8,256]{2,1,0:T(8,128)(2,1)}), bf16[256,8,256]{2,1,0:T(8,128)(2,1)S(1)}, u32[]{:S(2)}, u32[]{:S(2)}) async-start(bf16[256,8,256]{2,1,0:T(8,128)(2,1)} %fusion.8), calls=%async_computation.3 | async-start | bytes 2097152 | tf_op jit(solution)/shard_map/all_to_all | solution.py:54
  176.4 269.8 %all-reduce.4.cloned.1.call-start = ((), (), s32[]{:S(2)}) async-start(), calls=%async_computation.4 | async-start | bytes 524288 | tf_op jit(solution)/shard_map/psum | solution.py:59
Sparse Core Ops, SparseCore 0:
  183.2 262.8 all-reduce.3
where the time goes:
time: 467 us; the launch traced here: 466 us
  waiting for transfers between devices  297 us (64%)
  blocking collectives  82.4 us (18%)
  matrix products  29.2 us (6%)
  local copies, waits for them, and re-layouts  25.3 us (5%)
  between operations  14.3 us (3%)
  starting transfers between devices  13.5 us (3%)
    psum x1, waiting for transfers between devices, local_block(): lax.psum(jnp.einsum('tm,te->me', tokens, d_logits, preferred_element_type...  268 us
    all_to_all x1, blocking collectives, local_block(): lax.all_to_all(send_x.reshape(n_exp, cap_rows, d_model), 'ep', 0, 0, tile...  45.7 us
    all_to_all x1, blocking collectives, local_block(): lax.all_to_all(send_dy.reshape(n_exp, cap_rows, d_model), 'ep', 0, 0, til...  36.7 us
    all_to_all x1, waiting for transfers between devices, local_block(): lax.all_to_all(y_rows.reshape(n_exp, cap_rows, d_model), 'ep', 0, 0, tile...  29.5 us
  transfers between devices with their start and end apart: 3, of which 2 were waited for; matrix products, arithmetic and copies ran while one was open for 3% of the time, Pallas kernels for 0%

commit v1 on v0

--- a/solution.py
+++ b/solution.py
@@ -56,7 +56,10 @@
     d_sel = gate_val * (d_gate - jnp.sum(gate_val * d_gate, axis=1, keepdims=True))
     d_logits = jnp.sum(jnp.where(choice_hot, d_sel[:, :, None], 0.0), axis=1).astype(jnp.bfloat16)
     grad_x = (jnp.sum(dx_pair.astype(jnp.float32), axis=1) + jnp.einsum('te,me->tm', d_logits, w_gate, preferred_element_type=jnp.float32)).astype(jnp.bfloat16)
-    grad_w_gate = lax.psum(jnp.einsum('tm,te->me', tokens, d_logits, preferred_element_type=jnp.float32), 'ep')
+    d_slots = jnp.take(jnp.concatenate([d_sel.reshape(-1).astype(jnp.bfloat16), jnp.zeros((1,), jnp.bfloat16)]), src_choice, axis=0)
+    recv_d = lax.all_to_all(d_slots.reshape(n_exp, cap_rows), 'ep', 0, 0, tiled=True).reshape(1, n_slots)
+    gate_col = jnp.dot(recv_d, recv_x, preferred_element_type=jnp.float32)
+    grad_w_gate = lax.all_gather(gate_col, 'ep', axis=0, tiled=True).T
     return y_out, grad_x, g_w_in[None], g_w_out[None], grad_w_gate
 
 

time: 467 us -> 302 us (0.65)
  waiting for transfers between devices: 297 us -> 62.6 us
  blocking collectives: 82.4 us -> 136 us
  starting transfers between devices: 13.5 us -> 30.1 us
  between operations: 14.3 us -> 0.93 us
  local copies, waits for them, and re-layouts: 25.3 us -> 38.1 us
    psum x1 -> x0, waiting for transfers between devices: 268 us -> none  [local_block(): lax.psum(jnp.einsum('tm,te->me', tokens, d_logits, preferred_element_type...]
    all_gather x0 -> x1, blocking collectives: none -> 90.7 us  [local_block(): grad_w_gate = lax.all_gather(gate_col, 'ep', axis=0, tiled=True).T]
    all_to_all x1 -> x0, blocking collectives: 36.7 us -> none  [local_block(): lax.all_to_all(send_dy.reshape(n_exp, cap_rows, d_model), 'ep', 0, 0, til...]
    all_to_all x0 -> x2, waiting for transfers between devices: none -> 32.9 us  [the longest x1 29.2 us: local_block(): lax.all_to_all(send_dy.reshape(n_exp, cap_rows, d_model), 'ep', 0, 0, til...]
    all_to_all x0 -> x2, starting transfers between devices: none -> 13.3 us  [the longest x1 6.69 us: local_block(): lax.all_to_all(d_slots.reshape(n_exp, cap_rows), 'ep', 0, 0, tiled=True)]
    gather x0 -> x1, local copies, waits for them, and re-layouts: none -> 12.5 us  [local_block(): jnp.take(jnp.concatenate([d_sel.reshape(-1).astype(jnp.bfloat16), jnp.zer...]
  transfers between devices with their start and end apart: 3 -> 4, of which waited for: 2 -> 3; matrix products, arithmetic and copies ran while one was open for 3% -> 8% of each run, Pallas kernels for 0% -> 0%
where the time goes in v1:
time: 302 us; the launch traced here: 301 us
  blocking collectives  136 us (45%)
  waiting for transfers between devices  62.6 us (21%)
  local copies, waits for them, and re-layouts  38.1 us (13%)
  starting transfers between devices  30.1 us (10%)
  matrix products  28.4 us (9%)
  other arithmetic  4.65 us (2%)
    all_gather x1, blocking collectives, local_block(): grad_w_gate = lax.all_gather(gate_col, 'ep', axis=0, tiled=True).T  90.7 us
    all_to_all x1, blocking collectives, local_block(): lax.all_to_all(send_x.reshape(n_exp, cap_rows, d_model), 'ep', 0, 0, tile...  45.7 us
    all_to_all x1, waiting for transfers between devices, local_block(): lax.all_to_all(y_rows.reshape(n_exp, cap_rows, d_model), 'ep', 0, 0, tile...  29.7 us
    all_to_all x1, waiting for transfers between devices, local_block(): lax.all_to_all(send_dy.reshape(n_exp, cap_rows, d_model), 'ep', 0, 0, til...  29.2 us
    gather x1, local copies, waits for them, and re-layouts, local_block(): jnp.take(jnp.concatenate([d_sel.reshape(-1).astype(jnp.bfloat16), jnp.zer...  12.5 us
    all_to_all x1, starting transfers between devices, local_block(): lax.all_to_all(dx_rows.reshape(n_exp, cap_rows, d_model), 'ep', 0, 0, til...  10 us
    dot_general x1, matrix products, local_block(): jnp.einsum('rm,hm->rh', recv_dy, w_two, preferred_element_type=jnp.float32)  8.33 us
    gather x1, local copies, waits for them, and re-layouts, local_block(): jnp.take(jnp.concatenate([dy_flat, zero_row], axis=0), src_choice, axis=0)  7.5 us
  transfers between devices with their start and end apart: 4, of which 3 were waited for; matrix products, arithmetic and copies ran while one was open for 8% of the time, Pallas kernels for 0%

profile of v1, /device:TPU:1, one launch (start us, length us, event | category | flops | bytes accessed | tf_op | source)
XLA Modules:
  0.0 301.1 jit_solution(18044668982037990911)
XLA Ops:
  0.6 0.0 copy-start
  0.6 0.8 copy.24
  1.5 0.7 broadcast_multiply_fusion
  2.1 0.1 eq.25
  2.2 0.1 fusion.20
  2.3 0.1 reduce_window_sum.11
  2.4 0.2 select_reduce_fusion.1
  2.6 0.1 copy.25
  2.7 0.1 mul.100
  2.8 0.8 scatter_custom_fusion
  3.7 0.1 broadcast_in_dim.87
  3.8 0.7 concatenate.9
  4.5 7.5 %gather_fusion = bf16[2048,256]{1,0:T(8,128)(2,1)S(1)} fusion(bf16[33,256]{1,0:T(8,128)(2,1)S(1)} %concatenate.9, s32[2048]{0:T(1024)S(1)} %get-tuple-element.30), kind=kCustom, calls=%fused_computation.2 | custom fusion | bytes 2105344 | tf_op jit(solution)/shard_map/jit(_take)/gather | solution.py:32
  12.0 0.4 bitcast_select_fusion.1
  12.5 45.7 %all_to_all.26 = bf16[256,8,256]{2,1,0:T(8,128)(2,1)S(1)} all-to-all(bf16[256,8,256]{2,1,0:T(8,128)(2,1)S(1)} %bitcast_select_fusion.1), channel_id=1, replica_groups=mesh['ep'=256] {'ep'}, dimensions={0} | all-to-all | bytes 2097152 | tf_op jit(solution)/shard_map/all_to_all | solution.py:33
  58.2 0.0 copy-done
  58.2 5.0 %multiply_convert_fusion = (bf16[2048,1024]{1,0:T(8,128)(2,1)S(1)}, f32[2048,1024]{1,0:T(8,128)}) fusion(bf16[1,256,1024]{2,1,0:T(8,128)(2,1)S(1)} %copy-done, bf16[256,8,256]{2,1,0:T(8,128)(2,1)S(1)} %all_to_all.26), kind=kOutput, calls=%fused_computation.15 | convolution fusion | flops 1092616192 | bytes 14155776 | tf_op jit(solution)/shard_map/dot_general | solution.py:34
  63.2 0.0 copy-start.5
  63.2 2.0 copy-done.8
  65.2 0.0 copy-done.6
  65.2 2.3 fusion.7
  67.4 6.7 %all-to-all-start.1 = ((bf16[256,8,256]{2,1,0:T(8,128)(2,1)}), bf16[256,8,256]{2,1,0:T(8,128)(2,1)S(1)}, u32[]{:S(2)}, u32[]{:S(2)}) async-start(bf16[256,8,256]{2,1,0:T(8,128)(2,1)} %fusion.7), calls=%async_computation.1 | async-start | bytes 2097152 | tf_op jit(solution)/shard_map/all_to_all | solution.py:38
  74.1 0.0 copy-done.4
  74.2 0.1 fusion.38
  74.4 0.0 copy-done.5
  74.4 0.2 select_reduce_fusion.2
  74.6 29.7 %all-to-all-done.1 = bf16[256,8,256]{2,1,0:T(8,128)(2,1)S(1)} async-done(((bf16[256,8,256]{2,1,0:T(8,128)(2,1)}), bf16[256,8,256]{2,1,0:T(8,128)(2,1)S(1)}, u32[]{:S(2)}, u32[]{:S(2)}) %all-to-all-start.1) | async-done | bytes 1048608 | tf_op jit(solution)/shard_map/all_to_all | solution.py:38
  104.3 0.7 gather_fusion.3
  105.0 0.1 broadcast_select_fusion
  105.1 0.1 fusion.21
  105.2 0.1 copy.31
  105.4 0.1 copy.23
  105.4 0.1 copy.27
  105.6 0.1 convert_element_type.65
  105.7 0.1 pad_maximum_fusion
  105.8 12.5 %gather_fusion.2 = bf16[2048]{0:T(1024)(128)(2,1)S(1)} fusion(bf16[65]{0:T(256)(128)(2,1)S(1)} %pad_maximum_fusion, s32[2048]{0:T(1024)S(1)} %get-tuple-element.29), kind=kCustom, calls=%fused_computation.4 | custom fusion | bytes 16384 | tf_op jit(solution)/shard_map/jit(_take)/gather | solution.py:59
  118.3 0.1 broadcast_in_dim.91
  118.4 0.1 div.31
  118.5 0.1 multiply_convert_fusion.1
  118.6 7.5 %gather_fusion.1 = bf16[2048,256]{1,0:T(8,128)(2,1)S(1)} fusion(bf16[65,256]{1,0:T(8,128)(2,1)S(1)} %concatenate.10, s32[2048]{0:T(1024)S(1)} %get-tuple-element.29), kind=kCustom, calls=%fused_computation.3 | custom fusion | bytes 2105344 | tf_op jit(solution)/shard_map/jit(_take)/gather | solution.py:47
  126.1 1.2 bitcast_select_fusion
  127.3 6.6 %all-to-all-start.2 = ((bf16[256,8,256]{2,1,0:T(8,128)(2,1)}), bf16[256,8,256]{2,1,0:T(8,128)(2,1)S(1)}, u32[]{:S(2)}, u32[]{:S(2)}) async-start(bf16[256,8,256]{2,1,0:T(8,128)(2,1)} %bitcast_select_fusion), calls=%async_computation.2 | async-start | bytes 2097152 | tf_op jit(solution)/shard_map/all_to_all | solution.py:48
  134.0 0.8 select_n.86
  134.8 29.2 %all-to-all-done.2 = bf16[256,8,256]{2,1,0:T(8,128)(2,1)S(1)} async-done(((bf16[256,8,256]{2,1,0:T(8,128)(2,1)}), bf16[256,8,256]{2,1,0:T(8,128)(2,1)S(1)}, u32[]{:S(2)}, u32[]{:S(2)}) %all-to-all-start.2) | async-done | bytes 1048608 | tf_op jit(solution)/shard_map/all_to_all | solution.py:48
  164.0 6.7 %all-to-all-start.4 = ((bf16[256,1,8]{2,1,0:T(2,128)(2,1)}), bf16[256,1,8]{2,1,0:T(2,128)(2,1)S(1)}, u32[]{:S(2)}, u32[]{:S(2)}) async-start(bf16[256,1,8]{2,1,0:T(2,128)(2,1)} %select_n.86), calls=%async_computation.4 | async-start | bytes 262144 | tf_op jit(solution)/shard_map/all_to_all | solution.py:60
  170.7 8.3 %fusion.6 = bf16[2048,1024]{1,0:T(8,128)(2,1)S(1)} fusion(f32[2048,1024]{1,0:T(8,128)} %get-tuple-element.32, bf16[256,8,256]{2,1,0:T(8,128)(2,1)S(1)} %all-to-all-done.2, bf16[1,1024,256]{2,1,0:T(8,128)(2,1)} %param.13), kind=kOutput, calls=%fused_computation.14 | convolution fusion | flops 1115684864 | bytes 14155776 | tf_op jit(solution)/shard_map/rm,hm->rh/dot_general | solution.py:50
  179.1 1.9 copy-done.7
  181.0 2.3 fusion.8
  183.3 3.7 %all-to-all-done.4 = bf16[256,1,8]{2,1,0:T(2,128)(2,1)S(1)} async-done(((bf16[256,1,8]{2,1,0:T(2,128)(2,1)}), bf16[256,1,8]{2,1,0:T(2,128)(2,1)S(1)}, u32[]{:S(2)}, u32[]{:S(2)}) %all-to-all-start.4) | async-done | bytes 4128 | tf_op jit(solution)/shard_map/all_to_all | solution.py:60
  187.0 10.0 %all-to-all-start.3 = ((bf16[256,8,256]{2,1,0:T(8,128)(2,1)}), bf16[256,8,256]{2,1,0:T(8,128)(2,1)S(1)}, u32[]{:S(2)}, u32[]{:S(2)}) async-start(bf16[256,8,256]{2,1,0:T(8,128)(2,1)} %fusion.8), calls=%async_computation.3 | async-start | bytes 2097152 | tf_op jit(solution)/shard_map/all_to_all | solution.py:54
  197.1 0.1 select_reduce_fusion
  197.2 0.8 multiply_reduce_fusion
  197.9 0.4 reduce
  198.3 0.1 reshape.258
  198.4 0.2 convolution_bitcast_fusion.2
  198.7 90.7 %all-gather.1 = f32[256,1,256]{2,1,0:T(1,128)S(1)} all-gather(f32[1,1,256]{2,1,0:T(1,128)S(1)} %convolution_bitcast_fusion.2), channel_id=2, replica_groups=mesh['ep'=256] {'ep'}, dimensions={0}, use_global_device_ids=true | all-gather | bytes 263168 | tf_op jit(solution)/shard_map/all_gather | solution.py:62
  289.4 0.8 copy.33
  290.2 4.4 %convolution_bitcast_fusion.1 = f32[1,256,1024]{2,1,0:T(8,128)} fusion(bf16[2048,1024]{1,0:T(8,128)(2,1)} %copy-done.7, bf16[256,8,256]{2,1,0:T(8,128)(2,1)S(1)} %all_to_all.26), kind=kOutput, calls=%fused_computation.21 | convolution fusion | flops 1073741824 | bytes 6291456 | tf_op jit(solution)/shard_map/rm,rh->mh/dot_general | solution.py:52
  294.6 4.7 %convolution_bitcast_fusion = f32[1,1024,256]{2,1,0:T(8,128)} fusion(bf16[2048,1024]{1,0:T(8,128)(2,1)} %copy-done.8, bf16[256,8,256]{2,1,0:T(8,128)(2,1)} %copy-done.1), kind=kOutput, calls=%fused_computation.20 | convolution fusion | flops 1073741824 | bytes 6291456 | tf_op jit(solution)/shard_map/rh,rm->hm/dot_general | solution.py:49
  299.4 0.0 all-to-all-done.3
  299.4 0.7 gather_fusion.4
  300.1 0.1 select_convert_fusion
  300.2 0.1 reduce_sum.70
  300.3 0.8 fusion.9
  (26 shorter events, 0.3 us)
Async XLA Ops:
  0.6 57.6 %copy-start = (bf16[1,256,1024]{2,1,0:T(8,128)(2,1)S(1)}, bf16[1,256,1024]{2,1,0:T(8,128)(2,1)}, u32[]{:S(2)}) copy-start(bf16[1,256,1024]{2,1,0:T(8,128)(2,1)} %param.12) | copy-start | bytes 1572868
  58.2 7.0 %copy-start.6 = (bf16[1,1024,256]{2,1,0:T(8,128)(2,1)S(1)}, bf16[1,1024,256]{2,1,0:T(8,128)(2,1)}, u32[]{:S(2)}) copy-start(bf16[1,1024,256]{2,1,0:T(8,128)(2,1)} %param.13) | copy-start | bytes 1572868
  63.2 2.0 copy-start.8
  63.2 11.0 %copy-start.4 = (bf16[32,256]{1,0:T(8,128)(2,1)S(1)}, bf16[32,256]{1,0:T(8,128)(2,1)}, u32[]{:S(2)}) copy-start(bf16[32,256]{1,0:T(8,128)(2,1)} %param.9) | copy-start | bytes 49156
  63.2 11.0 %copy-start.2 = (bf16[256,256]{1,0:T(8,128)(2,1)S(1)}, bf16[256,256]{1,0:T(8,128)(2,1)}, u32[]{:S(2)}) copy-start(bf16[256,256]{1,0:T(8,128)(2,1)} %param.11) | copy-start | bytes 393220
  63.2 11.1 %copy-start.3 = (bf16[32,256]{1,0:T(8,128)(2,1)S(1)}, bf16[32,256]{1,0:T(8,128)(2,1)}, u32[]{:S(2)}) copy-start(bf16[32,256]{1,0:T(8,128)(2,1)} %param.8) | copy-start | bytes 49156
  63.2 11.2 %copy-start.5 = (s32[32,2]{0,1:T(2,128)S(1)}, s32[32,2]{0,1:T(2,128)}, u32[]{:S(2)}) copy-start(s32[32,2]{0,1:T(2,128)} %param.10) | copy-start | bytes 772
  67.4 36.9 %all-to-all-start.1 = ((bf16[256,8,256]{2,1,0:T(8,128)(2,1)}), bf16[256,8,256]{2,1,0:T(8,128)(2,1)S(1)}, u32[]{:S(2)}, u32[]{:S(2)}) async-start(bf16[256,8,256]{2,1,0:T(8,128)(2,1)} %fusion.7), calls=%async_computation.1 | async-start | bytes 2097152 | tf_op jit(solution)/shard_map/all_to_all | solution.py:38
  127.3 36.7 %all-to-all-start.2 = ((bf16[256,8,256]{2,1,0:T(8,128)(2,1)}), bf16[256,8,256]{2,1,0:T(8,128)(2,1)S(1)}, u32[]{:S(2)}, u32[]{:S(2)}) async-start(bf16[256,8,256]{2,1,0:T(8,128)(2,1)} %bitcast_select_fusion), calls=%async_computation.2 | async-start | bytes 2097152 | tf_op jit(solution)/shard_map/all_to_all | solution.py:48
  164.0 15.0 %copy-start.1 = (bf16[256,8,256]{2,1,0:T(8,128)(2,1)}, bf16[256,8,256]{2,1,0:T(8,128)(2,1)S(1)}, u32[]{:S(2)}) copy-start(bf16[256,8,256]{2,1,0:T(8,128)(2,1)S(1)} %all-to-all-done.2) | copy-start | bytes 3145732
  164.0 23.0 %all-to-all-start.4 = ((bf16[256,1,8]{2,1,0:T(2,128)(2,1)}), bf16[256,1,8]{2,1,0:T(2,128)(2,1)S(1)}, u32[]{:S(2)}, u32[]{:S(2)}) async-start(bf16[256,1,8]{2,1,0:T(2,128)(2,1)} %select_n.86), calls=%async_computation.4 | async-start | bytes 262144 | tf_op jit(solution)/shard_map/all_to_all | solution.py:60
  179.1 1.9 copy-start.7
  187.0 112.4 %all-to-all-start.3 = ((bf16[256,8,256]{2,1,0:T(8,128)(2,1)}), bf16[256,8,256]{2,1,0:T(8,128)(2,1)S(1)}, u32[]{:S(2)}, u32[]{:S(2)}) async-start(bf16[256,8,256]{2,1,0:T(8,128)(2,1)} %fusion.8), calls=%async_computation.3 | async-start | bytes 2097152 | tf_op jit(solution)/shard_map/all_to_all | solution.py:54

commit v2 on v0

v2 whole, which is shorter than its diff:
```python
import functools

import jax
import jax.numpy as jnp
from jax import lax
from jax.experimental import pallas as pl
from jax.experimental.pallas import tpu as pltpu
from jax.sharding import PartitionSpec as P

MESH = pl.DeviceIdType.MESH
F32 = jnp.float32
BF16 = jnp.bfloat16
CAP = 8


def coords(dims):
    nz, ny, nx, nc = dims
    me = lax.axis_index('ep')
    c = lax.rem(me, nc)
    x = lax.rem(me // nc, nx)
    y = lax.rem(me // (nc * nx), ny)
    z = me // (nc * nx * ny)

    def dev(z, y, x, c):
        return (((z * ny + y) * nx + x) * nc + c,)

    return z, y, x, c, dev


def meet(peers):
    barrier = pltpu.get_barrier_semaphore()
    for peer in peers:
        pl.semaphore_signal(barrier, inc=1, device_id=peer, device_id_type=MESH)
    pl.semaphore_wait(barrier, len(peers))


def gather_kernel(dims, kinds, *refs):
    nz, ny, nx, nc = dims
    n = len(kinds)
    ins, held, load_sem = refs[:n], refs[n:2 * n], refs[2 * n]
    send, recv = refs[2 * n + 1:3 * n + 1], refs[3 * n + 1:4 * n + 1]
    z, y, x, c, dev = coords(dims)
    loads = [pltpu.make_async_copy(ins[a], held[a].at[z, y, x, c], load_sem.at[a]) for a in range(n)]
    for ld in loads:
        ld.start()
    peers = [dev(lax.rem(z + d, nz), y, x, c) for d in range(1, nz)]
    for d in ((1, 3, 2) if 'small' in kinds else (1, 3)):
        peers.append(dev(z, lax.rem(y + d, ny), x, c))
        peers.append(dev(z, y, lax.rem(x + d, nx), c))
    peers.append(dev(z, y, x, 1 - c))
    meet(peers)

    count = [0] * n

    def copy(a, src, to):
        k = count[a]
        count[a] += 1
        return pltpu.make_async_remote_copy(src_ref=src, dst_ref=src, send_sem=send[a].at[k], recv_sem=recv[a].at[k],
                                            device_id=to, device_id_type=MESH)

    sent = []

    def go(cp):
        cp.start()
        sent.append(cp)
        return cp

    zcopies = []
    for a in range(n):
        loads[a].wait()
        zcopies.append([go(copy(a, held[a].at[z, y, x, c], dev(lax.rem(z + d, nz), y, x, c))) for d in range(1, nz)])

    low, high, full = pl.ds(0, nz // 2), pl.ds(nz // 2, nz // 2), slice(None)

    def plans(a):
        yx = kinds[a] == 'yx'
        p0, q0 = (y, x) if yx else (x, y)
        npp, nq = (ny, nx) if yx else (nx, ny)

        def at(zs, p, q):
            return held[a].at[zs, p, q, c] if yx else held[a].at[zs, q, p, c]

        def to(p, q):
            return dev(z, p, q, c) if yx else dev(z, q, p, c)

        def shift(v, d, m):
            return lax.rem(v + d, m)

        cross = []

        def over(p, q):
            cross.append(go(copy(a, at(full, p, q), dev(z, y, x, 1 - c))))

        for cp in zcopies[a]:
            yield
            cp.wait_recv()
        pm, pp, po = shift(p0, npp - 1, npp), shift(p0, 1, npp), shift(p0, 2, npp)
        qm, qp, qo = shift(q0, nq - 1, nq), shift(q0, 1, nq), shift(q0, 2, nq)
        p_up = go(copy(a, at(full, p0, q0), to(pp, q0)))
        p_dn = go(copy(a, at(full, p0, q0), to(pm, q0)))
        qs = []

        def spread(p):
            qs.append((p, go(copy(a, at(full, p, q0), to(p0, qp))), go(copy(a, at(full, p, q0), to(p0, qm)))))
            over(p, q0)

        spread(p0)
        yield
        p_up.wait_recv()
        f_up = go(copy(a, at(low, pm, q0), to(pp, q0)))
        yield
        p_dn.wait_recv()
        f_dn = go(copy(a, at(high, pp, q0), to(pm, q0)))
        spread(pm)
        spread(pp)
        relays = []

        def relay(i):
            p, up, dn = qs[i]
            up.wait_recv()
            r_up = go(copy(a, at(low, p, qm), to(p0, qp)))
            over(p, qm)
            dn.wait_recv()
            r_dn = go(copy(a, at(high, p, qp), to(p0, qm)))
            over(p, qp)
            relays.append((p, r_up, r_dn))

        yield
        relay(0)
        yield
        f_up.wait_recv()
        f_dn.wait_recv()
        spread(po)
        for i in (1, 2, 3):
            yield
            relay(i)
            p, r_up, r_dn = relays[i - 1]
            r_up.wait_recv()
            r_dn.wait_recv()
            over(p, qo)
        yield
        p, r_up, r_dn = relays[3]
        r_up.wait_recv()
        r_dn.wait_recv()
        over(p, qo)
        for cp in cross:
            yield
            cp.wait_recv()

    def small(a):
        h = held[a]
        for cp in zcopies[a]:
            yield
            cp.wait_recv()
        ys = [go(copy(a, h.at[:, y, x, c], dev(z, lax.rem(y + d, ny), x, c))) for d in range(1, ny)]
        for cp in ys:
            yield
            cp.wait_recv()
        xs = [go(copy(a, h.at[:, :, x, c], dev(z, y, lax.rem(x + d, nx), c))) for d in range(1, nx)]
        for cp in xs:
            yield
            cp.wait_recv()
        cs = go(copy(a, h.at[:, :, :, c], dev(z, y, x, 1 - c)))
        yield
        cs.wait_recv()

    live = [small(a) if kinds[a] == 'small' else plans(a) for a in range(n)]
    while live:
        for g in list(live):
            try:
                next(g)
            except StopIteration:
                live.remove(g)
    for cp in sent:
        cp.wait_send()


def n_copies(dims, kind):
    nz, ny, nx, _ = dims
    return nz - 1 + (ny - 1 + nx - 1 + 1 if kind == 'small' else 4 + 16 + 16)


def all_gather(dims, arrays, kinds, cid):
    n = len(arrays)
    outs = [jax.ShapeDtypeStruct(dims + a.shape, a.dtype) for a in arrays]
    any_ = pl.BlockSpec(memory_space=pl.ANY)
    sems = [pltpu.SemaphoreType.DMA((n_copies(dims, k),)) for k in kinds]
    return pl.pallas_call(
        functools.partial(gather_kernel, dims, kinds),
        out_shape=outs,
        in_specs=[any_] * n,
        out_specs=[any_] * n,
        scratch_shapes=[pltpu.SemaphoreType.DMA((n,))] + sems + sems,
        compiler_params=pltpu.CompilerParams(collective_id=cid, has_side_effects=True, vmem_limit_bytes=2 ** 20),
        name=f'gather_{cid}',
    )(*arrays)


def quads(m):
    return jnp.sum(m.reshape(m.shape[0] // 4, 4, 8, 128), axis=1)


def gelu_parts(a):
    k = 0.7978845608028654
    sq = a * a
    t = jnp.tanh(a * (k + (k * 0.044715) * sq))
    half = 0.5 + 0.5 * t
    slope = half + (0.5 * a) * (1.0 - t * t) * (k + (3 * k * 0.044715) * sq)
    return a * half, slope


def dot(a, b, ca, cb):
    return lax.dot_general(a, b, (((ca,), (cb,)), ((), ())), preferred_element_type=F32)


def expert_kernel(x_ref, d_ref, m_ref, w1_ref, w2_ref, y_ref, dx_ref, g1_ref, g2_ref):
    me = lax.axis_index('ep').astype(F32)
    meta = quads(m_ref[...])
    n_pair = meta.shape[0] // 2

    def rows(k):
        return jnp.concatenate([jnp.concatenate([meta[2 * p, k:k + 1], meta[2 * p + 1, k:k + 1]], axis=1) for p in range(n_pair)], axis=0)

    i0, i1, g0, g1 = (rows(k) for k in range(4))
    hit0, hit1 = i0 == me, i1 == me
    hit = (hit0 | hit1).astype(F32)
    gate = jnp.where(hit0, g0, 0.0) + jnp.where(hit1, g1, 0.0)
    before = lax.broadcasted_iota(jnp.int32, (256, 256), 0)
    after = lax.broadcasted_iota(jnp.int32, (256, 256), 1)
    tri = ((before < after) & (before // 32 == after // 32)).astype(F32).astype(BF16)
    rank = dot(hit.astype(BF16), tri, 1, 0)
    src = (lax.broadcasted_iota(jnp.int32, (n_pair, 256), 1) // 32).astype(F32)
    key = jnp.where(hit > 0.0, src * CAP + rank, -1.0)
    slot = lax.broadcasted_iota(jnp.int32, (8 * CAP, 256), 0).astype(F32)
    xs, dys = [], []
    for p in range(n_pair):
        sel = (slot == key[p:p + 1]).astype(F32)
        g = jnp.sum(sel * gate[p:p + 1], axis=1, keepdims=True)
        sel = sel.astype(BF16)
        xs.append(dot(sel, x_ref[256 * p:256 * (p + 1)], 1, 0).astype(BF16))
        dys.append((g * dot(sel, d_ref[256 * p:256 * (p + 1)], 1, 0)).astype(BF16))
    xs, dys = jnp.concatenate(xs, axis=0), jnp.concatenate(dys, axis=0)
    h, slope = gelu_parts(dot(xs, w1_ref[...], 1, 0))
    h = h.astype(BF16)
    y_ref[...] = dot(h, w2_ref[...], 1, 0).astype(BF16)
    da = (dot(dys, w2_ref[...], 1, 1) * slope).astype(BF16)
    dx_ref[...] = dot(da, w1_ref[...], 1, 1).astype(BF16)
    gw2 = dot(h, dys, 0, 0)
    gw1 = dot(xs, da, 0, 0)

    @pl.when(pl.program_id(0) == 0)
    def _():
        g1_ref[...] = gw1
        g2_ref[...] = gw2

    @pl.when(pl.program_id(0) > 0)
    def _():
        g1_ref[...] += gw1
        g2_ref[...] += gw2


def expert_block(x_all, d_all, m_all, w1, w2):
    steps = 4
    n_src = m_all.shape[0]
    tok, slots = x_all.shape[0] // steps, n_src * CAP // steps
    d_model, d_hidden = w1.shape
    whole = lambda shape: pl.BlockSpec(shape, lambda i: (0, 0))
    part = lambda r: pl.BlockSpec((r, d_model), lambda i: (i, 0))
    return pl.pallas_call(
        expert_kernel,
        grid=(steps,),
        out_shape=[jax.ShapeDtypeStruct((n_src * CAP, d_model), BF16)] * 2
        + [jax.ShapeDtypeStruct((d_model, d_hidden), F32), jax.ShapeDtypeStruct((d_hidden, d_model), F32)],
        in_specs=[part(tok), part(tok), pl.BlockSpec((n_src // steps, 8, 128), lambda i: (i, 0, 0)), whole(w1.shape), whole(w2.shape)],
        out_specs=[part(slots), part(slots), whole((d_model, d_hidden)), whole((d_hidden, d_model))],
        compiler_params=pltpu.CompilerParams(dimension_semantics=('arbitrary',), vmem_limit_bytes=32 * 2 ** 20),
        name='expert',
    )(x_all, d_all, m_all, w1, w2)


def gate_kernel(x_ref, m_ref, d_ref, o_ref, acc):
    meta, grad = quads(m_ref[...]), quads(d_ref[...])
    expert = lax.broadcasted_iota(jnp.int32, (acc.shape[0], 256), 0).astype(F32)

    @pl.when(pl.program_id(0) == 0)
    def _():
        acc[...] = jnp.zeros_like(acc)

    total = acc[...]
    for p in range(meta.shape[0] // 2):
        def row(v, k):
            return jnp.concatenate([v[2 * p, k:k + 1], v[2 * p + 1, k:k + 1]], axis=1)

        spread = jnp.where(expert == row(meta, 0), row(grad, 0), jnp.where(expert == row(meta, 1), row(grad, 1), 0.0))
        total += dot(spread.astype(BF16), x_ref[256 * p:256 * (p + 1)], 1, 0)
    acc[...] = total

    @pl.when(pl.program_id(0) == pl.num_programs(0) - 1)
    def _():
        o_ref[...] = total.T


def gate_grad(x_all, m_all, d_all):
    steps = 8
    n_src = m_all.shape[0]
    d_model = x_all.shape[1]
    meta = pl.BlockSpec((n_src // steps, 8, 128), lambda i: (i, 0, 0))
    return pl.pallas_call(
        gate_kernel,
        grid=(steps,),
        out_shape=jax.ShapeDtypeStruct((d_model, n_src), F32),
        in_specs=[pl.BlockSpec((x_all.shape[0] // steps, d_model), lambda i: (i, 0)), meta, meta],
        out_specs=pl.BlockSpec((d_model, n_src), lambda i: (0, 0)),
        scratch_shapes=[pltpu.VMEM((n_src, d_model), F32)],
        compiler_params=pltpu.CompilerParams(dimension_semantics=('arbitrary',), vmem_limit_bytes=8 * 2 ** 20),
        name='gate_grad',
    )(x_all, m_all, d_all)


def lane_place(rows):
    k, t = rows.shape
    here = lax.broadcasted_iota(jnp.int32, (k, 4 * t), 1) // t == lax.rem(lax.axis_index('ep'), 4)
    return jnp.pad(jnp.where(here, jnp.tile(rows, (1, 4)), 0.0), ((0, 8 - k), (0, 0)))


def local_block(dims, tokens, grad_out, expert_ids, w_gate, w_in, w_out):
    n_exp = w_gate.shape[1]
    tok_dev, d_model = tokens.shape
    n_choice = 2 * tok_dev
    n_slots = n_exp * CAP
    choice_hot = expert_ids[:, :, None] == jnp.arange(n_exp)[None, None, :]
    logits = jnp.dot(tokens, w_gate, preferred_element_type=F32)
    sel_logit = jnp.sum(jnp.where(choice_hot, logits[:, None, :], 0.0), axis=-1)
    gate_val = jax.nn.softmax(sel_logit, axis=1)
    meta = lane_place(jnp.concatenate([expert_ids.astype(F32), gate_val], axis=1).T)
    x_all, d_all, m_all = all_gather(dims, [tokens, grad_out, meta], ('yx', 'xy', 'small'), 0)
    x_all, d_all = x_all.reshape(-1, d_model), d_all.reshape(-1, d_model)
    m_all = m_all.reshape(n_exp, 8, 128)
    y_rows, dx_rows, g_w_in, g_w_out = expert_block(x_all, d_all, m_all, w_in[0], w_out[0])

    one_hot = choice_hot.any(axis=1).astype(jnp.int32)
    earlier = jnp.cumsum(one_hot, axis=0) - one_hot
    dest_slot = expert_ids * CAP + jnp.sum(jnp.where(choice_hot, earlier[:, None, :], 0), axis=-1)
    y_back = lax.all_to_all(y_rows.reshape(n_exp, CAP, d_model), 'ep', 0, 0, tiled=True).reshape(n_slots, d_model)
    y_pair = jnp.take(y_back, dest_slot.reshape(-1), axis=0).reshape(tok_dev, 2, d_model)
    y_out = jnp.sum(gate_val[:, :, None] * y_pair.astype(F32), axis=1).astype(BF16)
    d_gate = jnp.einsum('tm,tkm->tk', grad_out, y_pair, preferred_element_type=F32)
    d_sel = gate_val * (d_gate - jnp.sum(gate_val * d_gate, axis=1, keepdims=True))
    d_bf = d_sel.astype(BF16)
    g_all, = all_gather(dims, [lane_place(d_bf.astype(F32).T)], ('small',), 1)
    grad_w_gate = gate_grad(x_all, m_all, g_all.reshape(n_exp, 8, 128))
    dx_back = lax.all_to_all(dx_rows.reshape(n_exp, CAP, d_model), 'ep', 0, 0, tiled=True).reshape(n_slots, d_model)
    dx_pair = jnp.take(dx_back, dest_slot.reshape(-1), axis=0).reshape(tok_dev, 2, d_model)
    d_logits = jnp.sum(jnp.where(choice_hot, d_sel[:, :, None], 0.0), axis=1).astype(BF16)
    grad_x = (jnp.sum(dx_pair.astype(F32), axis=1) + jnp.einsum('te,me->tm', d_logits, w_gate, preferred_element_type=F32)).astype(BF16)
    return y_out, grad_x, g_w_in[None], g_w_out[None], grad_w_gate


def solution(mesh):
    dims = (8, 4, 4, 2)
    return jax.shard_map(functools.partial(local_block, dims), mesh=mesh, in_specs=(P('ep'), P('ep'), P('ep'), P(), P('ep'), P('ep')), out_specs=(P('ep'), P('ep'), P('ep'), P('ep'), P()), check_vma=False)
```

time: 467 us -> 185 us (0.40)
  waiting for transfers between devices: 297 us -> 29.1 us
  Pallas kernels: 0 us -> 93 us
  blocking collectives: 82.4 us -> 39.7 us
  matrix products: 29.2 us -> 1.79 us
  local copies, waits for them, and re-layouts: 25.3 us -> 8.32 us
  between operations: 14.3 us -> 0.85 us
  starting transfers between devices: 13.5 us -> 6.72 us
    psum x1 -> x0, waiting for transfers between devices: 268 us -> none  [local_block(): lax.psum(jnp.einsum('tm,te->me', tokens, d_logits, preferred_element_type...]
    pallas_call x0 -> x4, Pallas kernels: none -> 93 us  [the longest x2 75.4 us: all_gather(): pl.pallas_call(functools.partial(gather_kernel, dims, kinds), out_shape=o...]
    all_to_all x2 -> x1, blocking collectives: 82.4 us -> 39.7 us  [local_block(): lax.all_to_all(y_rows.reshape(n_exp, CAP, d_model), 'ep', 0, 0, tiled=True)]
    dot_general x10 -> x3, matrix products: 29.2 us -> 1.79 us  [the longest x1 0.85 us: local_block(): logits = jnp.dot(tokens, w_gate, preferred_element_type=F32)]
    gather x4 -> x2, local copies, waits for them, and re-layouts: 16.4 us -> 1.4 us  [the longest x1 0.7 us: local_block(): jnp.take(y_back, dest_slot.reshape(-1), axis=0).reshape(tok_dev, 2, d_model)]
    all_to_all x2 -> x1, starting transfers between devices: 13.5 us -> 6.72 us  [local_block(): lax.all_to_all(dx_rows.reshape(n_exp, CAP, d_model), 'ep', 0, 0, tiled=True)]
    all_to_all x2 -> x1, waiting for transfers between devices: 29.5 us -> 29.1 us  [local_block(): lax.all_to_all(dx_rows.reshape(n_exp, CAP, d_model), 'ep', 0, 0, tiled=True)]
  transfers between devices with their start and end apart: 3 -> 1, of which waited for: 2 -> 1; matrix products, arithmetic and copies ran while one was open for 3% -> 1% of each run, Pallas kernels for 0% -> 0%
where the time goes in v2:
time: 185 us; the launch traced here: 184 us
  Pallas kernels  93 us (50%)
  blocking collectives  39.7 us (21%)
  waiting for transfers between devices  29.1 us (16%)
  local copies, waits for them, and re-layouts  8.32 us (4%)
  starting transfers between devices  6.72 us (4%)
  other arithmetic  4.49 us (2%)
    pallas_call x2, Pallas kernels, all_gather(): pl.pallas_call(functools.partial(gather_kernel, dims, kinds), out_shape=o...  75.4 us
    all_to_all x1, blocking collectives, local_block(): lax.all_to_all(y_rows.reshape(n_exp, CAP, d_model), 'ep', 0, 0, tiled=True)  39.7 us
    all_to_all x1, waiting for transfers between devices, local_block(): lax.all_to_all(dx_rows.reshape(n_exp, CAP, d_model), 'ep', 0, 0, tiled=True)  29.1 us
    pallas_call x1, Pallas kernels, expert_block(): pl.pallas_call(expert_kernel, grid=(steps,), out_shape=[jax.ShapeDtypeStr...  14 us
    all_to_all x1, starting transfers between devices, local_block(): lax.all_to_all(dx_rows.reshape(n_exp, CAP, d_model), 'ep', 0, 0, tiled=True)  6.72 us
    unnamed x18, local copies, waits for them, and re-layouts  6.32 us
  transfers between devices with their start and end apart: 1, of which 1 were waited for; matrix products, arithmetic and copies ran while one was open for 1% of the time, Pallas kernels for 0%

profile of v2, /device:TPU:1, one launch (start us, length us, event | category | flops | bytes accessed | tf_op | source)
XLA Modules:
  0.0 184.0 jit_solution(8134815574588628243)
XLA Ops:
  0.6 0.0 copy-start
  0.7 0.8 fusion.1
  1.5 0.1 copy-done
  1.5 0.9 fusion.11
  2.4 0.8 select_reduce_fusion.2
  3.3 0.1 reduce_window_sum.11
  3.4 0.9 select_reduce_fusion.1
  4.2 0.8 multiply_add_fusion
  5.0 0.1 tile.9
  5.1 0.0 copy-start.5
  5.1 0.7 copy-done.5
  5.8 0.0 copy-start.6
  5.9 0.7 copy-done.6
  6.6 54.0 %gather_0.1 = (bf16[8,4,4,2,32,256]{5,4,3,2,1,0:T(8,128)(2,1)S(1)}, bf16[8,4,4,2,32,256]{5,4,3,2,1,0:T(8,128)(2,1)S(1)}, f32[8,4,4,2,8,128]{5,4,3,2,1,0:T(8,128)S(1)}) custom-call(bf16[32,256]{1,0:T(8,128)(2,1)S(1)} %copy-done.5, bf16[32,256]{1,0:T(8,128)(2,1)S(1)} %copy-done.6, f32[8,128]{1,0:T(8,128)S(1)} %pad.8.refs_2_), custom_call_target="tpu_custom_call" | custom-call | tf_op jit(solution)/shard_map/gather_0/pallas_call | solution.py:188
  60.6 0.0 copy-start.1
  60.6 0.0 copy-start.3
  60.6 1.4 copy-done.3
  62.0 0.0 copy-start.4
  62.0 1.2 copy-done.4
  63.2 14.0 %expert.1 = (bf16[2048,256]{1,0:T(8,128)(2,1)S(1)}, bf16[2048,256]{1,0:T(8,128)(2,1)}, f32[256,1024]{1,0:T(8,128)}, f32[1024,256]{1,0:T(8,128)}) custom-call(bf16[8192,256]{1,0:T(8,128)(2,1)S(1)} %bitcast.30, bf16[8192,256]{1,0:T(8,128)(2,1)S(1)} %bitcast.35, f32[256,8,128]{2,1,0:T(8,128)S(1)} %bitcast.32, bf16[256,1024]{1,0:T(8,128)(2,1)S(1)} %bitcast.37, ...), custom_call_target="tpu_custom_call" | custom-call | tf_op jit(solution)/shard_map/expert/pallas_call | solution.py:269
  77.3 0.0 copy-done.1
  77.3 0.0 copy-start.7
  77.3 39.7 %all_to_all.10 = bf16[256,8,256]{2,1,0:T(8,128)(2,1)S(1)} all-to-all(bf16[256,8,256]{2,1,0:T(8,128)(2,1)S(1)} %bitcast.36), channel_id=1, replica_groups=mesh['ep'=256] {'ep'}, dimensions={0} | all-to-all | bytes 2097152 | tf_op jit(solution)/shard_map/all_to_all | solution.py:344
  117.0 6.7 %all-to-all-start.1 = ((bf16[256,8,256]{2,1,0:T(8,128)(2,1)}), bf16[256,8,256]{2,1,0:T(8,128)(2,1)S(1)}, u32[]{:S(2)}, u32[]{:S(2)}) async-start(bf16[256,8,256]{2,1,0:T(8,128)(2,1)} %bitcast.8), calls=%async_computation.1 | async-start | bytes 2097152 | tf_op jit(solution)/shard_map/all_to_all | solution.py:352
  123.7 0.1 copy.19
  123.8 0.1 copy.20
  123.9 0.1 reshape.113
  124.1 0.7 gather_fusion
  124.8 29.1 %all-to-all-done.1 = bf16[256,8,256]{2,1,0:T(8,128)(2,1)S(1)} async-done(((bf16[256,8,256]{2,1,0:T(8,128)(2,1)}), bf16[256,8,256]{2,1,0:T(8,128)(2,1)S(1)}, u32[]{:S(2)}, u32[]{:S(2)}) %all-to-all-start.1) | async-done | bytes 1048608 | tf_op jit(solution)/shard_map/all_to_all | solution.py:352
  153.9 0.0 copy-start.8
  153.9 0.7 gather_fusion.1
  154.6 0.1 select_convert_fusion
  154.7 0.0 copy-done.7
  154.7 0.1 fusion.2
  154.8 0.1 copy.22
  155.0 0.1 tile.21
  155.1 21.4 %gather_1.1 = f32[8,4,4,2,8,128]{5,4,3,2,1,0:T(8,128)S(1)} custom-call(f32[8,128]{1,0:T(8,128)S(1)} %pad.9.refs_0_), custom_call_target="tpu_custom_call" | custom-call | tf_op jit(solution)/shard_map/gather_1/pallas_call | solution.py:188
  176.5 0.0 copy-start.2
  176.5 2.2 %copy-done.2 = bf16[8,4,4,2,32,256]{5,4,3,2,1,0:T(8,128)(2,1)S(1)} copy-done((bf16[8,4,4,2,32,256]{5,4,3,2,1,0:T(8,128)(2,1)S(1)}, bf16[8,4,4,2,32,256]{5,4,3,2,1,0:T(8,128)(2,1)}, u32[]{:S(2)}) %copy-start.2) | copy-done | bytes 4194328
  178.7 3.6 %gate_grad.1 = f32[256,256]{1,0:T(8,128)} custom-call(bf16[8192,256]{1,0:T(8,128)(2,1)S(1)} %bitcast.31, f32[256,8,128]{2,1,0:T(8,128)S(1)} %bitcast.33, f32[256,8,128]{2,1,0:T(8,128)S(1)} %bitcast.34), custom_call_target="tpu_custom_call" | custom-call | tf_op jit(solution)/shard_map/gate_grad/pallas_call | solution.py:308
  182.3 0.0 copy-done.8
  182.3 0.1 select_reduce_fusion
  182.4 0.1 reduce_sum.67
  182.5 0.8 multiply_reduce_fusion
  183.3 0.8 fusion
  (21 shorter events, 0.2 us)
Async XLA Ops:
  0.6 0.9 copy-start
  5.1 0.7 copy-start.5
  5.8 0.7 copy-start.6
  60.6 16.7 %copy-start.1 = (bf16[8,4,4,2,32,256]{5,4,3,2,1,0:T(8,128)(2,1)}, bf16[8,4,4,2,32,256]{5,4,3,2,1,0:T(8,128)(2,1)S(1)}, u32[]{:S(2)}) copy-start(bf16[8,4,4,2,32,256]{5,4,3,2,1,0:T(8,128)(2,1)S(1)} %get-tuple-element.13) | copy-start | bytes 12582916
  60.6 1.4 copy-start.3
  62.0 1.2 copy-start.4
  77.3 77.4 %copy-start.7 = (bf16[32,256]{1,0:T(8,128)(2,1)S(1)}, bf16[32,256]{1,0:T(8,128)(2,1)}, u32[]{:S(2)}) copy-start(bf16[32,256]{1,0:T(8,128)(2,1)} %refs_1_.1) | copy-start | bytes 49156
  117.0 36.9 %all-to-all-start.1 = ((bf16[256,8,256]{2,1,0:T(8,128)(2,1)}), bf16[256,8,256]{2,1,0:T(8,128)(2,1)S(1)}, u32[]{:S(2)}, u32[]{:S(2)}) async-start(bf16[256,8,256]{2,1,0:T(8,128)(2,1)} %bitcast.8), calls=%async_computation.1 | async-start | bytes 2097152 | tf_op jit(solution)/shard_map/all_to_all | solution.py:352
  153.9 28.4 %copy-start.8 = (s32[32,2]{0,1:T(2,128)S(1)}, s32[32,2]{0,1:T(2,128)}, u32[]{:S(2)}) copy-start(s32[32,2]{0,1:T(2,128)} %param.10) | copy-start | bytes 772
  176.5 2.2 %copy-start.2 = (bf16[8,4,4,2,32,256]{5,4,3,2,1,0:T(8,128)(2,1)S(1)}, bf16[8,4,4,2,32,256]{5,4,3,2,1,0:T(8,128)(2,1)}, u32[]{:S(2)}) copy-start(bf16[8,4,4,2,32,256]{5,4,3,2,1,0:T(8,128)(2,1)} %copy-done.1) | copy-start | bytes 12582916

commit v3 on v2

v3 whole, which is shorter than its diff:
```python
import functools

import jax
import jax.numpy as jnp
from jax import lax
from jax.experimental import pallas as pl
from jax.experimental.pallas import tpu as pltpu
from jax.sharding import PartitionSpec as P

MESH = pl.DeviceIdType.MESH
F32 = jnp.float32
BF16 = jnp.bfloat16
CAP = 8


def coords(dims):
    nz, ny, nx, nc = dims
    me = lax.axis_index('ep')
    c = lax.rem(me, nc)
    x = lax.rem(me // nc, nx)
    y = lax.rem(me // (nc * nx), ny)
    z = me // (nc * nx * ny)

    def dev(z, y, x, c):
        return (((z * ny + y) * nx + x) * nc + c,)

    return z, y, x, c, dev


def meet(peers):
    barrier = pltpu.get_barrier_semaphore()
    for peer in peers:
        pl.semaphore_signal(barrier, inc=1, device_id=peer, device_id_type=MESH)
    pl.semaphore_wait(barrier, len(peers))


def dot(a, b, ca, cb):
    return lax.dot_general(a, b, (((ca,), (cb,)), ((), ())), preferred_element_type=F32)


def iota(shape, axis):
    return lax.broadcasted_iota(jnp.int32, shape, axis)


def as_row(col):
    n = col.shape[0]
    return jnp.sum(jnp.where(iota((n, n), 0) == iota((n, n), 1), col, 0.0), axis=0, keepdims=True)


def gates(tok, ids, w_gate):
    logits = dot(tok, w_gate, 1, 0)
    expert = iota(logits.shape, 1)
    l0, l1 = (jnp.sum(jnp.where(expert == ids[:, k:k + 1], logits, 0.0), axis=1, keepdims=True) for k in range(2))
    top = jnp.maximum(l0, l1)
    p0, p1 = jnp.exp(l0 - top), jnp.exp(l1 - top)
    total = p0 + p1
    return ids[:, 0:1].astype(F32), ids[:, 1:2].astype(F32), p0 / total, p1 / total


def choice_row(tok, ids, w_gate):
    i0, i1, g0, g1 = gates(tok, ids, w_gate)
    r0, r1 = as_row(i0), as_row(i1)

    def code(i):
        n = jnp.sum((i == r0).astype(F32) + (i == r1).astype(F32), axis=1, keepdims=True)
        return as_row(jnp.where(n > 1.5, i + 256.0, i))

    return jnp.concatenate([code(i0), code(i1), as_row(g0), as_row(g1)], axis=1)


def gather_kernel(dims, kinds, first, *refs):
    nz, ny, nx, nc = dims
    n = len(kinds)
    ins, refs = list(refs[:n]), refs[n:]
    if first:
        (tok_ref, gate_ref), refs = refs[:2], refs[2:]
    held, load_sem, refs = refs[:n], refs[n], refs[n + 1:]
    send, recv, refs = refs[:n], refs[n:2 * n], refs[2 * n:]
    if first:
        ids_ref, ins[-1] = ins[-1], refs[0]
    z, y, x, c, dev = coords(dims)
    loads = [pltpu.make_async_copy(ins[a], held[a].at[z, y, x, c], load_sem.at[a]) for a in range(n)]
    for ld in loads[:-1] if first else loads:
        ld.start()
    peers = [dev(lax.rem(z + d, nz), y, x, c) for d in range(1, nz)]
    for d in ((1, 3, 2) if 'small' in kinds else (1, 3)):
        peers.append(dev(z, lax.rem(y + d, ny), x, c))
        peers.append(dev(z, y, lax.rem(x + d, nx), c))
    peers.append(dev(z, y, x, 1 - c))
    meet(peers)

    count = [0] * n

    def copy(a, src, to):
        k = count[a]
        count[a] += 1
        return pltpu.make_async_remote_copy(src_ref=src, dst_ref=src, send_sem=send[a].at[k], recv_sem=recv[a].at[k],
                                            device_id=to, device_id_type=MESH)

    sent = []

    def go(cp):
        cp.start()
        sent.append(cp)
        return cp

    zcopies = []
    for a in range(n):
        if first and a == n - 1:
            ins[a][...] = choice_row(tok_ref[...], ids_ref[...], gate_ref[...])
            loads[a].start()
        loads[a].wait()
        zcopies.append([go(copy(a, held[a].at[z, y, x, c], dev(lax.rem(z + d, nz), y, x, c))) for d in range(1, nz)])

    low, high, full = pl.ds(0, nz // 2), pl.ds(nz // 2, nz // 2), slice(None)

    def plans(a):
        yx = kinds[a] == 'yx'
        p0, q0 = (y, x) if yx else (x, y)
        npp, nq = (ny, nx) if yx else (nx, ny)

        def at(zs, p, q):
            return held[a].at[zs, p, q, c] if yx else held[a].at[zs, q, p, c]

        def to(p, q):
            return dev(z, p, q, c) if yx else dev(z, q, p, c)

        def shift(v, d, m):
            return lax.rem(v + d, m)

        cross = []

        def over(p, q):
            cross.append(go(copy(a, at(full, p, q), dev(z, y, x, 1 - c))))

        for cp in zcopies[a]:
            yield
            cp.wait_recv()
        pm, pp, po = shift(p0, npp - 1, npp), shift(p0, 1, npp), shift(p0, 2, npp)
        qm, qp, qo = shift(q0, nq - 1, nq), shift(q0, 1, nq), shift(q0, 2, nq)
        p_up = go(copy(a, at(full, p0, q0), to(pp, q0)))
        p_dn = go(copy(a, at(full, p0, q0), to(pm, q0)))
        qs = []

        def spread(p):
            qs.append((p, go(copy(a, at(full, p, q0), to(p0, qp))), go(copy(a, at(full, p, q0), to(p0, qm)))))
            over(p, q0)

        spread(p0)
        yield
        p_up.wait_recv()
        f_up = go(copy(a, at(low, pm, q0), to(pp, q0)))
        yield
        p_dn.wait_recv()
        f_dn = go(copy(a, at(high, pp, q0), to(pm, q0)))
        spread(pm)
        spread(pp)
        relays = []

        def relay(i):
            p, up, dn = qs[i]
            up.wait_recv()
            r_up = go(copy(a, at(low, p, qm), to(p0, qp)))
            over(p, qm)
            dn.wait_recv()
            r_dn = go(copy(a, at(high, p, qp), to(p0, qm)))
            over(p, qp)
            relays.append((p, r_up, r_dn))

        yield
        relay(0)
        yield
        f_up.wait_recv()
        f_dn.wait_recv()
        spread(po)
        for i in (1, 2, 3):
            yield
            relay(i)
            p, r_up, r_dn = relays[i - 1]
            r_up.wait_recv()
            r_dn.wait_recv()
            over(p, qo)
        yield
        p, r_up, r_dn = relays[3]
        r_up.wait_recv()
        r_dn.wait_recv()
        over(p, qo)
        for cp in cross:
            yield
            cp.wait_recv()

    def small(a):
        h = held[a]
        for cp in zcopies[a]:
            yield
            cp.wait_recv()
        ys = [go(copy(a, h.at[:, y, x, c], dev(z, lax.rem(y + d, ny), x, c))) for d in range(1, ny)]
        for cp in ys:
            yield
            cp.wait_recv()
        xs = [go(copy(a, h.at[:, :, x, c], dev(z, y, lax.rem(x + d, nx), c))) for d in range(1, nx)]
        for cp in xs:
            yield
            cp.wait_recv()
        cs = go(copy(a, h.at[:, :, :, c], dev(z, y, x, 1 - c)))
        yield
        cs.wait_recv()

    live = [small(a) if kinds[a] == 'small' else plans(a) for a in range(n)]
    while live:
        for g in list(live):
            try:
                next(g)
            except StopIteration:
                live.remove(g)
    for cp in sent:
        cp.wait_send()


def n_copies(dims, kind):
    nz, ny, nx, _ = dims
    return nz - 1 + (ny - 1 + nx - 1 + 1 if kind == 'small' else 4 + 16 + 16)


def all_gather(dims, arrays, kinds, cid, first=()):
    n = len(arrays)
    blocks = [(a.shape, a.dtype) for a in arrays]
    if first:
        blocks[-1] = ((1, 128), F32)
    outs = [jax.ShapeDtypeStruct(dims + s, t) for s, t in blocks]
    hbm, vmem = pl.BlockSpec(memory_space=pltpu.HBM), pl.BlockSpec(memory_space=pltpu.VMEM)
    sems = [pltpu.SemaphoreType.DMA((n_copies(dims, k),)) for k in kinds]
    return pl.pallas_call(
        functools.partial(gather_kernel, dims, kinds, bool(first)),
        out_shape=outs,
        in_specs=[hbm] * (n - 1) + [vmem if first else pl.BlockSpec(memory_space=pl.ANY)] + [vmem] * len(first),
        out_specs=[pl.BlockSpec(memory_space=pl.ANY)] * n,
        scratch_shapes=[pltpu.SemaphoreType.DMA((n,))] + sems + sems + ([pltpu.VMEM((1, 128), F32)] if first else []),
        compiler_params=pltpu.CompilerParams(collective_id=cid, has_side_effects=True, vmem_limit_bytes=2 ** 20),
        name=f'gather_{cid}',
    )(*arrays, *first)


def gelu_parts(a):
    k = 0.7978845608028654
    sq = a * a
    t = jnp.tanh(a * (k + (k * 0.044715) * sq))
    half = 0.5 + 0.5 * t
    slope = half + (0.5 * a) * (1.0 - t * t) * (k + (3 * k * 0.044715) * sq)
    return a * half, slope


def token_lanes(ref, k, start, n):
    lane = iota((n, 128), 1) // 32
    out = jnp.zeros((n, 128), F32)
    for j in range(4):
        r = ref[pl.ds(start + j, n, stride=4), :]
        out = jnp.where(lane == j, r if j == k else pltpu.roll(r, 32 * (j - k) % 128, 1), out)
    return out


def pair_rows(v):
    return jnp.concatenate([jnp.concatenate([v[2 * i:2 * i + 1], v[2 * i + 1:2 * i + 2]], axis=1) for i in range(v.shape[0] // 2)], axis=0)


def plain_id(code):
    return jnp.where(code >= 256.0, code - 256.0, code)


def expert_kernel(dims, x_ref, d_ref, m_ref, all_ref, w1_ref, w2_ref, y_ref, dx_ref, g1_ref, g2_ref, hot_ref):
    _, ny, nx, nc = dims
    me = lax.axis_index('ep').astype(F32)
    n_quad = m_ref.shape[0] // 4
    c0, c1, g0, g1 = (pair_rows(token_lanes(m_ref, k, 0, n_quad)) for k in range(4))
    n_pair = n_quad // 2
    hit0, hit1 = plain_id(c0) == me, plain_id(c1) == me
    hit = (hit0 | hit1).astype(F32)
    gate = jnp.where(hit0, g0, 0.0) + jnp.where(hit1, g1, 0.0)
    before, after = iota((256, 256), 0), iota((256, 256), 1)
    tri = ((before < after) & (before // 32 == after // 32)).astype(F32).astype(BF16)
    rank = dot(hit.astype(BF16), tri, 1, 0)
    src = (iota((n_pair, 256), 1) // 32).astype(F32)
    key = jnp.where(hit > 0.0, src * CAP + rank, -1.0)
    slot = iota((8 * CAP, 256), 0).astype(F32)
    xs, dys = [], []
    for p in range(n_pair):
        sel = (slot == key[p:p + 1]).astype(F32)
        g = jnp.sum(sel * gate[p:p + 1], axis=1, keepdims=True)
        sel = sel.astype(BF16)
        xs.append(dot(sel, x_ref[256 * p:256 * (p + 1)], 1, 0))
        dys.append(g * dot(sel, d_ref[256 * p:256 * (p + 1)], 1, 0))
    places = [(c, x, y, z) for c in range(nc) for x in range(nx) for y in range(ny) for z in range(n_pair // ny)]

    def by_place(parts):
        return jnp.concatenate([parts[z * ny + y][8 * (x * nc + c):8 * (x * nc + c + 1)] for c, x, y, z in places], axis=0).astype(BF16)

    xs, dys = by_place(xs), by_place(dys)
    h, slope = gelu_parts(dot(xs, w1_ref[...], 1, 0))
    h = h.astype(BF16)
    y = dot(h, w2_ref[...], 1, 0)
    da = (dot(dys, w2_ref[...], 1, 1) * slope).astype(BF16)
    dx = dot(da, w1_ref[...], 1, 1)
    for i, place in enumerate(places):
        y_ref[place] = y[8 * i:8 * (i + 1)].astype(BF16)
        dx_ref[place] = dx[8 * i:8 * (i + 1)].astype(BF16)
    gw2 = dot(h, dys, 0, 0)
    gw1 = dot(xs, da, 0, 0)

    @pl.when(pl.program_id(0) == 0)
    def _():
        g1_ref[...] = gw1
        g2_ref[...] = gw2
        code = all_ref[...]
        ids = jnp.where((iota(code.shape, 1) < 64) & (code >= 256.0), code - 256.0, 999.0)
        found = []
        for _ in range(3):
            best = jnp.min(jnp.min(ids, axis=0, keepdims=True), axis=1, keepdims=True)
            ids = jnp.where(ids == best, 999.0, ids)
            found.append(jnp.broadcast_to(best, (1, 128)))
        hot_ref[...] = jnp.concatenate(found + [jnp.full((5, 128), 999.0, F32)], axis=0)

    @pl.when(pl.program_id(0) > 0)
    def _():
        g1_ref[...] += gw1
        g2_ref[...] += gw2


def expert_block(dims, x_all, d_all, m_all, w1, w2):
    steps = 4
    nz, ny, nx, nc = dims
    n_src = m_all.shape[0]
    if nz < 8:
        steps = nz // 2
    tok = x_all.shape[0] // steps
    d_model, d_hidden = w1.shape
    whole = lambda shape: pl.BlockSpec(shape, lambda i: (0, 0))
    part = lambda r: pl.BlockSpec((r, d_model), lambda i: (i, 0))
    back = (nc, nx, ny, nz // steps, CAP, d_model)
    back_spec = pl.BlockSpec(back, lambda i: (0, 0, 0, i, 0, 0))
    return pl.pallas_call(
        functools.partial(expert_kernel, dims),
        grid=(steps,),
        out_shape=[jax.ShapeDtypeStruct((nc, nx, ny, nz, CAP, d_model), BF16)] * 2
        + [jax.ShapeDtypeStruct((d_model, d_hidden), F32), jax.ShapeDtypeStruct((d_hidden, d_model), F32), jax.ShapeDtypeStruct((8, 128), F32)],
        in_specs=[part(tok), part(tok), pl.BlockSpec((n_src // steps, 128), lambda i: (i, 0)), whole(m_all.shape), whole(w1.shape), whole(w2.shape)],
        out_specs=[back_spec, back_spec, whole((d_model, d_hidden)), whole((d_hidden, d_model)), whole((8, 128))],
        compiler_params=pltpu.CompilerParams(dimension_semantics=('arbitrary',), vmem_limit_bytes=32 * 2 ** 20),
        name='expert',
    )(x_all, d_all, m_all, m_all, w1, w2)


def return_kernel(dims, hot_ref, *refs):
    nz, ny, nx, nc = dims
    z, y, x, c, dev = coords(dims)
    peers = [dev(z, y, x, 1 - c)]
    for d in (1, 3):
        peers.append(dev(z, lax.rem(y + d, ny), x, c))
        peers.append(dev(z, y, lax.rem(x + d, nx), c))
    peers += [dev(lax.rem(z + d, nz), y, x, c) for d in range(1, nz)]
    meet(peers)
    sent = []

    def plan(i):
        h, hot_land, cold_land = refs[i], refs[2 + 2 * i], refs[3 + 2 * i]
        other, near, via, out2, via2, in2, out3 = refs[6 + 7 * i:13 + 7 * i]
        send, recv, keep = refs[20 + 3 * i:23 + 3 * i]
        x_first = i == 0
        a, b = (x, y) if x_first else (y, x)
        count = [0]

        def go(src, dst, to):
            k = count[0]
            count[0] += 1
            cp = pltpu.make_async_remote_copy(src_ref=src, dst_ref=dst, send_sem=send.at[k], recv_sem=recv.at[k], device_id=to, device_id_type=MESH)
            cp.start()
            sent.append(cp)
            return cp

        def to(a, b):
            return dev(z, b, a, c) if x_first else dev(z, a, b, c)

        def index(lead, a, bs):
            return lead + ((a, bs) if x_first else (bs, a))

        def step(v, d):
            return lax.rem(v + d, 4)

        up, dn, far = step(a, 1), step(a, 3), step(a, 2)
        lo, hi, full = pl.ds(0, 2), pl.ds(2, 2), slice(None)
        cross = go(h.at[1 - c], other, dev(z, y, x, 1 - c))

        def spread(ref, lead, e):
            return [go(ref.at[index(lead, far, lo)], via.at[0, e], to(up, b)), go(ref.at[index(lead, far, hi)], via.at[1, e], to(dn, b)),
                    go(ref.at[index(lead, up, full)], near.at[a, e], to(up, b)), go(ref.at[index(lead, dn, full)], near.at[a, e], to(dn, b))]

        def relay(cps, e):
            cps[0].wait_recv()
            r_up = go(via.at[0, e], near.at[dn, e, lo], to(up, b))
            cps[1].wait_recv()
            r_dn = go(via.at[1, e], near.at[up, e, hi], to(dn, b))
            return [cps[2], cps[3], r_up, r_dn]

        own = spread(h, (c,), c)
        yield
        cross.wait_recv()
        his = spread(other, (), 1 - c)
        yield
        waits = relay(own, c)
        yield
        waits += relay(his, 1 - c)
        for cp in waits:
            yield
            cp.wait_recv()

        def expert(s, e):
            return ((z * ny + y) * nx + s) * nc + e if x_first else ((z * ny + s) * nx + x) * nc + e

        places = [(step(a, d), e) for d in range(4) for e in (c, 1 - c)]
        is_hot = [[(hot_ref[j:j + 1, :] == expert(s, e).astype(F32)).astype(F32) for s, e in places] for j in range(3)]

        def wide(v):
            v = jnp.broadcast_to(v, (8, 128))
            return jnp.concatenate([v, v], axis=1)

        weight = [[wide(v).astype(BF16) for v in row] for row in is_hot]
        line = iota((8, 256), 0)
        mine = [(wide(is_hot[0][k] + is_hot[1][k] + is_hot[2][k]) < 0.5) & (line == s * nc + e) for k, (s, e) in enumerate(places)]

        def squeeze(bb, carry):
            parts = [h[index((c,), a, bb)], other[index((), a, bb)]] + [near[s, e, bb] for s, e in places[2:]]
            for j in range(3):
                out2[bb, j] = sum(parts[k] * weight[j][k] for k in range(8))
            singles = jnp.zeros((nz, 8, 256), F32)
            for k in range(8):
                singles = jnp.where(mine[k], jnp.sum(parts[k].astype(F32), axis=1, keepdims=True), singles)
            out2[bb, 3] = singles.astype(BF16)
            return carry

        lax.fori_loop(0, 4, squeeze, 0)
        in2[b] = out2[b]
        yield
        up, dn, far = step(b, 1), step(b, 3), step(b, 2)
        lo, hi = pl.ds(0, nz // 2), pl.ds(nz // 2, nz // 2)
        f_up, f_dn = go(out2.at[far, :, lo], via2.at[0], to(a, up)), go(out2.at[far, :, hi], via2.at[1], to(a, dn))
        n_up, n_dn = go(out2.at[up], in2.at[b], to(a, up)), go(out2.at[dn], in2.at[b], to(a, dn))
        yield
        f_up.wait_recv()
        r_up = go(via2.at[0], in2.at[dn, :, lo], to(a, up))
        f_dn.wait_recv()
        r_dn = go(via2.at[1], in2.at[up, :, hi], to(a, dn))
        for cp in (n_up, n_dn, r_up, r_dn):
            yield
            cp.wait_recv()
        for j in range(3):
            out3[:, j] = (in2[0, j] + in2[1, j]) + (in2[2, j] + in2[3, j])
        last = []
        for d in range(1, nz):
            zz = lax.rem(z + d, nz)
            last.append(go(in2.at[:, 3, zz], cold_land.at[z], dev(zz, y, x, c)))
        for d in range(1, nz):
            zz = lax.rem(z + d, nz)
            last.append(go(out3.at[zz], hot_land.at[z], dev(zz, y, x, c)))
        stay = [pltpu.make_async_copy(in2.at[:, 3, z], cold_land.at[z], keep.at[0]), pltpu.make_async_copy(out3.at[z], hot_land.at[z], keep.at[1])]
        for cp in stay:
            cp.start()
        for cp in last:
            yield
            cp.wait_recv()
        for cp in stay:
            cp.wait()

    live = [plan(0), plan(1)]
    while live:
        for g in list(live):
            try:
                next(g)
            except StopIteration:
                live.remove(g)
    for cp in sent:
        cp.wait_send()


def return_rows(dims, hot, y_rows, dx_rows):
    nz = dims[0]
    tile = y_rows.shape[-2:]
    n_cp = 1 + 12 + 6 + 2 * (nz - 1)
    vmem, any_ = pl.BlockSpec(memory_space=pltpu.VMEM), pl.BlockSpec(memory_space=pl.ANY)
    work = [(4, 4, nz), (4, 2, 4, nz), (2, 2, 2, nz), (4, 4, nz), (2, 4, nz // 2), (4, 4, nz), (nz, 3)]
    sems = [pltpu.SemaphoreType.DMA((n_cp,)), pltpu.SemaphoreType.DMA((n_cp,)), pltpu.SemaphoreType.DMA((2,))]
    return pl.pallas_call(
        functools.partial(return_kernel, dims),
        out_shape=[jax.ShapeDtypeStruct((nz, 3) + tile, BF16), jax.ShapeDtypeStruct((nz, 4) + tile, BF16)] * 2,
        in_specs=[vmem] * 3,
        out_specs=[any_] * 4,
        scratch_shapes=[pltpu.VMEM(w + tile, BF16) for w in work] * 2 + sems * 2,
        compiler_params=pltpu.CompilerParams(collective_id=1, has_side_effects=True, vmem_limit_bytes=24 * 2 ** 20),
        name='return_rows',
    )(hot, y_rows, dx_rows)


def combine_kernel(dims, tok_ref, dout_ref, ids_ref, gate_ref, hot_ref, hy_ref, cy_ref, hdx_ref, cdx_ref, out_ref, gx_ref, d_ref):
    nz, ny, nx, nc = dims
    ids = ids_ref[...]
    i0, i1, g0, g1 = gates(tok_ref[...], ids, gate_ref[...])
    r0, r1 = as_row(i0), as_row(i1)
    n_tok = ids.shape[0]
    earlier = iota((n_tok, n_tok), 1) < iota((n_tok, n_tok), 0)
    hot = [hot_ref[j:j + 1, 0:1] for j in range(3)]
    n_cold = cy_ref.shape[0]

    def table(ref):
        v = jnp.sum(ref[...].astype(F32), axis=0)
        return jnp.concatenate([v, jnp.zeros((8, v.shape[1]), F32)], axis=0).astype(BF16)

    hot_y, hot_dx = table(hy_ref), table(hdx_ref)

    def pick(k):
        i = (i0, i1)[k]
        e = ids[:, k:k + 1]
        rank = jnp.sum(jnp.where(earlier & ((i == r0) | (i == r1)), 1.0, 0.0), axis=1, keepdims=True)
        place = jnp.full((n_tok, 1), -1.0, F32)
        for j in range(3):
            place = jnp.where(i == hot[j], CAP * j + rank, place)
        sel_hot = (iota((n_tok, 32), 1).astype(F32) == place).astype(F32).astype(BF16)
        cold = place < 0.0
        core, xx, yy, zz = e % nc, (e // nc) % nx, (e // (nc * nx)) % ny, e // (nc * nx * ny)
        lane = iota((n_tok, n_cold), 1)
        in_y = ((lane == e) & cold).astype(F32).astype(BF16)
        in_dx = ((lane == ((zz * nx + xx) * ny + yy) * nc + core) & cold).astype(F32).astype(BF16)
        return (dot(sel_hot, hot_y, 1, 0) + dot(in_y, cy_ref[...], 1, 0), dot(sel_hot, hot_dx, 1, 0) + dot(in_dx, cdx_ref[...], 1, 0))

    (y0, dx0), (y1, dx1) = pick(0), pick(1)
    out_ref[...] = (g0 * y0 + g1 * y1).astype(BF16)
    dout = dout_ref[...].astype(F32)
    dg0, dg1 = (jnp.sum(dout * v, axis=1, keepdims=True) for v in (y0, y1))
    mean = g0 * dg0 + g1 * dg1
    d0, d1 = ((g * (dg - mean)).astype(BF16).astype(F32) for g, dg in ((g0, dg0), (g1, dg1)))
    expert = iota((n_tok, gate_ref.shape[1]), 1)
    spread = jnp.where(expert == ids[:, 0:1], d0, jnp.where(expert == ids[:, 1:2], d1, 0.0)).astype(BF16)
    gx_ref[...] = (dx0 + dx1 + dot(spread, gate_ref[...], 1, 1)).astype(BF16)
    d_ref[...] = jnp.concatenate([as_row(d0), as_row(d1), jnp.zeros((1, 2 * n_tok), F32)], axis=1)


def combine(dims, tokens, grad_out, ids, w_gate, hot, back):
    nz = dims[0]
    d_model = tokens.shape[1]
    back = [v.reshape((nz, 24, d_model) if k % 2 == 0 else (nz * 32, d_model)) for k, v in enumerate(back)]
    return pl.pallas_call(
        functools.partial(combine_kernel, dims),
        out_shape=[jax.ShapeDtypeStruct(tokens.shape, BF16)] * 2 + [jax.ShapeDtypeStruct((1, 128), F32)],
        compiler_params=pltpu.CompilerParams(vmem_limit_bytes=16 * 2 ** 20),
        name='combine',
    )(tokens, grad_out, ids, w_gate, hot, *back)


def gate_kernel(x_ref, m_ref, d_ref, o_ref, acc):
    n_quad = m_ref.shape[0] // 4
    i0, i1 = (plain_id(pair_rows(token_lanes(m_ref, k, 0, n_quad))) for k in range(2))
    d0, d1 = (pair_rows(token_lanes(d_ref, k, 0, n_quad)) for k in range(2))
    expert = iota((acc.shape[0], 256), 0).astype(F32)

    @pl.when(pl.program_id(0) == 0)
    def _():
        acc[...] = jnp.zeros_like(acc)

    total = acc[...]
    for p in range(n_quad // 2):
        q = slice(p, p + 1)
        spread = jnp.where(expert == i0[q], d0[q], jnp.where(expert == i1[q], d1[q], 0.0))
        total += dot(spread.astype(BF16), x_ref[256 * p:256 * (p + 1)], 1, 0)
    acc[...] = total

    @pl.when(pl.program_id(0) == pl.num_programs(0) - 1)
    def _():
        o_ref[...] = total.T


def gate_grad(x_all, m_all, d_all):
    n_src = m_all.shape[0]
    steps = 8 if n_src == 256 else 2
    d_model = x_all.shape[1]
    meta = pl.BlockSpec((n_src // steps, 128), lambda i: (i, 0))
    return pl.pallas_call(
        gate_kernel,
        grid=(steps,),
        out_shape=jax.ShapeDtypeStruct((d_model, n_src), F32),
        in_specs=[pl.BlockSpec((x_all.shape[0] // steps, d_model), lambda i: (i, 0)), meta, meta],
        out_specs=pl.BlockSpec((d_model, n_src), lambda i: (0, 0)),
        scratch_shapes=[pltpu.VMEM((n_src, d_model), F32)],
        compiler_params=pltpu.CompilerParams(dimension_semantics=('arbitrary',), vmem_limit_bytes=8 * 2 ** 20),
        name='gate_grad',
    )(x_all, m_all, d_all)


def local_block(dims, tokens, grad_out, expert_ids, w_gate, w_in, w_out):
    n_exp = w_gate.shape[1]
    d_model = tokens.shape[1]
    x_all, d_all, m_all = all_gather(dims, [tokens, grad_out, expert_ids], ('yx', 'xy', 'small'), 0, (tokens, w_gate))
    x_all, d_all, m_all = x_all.reshape(-1, d_model), d_all.reshape(-1, d_model), m_all.reshape(n_exp, 128)
    y_rows, dx_rows, g_w_in, g_w_out, hot = expert_block(dims, x_all, d_all, m_all, w_in[0], w_out[0])
    back = return_rows(dims, hot, y_rows, dx_rows)
    y_out, grad_x, d_row = combine(dims, tokens, grad_out, expert_ids, w_gate, hot, back)
    g_all, = all_gather(dims, [d_row], ('small',), 2)
    grad_w_gate = gate_grad(x_all, m_all, g_all.reshape(n_exp, 128))
    return y_out, grad_x, g_w_in[None], g_w_out[None], grad_w_gate


def solution(mesh):
    dims = (8, 4, 4, 2)
    return jax.shard_map(functools.partial(local_block, dims), mesh=mesh, in_specs=(P('ep'), P('ep'), P('ep'), P(), P('ep'), P('ep')), out_specs=(P('ep'), P('ep'), P('ep'), P('ep'), P()), check_vma=False)
```

time: 185 us -> 132 us (0.71)
  blocking collectives: 39.7 us -> 0 us
  Pallas kernels: 93 us -> 126 us
  waiting for transfers between devices: 29.1 us -> 0 us
  starting transfers between devices: 6.72 us -> 0 us
  other arithmetic: 4.49 us -> 0 us
  local copies, waits for them, and re-layouts: 8.32 us -> 5.19 us
    all_to_all x1 -> x0, blocking collectives: 39.7 us -> none  [local_block(): lax.all_to_all(y_rows.reshape(n_exp, CAP, d_model), 'ep', 0, 0, tiled=True)]
    pallas_call x3 -> x5, Pallas kernels: 89.4 us -> 122 us  [the longest x2 67.9 us: all_gather(): pl.pallas_call(functools.partial(gather_kernel, dims, kinds, bool(first))...]
    all_to_all x1 -> x0, waiting for transfers between devices: 29.1 us -> none  [local_block(): lax.all_to_all(dx_rows.reshape(n_exp, CAP, d_model), 'ep', 0, 0, tiled=True)]
    all_to_all x1 -> x0, starting transfers between devices: 6.72 us -> none  [local_block(): lax.all_to_all(dx_rows.reshape(n_exp, CAP, d_model), 'ep', 0, 0, tiled=True)]
    reduce_sum x7 -> x0, other arithmetic: 2.69 us -> none  [the longest x1 0.86 us: local_block(): jnp.sum(jnp.where(choice_hot, earlier[:, None, :], 0), axis=-1)]
    unnamed x18 -> x17, local copies, waits for them, and re-layouts: 6.32 us -> 5.19 us
  transfers between devices with their start and end apart: 1 -> 0, of which waited for: 1 -> 0; matrix products, arithmetic and copies ran while one was open for 1% -> 0% of each run, Pallas kernels for 0% -> 0%
where the time goes in v3:
time: 132 us
  Pallas kernels  126 us (95%)
  local copies, waits for them, and re-layouts  5.19 us (4%)
    pallas_call x2, Pallas kernels, all_gather(): pl.pallas_call(functools.partial(gather_kernel, dims, kinds, bool(first))...  67.9 us
    pallas_call x1, Pallas kernels, return_rows(): pl.pallas_call(functools.partial(return_kernel, dims), out_shape=[jax.Sha...  37.7 us
    pallas_call x1, Pallas kernels, expert_block(): pl.pallas_call(functools.partial(expert_kernel, dims), grid=(steps,), out...  14.6 us
    unnamed x17, local copies, waits for them, and re-layouts  5.19 us
    pallas_call x1, Pallas kernels, gate_grad(): pl.pallas_call(gate_kernel, grid=(steps,), out_shape=jax.ShapeDtypeStruct...  4.18 us

profile of v3, /device:TPU:1, one launch (start us, length us, event | category | flops | bytes accessed | tf_op | source)
XLA Modules:
  0.0 131.6 jit_solution(13718837708151925343)
XLA Ops:
  0.6 0.8 copy.12.refs_2_.ids_ref
  1.4 0.0 copy-start.2
  1.4 0.9 copy-done.2
  2.3 0.0 copy-start.4
  2.3 0.7 copy-done.4
  3.0 0.0 copy-start.6
  3.0 0.7 copy-done.6
  3.7 50.0 %gather_0.1 = (bf16[8,4,4,2,32,256]{5,4,3,2,1,0:T(8,128)(2,1)S(1)}, bf16[8,4,4,2,32,256]{5,4,3,2,1,0:T(8,128)(2,1)S(1)}, f32[8,4,4,2,1,128]{5,4,3,2,1,0:T(1,128)S(1)}) custom-call(bf16[32,256]{1,0:T(8,128)(2,1)S(1)} %copy-done.4, bf16[32,256]{1,0:T(8,128)(2,1)S(1)} %copy-done.6, s32[32,2]{1,0:T(8,128)S(1)} %copy.12.refs_2_.ids_ref, ...), custom_call_target="tpu_custom_call" | custom-call | tf_op jit(solution)/shard_map/gather_0/pallas_call | solution.py:233
  53.8 0.0 copy-start
  53.8 1.0 copy-done
  54.8 0.0 copy-start.1
  54.8 1.0 copy-done.1
  55.8 0.0 copy-start.3
  55.8 0.0 copy-start.5
  55.8 0.0 copy-start.7
  55.8 14.6 %expert.1 = (bf16[2,4,4,8,8,256]{5,4,3,2,1,0:T(8,128)(2,1)S(1)}, bf16[2,4,4,8,8,256]{5,4,3,2,1,0:T(8,128)(2,1)S(1)}, f32[256,1024]{1,0:T(8,128)}, f32[1024,256]{1,0:T(8,128)}, f32[8,128]{1,0:T(8,128)S(1)}) custom-call(bf16[8192,256]{1,0:T(8,128)(2,1)S(1)} %bitcast.12, bf16[8192,256]{1,0:T(8,128)(2,1)S(1)} %bitcast.14, f32[256,128]{1,0:T(8,128)S(1)} %bitcast.15, ...), custom_call_target="tpu_custom_call" | custom-call | tf_op jit(solution)/shard_map/expert/pallas_call | solution.py:340
  70.5 37.7 %return_rows.1 = (bf16[8,3,8,256]{3,2,1,0:T(8,128)(2,1)S(1)}, bf16[8,4,8,256]{3,2,1,0:T(8,128)(2,1)S(1)}, bf16[8,3,8,256]{3,2,1,0:T(8,128)(2,1)S(1)}, bf16[8,4,8,256]{3,2,1,0:T(8,128)(2,1)S(1)}) custom-call(f32[8,128]{1,0:T(8,128)S(1)} %get-tuple-element.23.hot_ref, bf16[2,4,4,8,8,256]{5,4,3,2,1,0:T(8,128)(2,1)S(1)} %get-tuple-element.24.refs_0_, ...), custom_call_target="tpu_custom_call" | custom-call | tf_op jit(solution)/shard_map/return_rows/pallas_call | solution.py:490
  108.2 0.0 copy-done.3
  108.2 0.0 copy-done.5
  108.3 0.0 copy-done.7
  108.3 1.3 combine.1
  109.6 17.9 %gather_2.1 = f32[8,4,4,2,1,128]{5,4,3,2,1,0:T(1,128)S(1)} custom-call(f32[1,128]{1,0:T(1,128)S(1)} %get-tuple-element.34.refs_0_), custom_call_target="tpu_custom_call" | custom-call | tf_op jit(solution)/shard_map/gather_2/pallas_call | solution.py:233
  127.4 4.2 %gate_grad.1 = f32[256,256]{1,0:T(8,128)} custom-call(bf16[8192,256]{1,0:T(8,128)(2,1)S(1)} %bitcast.13, f32[256,128]{1,0:T(8,128)S(1)} %bitcast.17, f32[256,128]{1,0:T(8,128)S(1)} %bitcast.20), custom_call_target="tpu_custom_call" | custom-call | tf_op jit(solution)/shard_map/gate_grad/pallas_call | solution.py:583
Async XLA Ops:
  1.4 0.9 copy-start.2
  2.3 0.7 copy-start.4
  3.0 0.7 copy-start.6
  53.8 1.0 copy-start
  54.8 1.0 copy-start.1
  55.8 52.4 %copy-start.3 = (bf16[256,256]{1,0:T(8,128)(2,1)S(1)}, bf16[256,256]{1,0:T(8,128)(2,1)}, u32[]{:S(2)}) copy-start(bf16[256,256]{1,0:T(8,128)(2,1)} %gate_ref.1) | copy-start | bytes 393220
  55.8 52.4 %copy-start.5 = (bf16[32,256]{1,0:T(8,128)(2,1)S(1)}, bf16[32,256]{1,0:T(8,128)(2,1)}, u32[]{:S(2)}) copy-start(bf16[32,256]{1,0:T(8,128)(2,1)} %tok_ref.1) | copy-start | bytes 49156
  55.8 52.4 %copy-start.7 = (bf16[32,256]{1,0:T(8,128)(2,1)S(1)}, bf16[32,256]{1,0:T(8,128)(2,1)}, u32[]{:S(2)}) copy-start(bf16[32,256]{1,0:T(8,128)(2,1)} %dout_ref.1) | copy-start | bytes 49156

commit v4 on v0

v4 whole, which is shorter than its diff:
```python
import functools
import itertools

import jax
import jax.numpy as jnp
from jax import lax
from jax.experimental import pallas as pl
from jax.experimental.pallas import tpu as pltpu
from jax.sharding import PartitionSpec as P

MESH = pl.DeviceIdType.MESH
F32 = jnp.float32
BF16 = jnp.bfloat16
CAP = 8


def coords(dims):
    nz, ny, nx, nc = dims
    me = lax.axis_index('ep')
    c = lax.rem(me, nc)
    x = lax.rem(me // nc, nx)
    y = lax.rem(me // (nc * nx), ny)
    z = me // (nc * nx * ny)

    def dev(z, y, x, c):
        return (((z * ny + y) * nx + x) * nc + c,)

    return z, y, x, c, dev


def meet(peers):
    barrier = pltpu.get_barrier_semaphore()
    for peer in peers:
        pl.semaphore_signal(barrier, inc=1, device_id=peer, device_id_type=MESH)
    pl.semaphore_wait(barrier, len(peers))


def dot(a, b, ca, cb):
    return lax.dot_general(a, b, (((ca,), (cb,)), ((), ())), preferred_element_type=F32)


def iota(shape, axis):
    return lax.broadcasted_iota(jnp.int32, shape, axis)


def as_row(col):
    n = col.shape[0]
    return jnp.sum(jnp.where(iota((n, n), 0) == iota((n, n), 1), col, 0.0), axis=0, keepdims=True)


def as_col(row):
    n = row.shape[1]
    return jnp.sum(jnp.where(iota((n, n), 0) == iota((n, n), 1), row, 0.0), axis=1, keepdims=True)


def gates(tok, i0, i1, w_gate):
    logits = dot(tok, w_gate, 1, 0)
    expert = iota(logits.shape, 1).astype(F32)
    l0, l1 = (jnp.sum(jnp.where(expert == i, logits, 0.0), axis=1, keepdims=True) for i in (i0, i1))
    top = jnp.maximum(l0, l1)
    p0, p1 = jnp.exp(l0 - top), jnp.exp(l1 - top)
    total = p0 + p1
    return p0 / total, p1 / total


def choice_row(tok, ids, w_gate):
    r0, r1 = ids[0:1].astype(F32), ids[1:2].astype(F32)
    i0, i1 = as_col(r0), as_col(r1)
    g0, g1 = gates(tok, i0, i1, w_gate)

    def code(i):
        n = jnp.sum((i == r0).astype(F32) + (i == r1).astype(F32), axis=1, keepdims=True)
        return as_row(jnp.where(n > 1.5, i + 256.0, i))

    return jnp.concatenate([code(i0), code(i1), as_row(g0), as_row(g1)], axis=1)


def gelu_parts(a):
    k = 0.7978845608028654
    sq = a * a
    t = jnp.tanh(a * (k + (k * 0.044715) * sq))
    half = 0.5 + 0.5 * t
    slope = half + (0.5 * a) * (1.0 - t * t) * (k + (3 * k * 0.044715) * sq)
    return a * half, slope


def token_lanes(ref, k, start, n):
    lane = iota((n, 128), 1) // 32
    out = jnp.zeros((n, 128), F32)
    for j in range(4):
        r = ref[pl.ds(start + j, n, stride=4), :]
        out = jnp.where(lane == j, r if j == k else pltpu.roll(r, 32 * (j - k) % 128, 1), out)
    return out


def pair_rows(v):
    return jnp.concatenate([jnp.concatenate([v[2 * i:2 * i + 1], v[2 * i + 1:2 * i + 2]], axis=1) for i in range(v.shape[0] // 2)], axis=0)


def plain_id(code):
    return jnp.where(code >= 256.0, code - 256.0, code)


class Links:
    def __init__(self, send, recv, sent):
        self.send, self.recv, self.sent, self.k = send, recv, sent, 0

    def go(self, src, dst, to):
        cp = pltpu.make_async_remote_copy(src_ref=src, dst_ref=dst, send_sem=self.send.at[self.k], recv_sem=self.recv.at[self.k], device_id=to, device_id_type=MESH)
        self.k += 1
        cp.start()
        self.sent.append(cp)
        return cp


def take_turns(plans):
    live = list(plans)
    while live:
        for g in list(live):
            if next(g, 'end') == 'end':
                live.remove(g)


def block_kernel(dims, sizes, *refs):
    nz, ny, nx, nc = dims
    refs = iter(refs)
    refs = [list(itertools.islice(refs, n)) for n in sizes]
    (tok_hbm, dout_hbm, ids_hbm, wg_hbm, w1_hbm, w2_hbm), outs, held, kept, rows, works, (load_sem, keep_sem, save_sem), sems = refs
    out_ref, gx_ref, x_all, m_all, d_land, g1_ref, g2_ref = held
    tok, dout, ids, wg, w1, w2, row, m_land, g_all, xs_ref, dys_ref, h_ref, da_ref, hot_ref, d_row = kept
    z, y, x, c, dev = coords(dims)
    sent, saves = [], []

    def save(k, part=None):
        src, dst = (held[k], outs[k]) if part is None else (held[k].at[part], outs[k].at[part])
        cp = pltpu.make_async_copy(src, dst, save_sem.at[len(saves)])
        cp.start()
        saves.append(cp)

    links = [Links(send, recv, sent) for send, recv in zip(sems[::2], sems[1::2])]

    loads = [pltpu.make_async_copy(s, d, load_sem.at[k]) for k, (s, d) in enumerate(
        [(tok_hbm, x_all.at[z, y, x, c]), (dout_hbm, g_all.at[z, y, x, c]), (tok_hbm, tok), (ids_hbm, ids), (wg_hbm, wg), (dout_hbm, dout), (w1_hbm, w1), (w2_hbm, w2)])]
    for ld in loads:
        ld.start()
    peers = [dev(lax.rem(z + d, nz), y, x, c) for d in range(1, nz)]
    for d in (1, 2, 3):
        peers.append(dev(z, lax.rem(y + d, ny), x, c))
        peers.append(dev(z, y, lax.rem(x + d, nx), c))
    peers.append(dev(z, y, x, 1 - c))
    meet(peers)

    full = slice(None)

    def along_z(link, ref):
        return [link.go(ref.at[z, y, x, c], ref.at[z, y, x, c], dev(lax.rem(z + d, nz), y, x, c)) for d in range(1, nz)]

    def gather(i, held, zcopies):
        link = links[i]
        yx = i == 0
        p0, q0 = (y, x) if yx else (x, y)
        low, high = pl.ds(0, nz // 2), pl.ds(nz // 2, nz // 2)

        def at(zs, p, q):
            return held.at[zs, p, q, c] if yx else held.at[zs, q, p, c]

        def to(p, q):
            return dev(z, p, q, c) if yx else dev(z, q, p, c)

        def go(ref, to):
            return link.go(ref, ref, to)

        def step(v, d):
            return lax.rem(v + d, 4)

        cross = []

        def over(p, q):
            cross.append(go(at(full, p, q), dev(z, y, x, 1 - c)))

        for cp in zcopies:
            yield
            cp.wait_recv()
        pm, pp, po = step(p0, 3), step(p0, 1), step(p0, 2)
        qm, qp, qo = step(q0, 3), step(q0, 1), step(q0, 2)
        p_up = go(at(full, p0, q0), to(pp, q0))
        p_dn = go(at(full, p0, q0), to(pm, q0))
        qs, relays = [], []

        def spread(p):
            qs.append((p, go(at(full, p, q0), to(p0, qp)), go(at(full, p, q0), to(p0, qm))))
            over(p, q0)

        def relay(i):
            p, up, dn = qs[i]
            up.wait_recv()
            r_up = go(at(low, p, qm), to(p0, qp))
            over(p, qm)
            dn.wait_recv()
            r_dn = go(at(high, p, qp), to(p0, qm))
            over(p, qp)
            relays.append((p, r_up, r_dn))

        spread(p0)
        yield
        p_up.wait_recv()
        f_up = go(at(low, pm, q0), to(pp, q0))
        yield
        p_dn.wait_recv()
        f_dn = go(at(high, pp, q0), to(pm, q0))
        spread(pm)
        spread(pp)
        yield
        relay(0)
        yield
        f_up.wait_recv()
        f_dn.wait_recv()
        spread(po)
        for i in range(1, 5):
            yield
            if i < 4:
                relay(i)
            p, r_up, r_dn = relays[i - 1]
            r_up.wait_recv()
            r_dn.wait_recv()
            over(p, qo)
        for cp in cross:
            yield
            cp.wait_recv()

    def gather_rows(link, held, order):
        have = [z, y, x, c]
        for axis in order:
            size = (nz, ny, nx, nc)[axis]
            part = held.at[tuple(have)]
            copies = []
            for d in range(1, size):
                there = [z, y, x, c]
                there[axis] = lax.rem(there[axis] + d, size)
                copies.append(link.go(part, part, dev(*there)))
            have[axis] = full
            for cp in copies:
                yield
                cp.wait_recv()

    loads[0].wait()
    z_tok = along_z(links[0], x_all)
    loads[1].wait()
    z_dout = along_z(links[1], g_all)
    for ld in loads[2:5]:
        ld.wait()
    row[...] = choice_row(tok[...], ids[...], wg[...])
    place = pltpu.make_async_copy(row, m_land.at[z, y, x, c], keep_sem.at[0])
    place.start()
    place.wait()
    take_turns([gather(0, x_all, z_tok), gather(1, g_all, z_dout), gather_rows(links[2], m_land, (0, 1, 2, 3))])

    def flatten(zz, carry):
        for k in range(ny * nx * nc):
            m_all[pl.ds(zz * (ny * nx * nc) + k, 1), :] = m_land[zz, k // (nx * nc), k // nc % nx, k % nc]
        return carry

    lax.fori_loop(0, nz, flatten, 0)
    for ld in loads[5:]:
        ld.wait()
    save(2)
    save(3)

    me = lax.axis_index('ep').astype(F32)
    code = m_all[...]
    left = jnp.where((iota(code.shape, 1) < 64) & (code >= 256.0), code - 256.0, 999.0)
    found = []
    for _ in range(3):
        best = jnp.min(jnp.min(left, axis=0, keepdims=True), axis=1, keepdims=True)
        left = jnp.where(left == best, 999.0, left)
        found.append(jnp.broadcast_to(best, (1, 128)))
    hot_ref[...] = jnp.concatenate(found + [jnp.full((5, 128), 999.0, F32)], axis=0)
    steps = 4 if nz == 8 else 1
    per = nz // steps
    n_quad = per * ny * nx * nc // 4
    n_pair = n_quad // 2
    n_slot = n_pair * 8 * CAP

    def run_expert(i, carry):
        c0, c1, g0, g1 = (pair_rows(token_lanes(m_all, k, pl.multiple_of(4 * n_quad * i, 4 * n_quad), n_quad)) for k in range(4))
        hit0, hit1 = plain_id(c0) == me, plain_id(c1) == me
        hit = (hit0 | hit1).astype(F32)
        gate = jnp.where(hit0, g0, 0.0) + jnp.where(hit1, g1, 0.0)
        before, after = iota((256, 256), 0), iota((256, 256), 1)
        tri = ((before < after) & (before // 32 == after // 32)).astype(F32).astype(BF16)
        rank = dot(hit.astype(BF16), tri, 1, 0)
        src = (iota((n_pair, 256), 1) // 32).astype(F32)
        key = jnp.where(hit > 0.0, src * CAP + rank, -1.0)
        slot = iota((8 * CAP, 256), 0).astype(F32)
        xs, dys = [], []
        for p in range(n_pair):
            sel = (slot == key[p:p + 1]).astype(F32)
            g = jnp.sum(sel * gate[p:p + 1], axis=1, keepdims=True)
            sel = sel.astype(BF16)
            xs.append(dot(sel, x_all[i * per + p // ny, p % ny].reshape(256, 256), 1, 0))
            dys.append(g * dot(sel, g_all[i * per + p // ny, p % ny].reshape(256, 256), 1, 0))
        places = [(cc, xx, yy, zz) for cc in range(nc) for xx in range(nx) for yy in range(ny) for zz in range(per)]

        def by_place(parts):
            return jnp.concatenate([parts[zz * ny + yy][8 * (xx * nc + cc):8 * (xx * nc + cc + 1)] for cc, xx, yy, zz in places], axis=0).astype(BF16)

        xs, dys = by_place(xs), by_place(dys)
        h, slope = gelu_parts(dot(xs, w1[...], 1, 0))
        h = h.astype(BF16)
        here = pl.ds(pl.multiple_of(i * n_slot, n_slot), n_slot)
        xs_ref[here], dys_ref[here], h_ref[here] = xs, dys, h
        yv = dot(h, w2[...], 1, 0)
        da = (dot(dys, w2[...], 1, 1) * slope).astype(BF16)
        da_ref[here] = da
        dxv = dot(da, w1[...], 1, 1)
        for k, (cc, xx, yy, zz) in enumerate(places):
            for half in range(2):
                lanes = slice(128 * half, 128 * (half + 1))
                rows[half][cc, xx, yy, i * per + zz] = yv[8 * k:8 * (k + 1), lanes].astype(BF16)
                rows[2 + half][cc, xx, yy, i * per + zz] = dxv[8 * k:8 * (k + 1), lanes].astype(BF16)
        return carry

    lax.fori_loop(0, steps, run_expert, 0)

    def back(i):
        h = rows[i]
        other, near, via, out2, via2, in2, out3, hot_land, cold_land = works[9 * i:9 * i + 9]
        go = links[3 + i].go
        x_first = i % 2 == 0
        a, b = (x, y) if x_first else (y, x)

        def to(a, b):
            return dev(z, b, a, c) if x_first else dev(z, a, b, c)

        def index(lead, a, bs):
            return lead + ((a, bs) if x_first else (bs, a))

        def step(v, d):
            return lax.rem(v + d, 4)

        up, dn, far = step(a, 1), step(a, 3), step(a, 2)
        lo, hi = pl.ds(0, 2), pl.ds(2, 2)
        cross = go(h.at[1 - c], other, dev(z, y, x, 1 - c))

        def spread(ref, lead, e):
            return [go(ref.at[index(lead, far, lo)], via.at[0, e], to(up, b)), go(ref.at[index(lead, far, hi)], via.at[1, e], to(dn, b)),
                    go(ref.at[index(lead, up, full)], near.at[a, e], to(up, b)), go(ref.at[index(lead, dn, full)], near.at[a, e], to(dn, b))]

        def relay(cps, e):
            cps[0].wait_recv()
            r_up = go(via.at[0, e], near.at[dn, e, lo], to(up, b))
            cps[1].wait_recv()
            r_dn = go(via.at[1, e], near.at[up, e, hi], to(dn, b))
            return [cps[2], cps[3], r_up, r_dn]

        own = spread(h, (c,), c)
        yield
        cross.wait_recv()
        his = spread(other, (), 1 - c)
        yield
        waits = relay(own, c)
        yield
        waits += relay(his, 1 - c)
        yield
        for cp in waits:
            cp.wait_recv()

        def expert(s, e):
            return ((z * ny + y) * nx + s) * nc + e if x_first else ((z * ny + s) * nx + x) * nc + e

        places = [(step(a, d), e) for d in range(4) for e in (c, 1 - c)]
        is_hot = [[(hot_ref[j:j + 1, :] == expert(s, e).astype(F32)).astype(F32) for s, e in places] for j in range(3)]
        wide = lambda v: jnp.broadcast_to(v, (8, 128))
        weight = [[wide(v).astype(BF16) for v in r] for r in is_hot]
        line = iota((8, 128), 0)
        mine = [(wide(is_hot[0][k] + is_hot[1][k] + is_hot[2][k]) < 0.5) & (line == s * nc + e) for k, (s, e) in enumerate(places)]

        def squeeze(bb, carry):
            parts = [h[index((c,), a, bb)], other[index((), a, bb)]] + [near[s, e, bb] for s, e in places[2:]]
            for j in range(3):
                out2[bb, j] = sum(parts[k] * weight[j][k] for k in range(8))
            singles = jnp.zeros((nz, 8, 128), F32)
            for k in range(8):
                singles = jnp.where(mine[k], jnp.sum(parts[k].astype(F32), axis=1, keepdims=True), singles)
            out2[bb, 3] = singles.astype(BF16)
            return carry

        lax.fori_loop(0, 4, squeeze, 0)
        up, dn, far = step(b, 1), step(b, 3), step(b, 2)
        lo, hi = pl.ds(0, nz // 2), pl.ds(nz // 2, nz // 2)
        f_up, f_dn = go(out2.at[far, :, lo], via2.at[0], to(a, up)), go(out2.at[far, :, hi], via2.at[1], to(a, dn))
        n_up, n_dn = go(out2.at[up], in2.at[b], to(a, up)), go(out2.at[dn], in2.at[b], to(a, dn))
        in2[b] = out2[b]
        yield
        f_up.wait_recv()
        r_up = go(via2.at[0], in2.at[dn, :, lo], to(a, up))
        f_dn.wait_recv()
        r_dn = go(via2.at[1], in2.at[up, :, hi], to(a, dn))
        yield
        for cp in (n_up, n_dn, r_up, r_dn):
            cp.wait_recv()
        for j in range(3):
            out3[:, j] = (in2[0, j] + in2[1, j]) + (in2[2, j] + in2[3, j])
        last = []
        for d in range(1, nz):
            zz = lax.rem(z + d, nz)
            last.append(go(in2.at[:, 3, zz], cold_land.at[z], dev(zz, y, x, c)))
        for d in range(1, nz):
            zz = lax.rem(z + d, nz)
            last.append(go(out3.at[zz], hot_land.at[z], dev(zz, y, x, c)))
        cold_land[z] = in2[:, 3, z]
        hot_land[z] = out3[z]
        yield
        for cp in last:
            cp.wait_recv()

    def weight_grad(k):
        if k % 2 == 0:
            part = slice(w2.shape[0] // 4 * (k // 2), w2.shape[0] // 4 * (k // 2 + 1))
            g2_ref[part, :] = dot(h_ref[:, part], dys_ref[...], 0, 0)
            save(6, (part, full))
        else:
            part = slice(w1.shape[1] // 4 * (k // 2), w1.shape[1] // 4 * (k // 2 + 1))
            g1_ref[:, part] = dot(xs_ref[...], da_ref[:, part], 0, 0)
            save(5, (full, part))

    ys, dxs = [back(0), back(1)], [back(2), back(3)]

    def advance(plans):
        for g in plans:
            next(g, None)

    todo = list(range(8))

    for turn in 'y x w y x ww yy w xx y w x y w y w xx w y'.replace(' ', ''):
        if turn == 'w':
            weight_grad(todo.pop(0))
        else:
            advance(ys if turn == 'y' else dxs)

    r0, r1 = ids[0:1].astype(F32), ids[1:2].astype(F32)
    i0, i1 = as_col(r0), as_col(r1)
    tokens = tok[...]
    g0, g1 = gates(tokens, i0, i1, wg[...])
    n_tok = tok.shape[0]
    earlier = iota((n_tok, n_tok), 1) < iota((n_tok, n_tok), 0)
    n_exp = wg.shape[1]

    def where_from(i):
        rank = jnp.sum(jnp.where(earlier & ((i == r0) | (i == r1)), 1.0, 0.0), axis=1, keepdims=True)
        slot = jnp.full((n_tok, 1), -1.0, F32)
        for j in range(3):
            slot = jnp.where(i == hot_ref[j:j + 1, 0:1], CAP * j + rank, slot)
        e = i.astype(jnp.int32)
        core, xx, yy, zz = e % nc, (e // nc) % nx, (e // (nc * nx)) % ny, e // (nc * nx * ny)
        lane, single = iota((n_tok, n_exp), 1), slot < 0.0
        pick = lambda m: m.astype(F32).astype(BF16)
        return pick(iota((n_tok, 32), 1).astype(F32) == slot), (pick((lane == e) & single), pick((lane == ((zz * nx + xx) * ny + yy) * nc + core) & single))

    chosen = [where_from(i0), where_from(i1)]

    def rows_of(kind):
        parts = []
        for half in range(2):
            hot_land, cold_land = works[9 * (kind + half) + 7:9 * (kind + half) + 9]
            hot = jnp.sum(hot_land[...].astype(F32), axis=0).reshape(24, 128)
            hot = jnp.concatenate([hot, jnp.zeros((8, 128), F32)], axis=0).astype(BF16)
            cold = cold_land[...].astype(F32).reshape(n_exp, 128).astype(BF16)
            parts.append([dot(by_slot, hot, 1, 0) + dot(by_place[half], cold, 1, 0) for by_slot, by_place in chosen])
        return [jnp.concatenate([parts[0][k], parts[1][k]], axis=1) for k in range(2)]

    y0, y1 = rows_of(0)
    out_ref[...] = (g0 * y0 + g1 * y1).astype(BF16)
    save(0)
    grad = dout[...].astype(F32)
    dg0, dg1 = (jnp.sum(grad * v, axis=1, keepdims=True) for v in (y0, y1))
    mean = g0 * dg0 + g1 * dg1
    d0, d1 = ((g * (dg - mean)).astype(BF16).astype(F32) for g, dg in ((g0, dg0), (g1, dg1)))
    d_row[...] = jnp.concatenate([as_row(d0), as_row(d1), jnp.zeros((1, 2 * n_tok), F32)], axis=1)
    place = pltpu.make_async_copy(d_row, d_land.at[z, y, x, c], keep_sem.at[1])
    place.start()
    place.wait()
    d_plan = gather_rows(links[7], d_land, (1, 2, 0, 3))
    next(d_plan)
    advance(dxs)
    expert = iota((n_tok, n_exp), 1).astype(F32)
    spread = jnp.where(expert == i0, d0, jnp.where(expert == i1, d1, 0.0)).astype(BF16)
    through_gate = dot(spread, wg[...], 1, 1)
    for _ in range(6):
        next(d_plan)
    advance(dxs)
    dx0, dx1 = rows_of(2)
    gx_ref[...] = (dx0 + dx1 + through_gate).astype(BF16)
    save(1)
    take_turns([d_plan])
    save(4)
    for cp in sent:
        cp.wait_send()
    for cp in saves:
        cp.wait()


def block_call(dims, tokens, grad_out, ids, w_gate, w1, w2):
    nz, ny, nx, nc = dims
    d_model, d_hidden = w1.shape
    n_tok = tokens.shape[0]
    n_dev = nz * ny * nx * nc
    n_row = n_dev * CAP
    tile = (CAP, 128)
    hbm = pl.BlockSpec(memory_space=pltpu.HBM)
    out = jax.ShapeDtypeStruct
    work = [(4, 4, nz), (4, 2, 4, nz), (2, 2, 2, nz), (4, 4, nz), (2, 4, nz // 2), (4, 4, nz), (nz, 3), (nz, 3), (nz, 4)]
    counts = [nz - 1 + 4 + 16 + 16] * 2 + [nz - 1 + 3 + 3 + 1] + [1 + 12 + 6 + 2 * (nz - 1)] * 4 + [nz - 1 + 3 + 3 + 1]
    sems = []
    for k in counts:
        sems += [pltpu.SemaphoreType.DMA((k,))] * 2
    results = [(tokens.shape, BF16), (tokens.shape, BF16), (dims + tokens.shape, BF16), ((n_dev, 128), F32), (dims + (1, 128), F32),
               ((d_model, d_hidden), F32), ((d_hidden, d_model), F32)]
    row, n_dma = (1, 128), 16
    kept = [(tokens.shape, BF16), (tokens.shape, BF16), (ids.shape, jnp.int32), (w_gate.shape, BF16), (w1.shape, BF16), (w2.shape, BF16), (row, F32), (dims + row, F32),
            (dims + tokens.shape, BF16), ((n_row, d_model), BF16), ((n_row, d_model), BF16), ((n_row, d_hidden), BF16), ((n_row, d_hidden), BF16), (tile, F32), (row, F32)]
    return pl.pallas_call(
        functools.partial(block_kernel, dims, (6, len(results), len(results), len(kept), 4, 4 * len(work), 3, len(sems))),
        out_shape=[out(*r) for r in results],
        in_specs=[hbm] * 6,
        out_specs=[hbm] * 7,
        scratch_shapes=[pltpu.VMEM(*r) for r in results + kept] + [pltpu.VMEM((nc, nx, ny, nz) + tile, BF16)] * 4 + [pltpu.VMEM(w + tile, BF16) for w in work] * 4
        + [pltpu.SemaphoreType.DMA((n_dma,))] * 3 + sems,
        compiler_params=pltpu.CompilerParams(collective_id=0, has_side_effects=True, vmem_limit_bytes=VMEM_LIMIT),
        name='block',
    )(tokens, grad_out, ids, w_gate, w1, w2)


VMEM_LIMIT = 67043328


def gate_kernel(x_ref, m_ref, d_ref, g1_ref, g2_ref, out_ref, gx_ref, o_ref, o1_ref, o2_ref, o3_ref, o4_ref, acc):
    o1_ref[...] = g1_ref[...]
    o2_ref[...] = g2_ref[...]
    o3_ref[...] = out_ref[...]
    o4_ref[...] = gx_ref[...]
    n_quad = m_ref.shape[0] // 4
    i0, i1 = (plain_id(pair_rows(token_lanes(m_ref, k, 0, n_quad))) for k in range(2))
    d0, d1 = (pair_rows(token_lanes(d_ref, k, 0, n_quad)) for k in range(2))
    expert = iota((acc.shape[0], 256), 0).astype(F32)

    @pl.when(pl.program_id(0) == 0)
    def _():
        acc[...] = jnp.zeros_like(acc)

    total = acc[...]
    for p in range(n_quad // 2):
        q = slice(p, p + 1)
        spread = jnp.where(expert == i0[q], d0[q], jnp.where(expert == i1[q], d1[q], 0.0))
        total += dot(spread.astype(BF16), x_ref[256 * p:256 * (p + 1)], 1, 0)
    acc[...] = total

    @pl.when(pl.program_id(0) == pl.num_programs(0) - 1)
    def _():
        o_ref[...] = total.T


def gate_grad(x_all, m_all, d_all, *through):
    n_src = m_all.shape[0]
    steps = 4 if n_src == 256 else 2
    d_model = x_all.shape[1]
    part = lambda shape: pl.BlockSpec((shape[0] // steps,) + shape[1:], lambda i: (i, 0))
    whole = lambda shape: pl.BlockSpec(shape, lambda i: (0, 0))
    specs = [part(v.shape) if v.shape[0] >= 64 else whole(v.shape) for v in through]
    out = jax.ShapeDtypeStruct
    return pl.pallas_call(
        gate_kernel,
        grid=(steps,),
        out_shape=[out((d_model, n_src), F32)] + [out(v.shape, v.dtype) for v in through],
        in_specs=[part(x_all.shape), part(m_all.shape), part(d_all.shape)] + specs,
        out_specs=[whole((d_model, n_src))] + specs,
        scratch_shapes=[pltpu.VMEM((n_src, d_model), F32)],
        compiler_params=pltpu.CompilerParams(dimension_semantics=('arbitrary',), vmem_limit_bytes=VMEM_LIMIT),
        name='gate_grad',
    )(x_all, m_all, d_all, *through)


def local_block(dims, tokens, grad_out, expert_ids, w_gate, w_in, w_out):
    n_exp = w_gate.shape[1]
    y_out, grad_x, x_all, m_all, d_all, g1, g2 = block_call(dims, tokens, grad_out, expert_ids.T, w_gate, w_in[0], w_out[0])
    grad_w_gate, g1, g2, y_out, grad_x = gate_grad(x_all.reshape(-1, tokens.shape[1]), m_all, d_all.reshape(n_exp, 128), g1, g2, y_out, grad_x)
    return y_out, grad_x, g1[None], g2[None], grad_w_gate


def solution(mesh):
    dims = (8, 4, 4, 2)
    return jax.shard_map(functools.partial(local_block, dims), mesh=mesh, in_specs=(P('ep'), P('ep'), P('ep'), P(), P('ep'), P('ep')), out_specs=(P('ep'), P('ep'), P('ep'), P('ep'), P()), check_vma=False)
```

time: 467 us -> 113 us (0.24)
  waiting for transfers between devices: 297 us -> 0 us
  Pallas kernels: 0 us -> 112 us
  blocking collectives: 82.4 us -> 0 us
  matrix products: 29.2 us -> 0 us
  local copies, waits for them, and re-layouts: 25.3 us -> 0 us
  between operations: 14.3 us -> 0.64 us
  starting transfers between devices: 13.5 us -> 0 us
    psum x1 -> x0, waiting for transfers between devices: 268 us -> none  [local_block(): lax.psum(jnp.einsum('tm,te->me', tokens, d_logits, preferred_element_type...]
    pallas_call x0 -> x2, Pallas kernels: none -> 112 us  [the longest x1 106 us: block_call(): pl.pallas_call(functools.partial(block_kernel, dims, (6, len(results), le...]
    all_to_all x2 -> x0, blocking collectives: 82.4 us -> none  [the longest x1 45.7 us: local_block(): lax.all_to_all(send_x.reshape(n_exp, cap_rows, d_model), 'ep', 0, 0, tile...]
    all_to_all x2 -> x0, waiting for transfers between devices: 29.5 us -> none  [the longest x1 29.5 us: local_block(): lax.all_to_all(y_rows.reshape(n_exp, cap_rows, d_model), 'ep', 0, 0, tile...]
    dot_general x10 -> x0, matrix products: 29.2 us -> none  [the longest x1 8.5 us: local_block(): jnp.einsum('rm,hm->rh', recv_dy, w_two, preferred_element_type=jnp.float32)]
    gather x4 -> x0, local copies, waits for them, and re-layouts: 16.4 us -> none  [the longest x1 7.5 us: local_block(): jnp.take(jnp.concatenate([dy_flat, zero_row], axis=0), src_choice, axis=0)]
    all_to_all x2 -> x0, starting transfers between devices: 13.5 us -> none  [the longest x1 6.74 us: local_block(): lax.all_to_all(dx_rows.reshape(n_exp, cap_rows, d_model), 'ep', 0, 0, til...]
    unnamed x20 -> x0, local copies, waits for them, and re-layouts: 6.45 us -> none
  transfers between devices with their start and end apart: 3 -> 0, of which waited for: 2 -> 0; matrix products, arithmetic and copies ran while one was open for 3% -> 0% of each run, Pallas kernels for 0% -> 0%
where the time goes in v4:
time: 113 us
  Pallas kernels  112 us (99%)
    pallas_call x1, Pallas kernels, block_call(): pl.pallas_call(functools.partial(block_kernel, dims, (6, len(results), le...  106 us
    pallas_call x1, Pallas kernels, gate_grad(): pl.pallas_call(gate_kernel, grid=(steps,), out_shape=[out((d_model, n_src...  6.02 us

profile of v4, /device:TPU:1, one launch (start us, length us, event | category | flops | bytes accessed | tf_op | source)
XLA Modules:
  0.0 112.7 jit_solution(10927826943282080637)
XLA Ops:
  0.6 106.0 %block.1 = (bf16[32,256]{1,0:T(8,128)(2,1)}, bf16[32,256]{1,0:T(8,128)(2,1)}, bf16[8,4,4,2,32,256]{5,4,3,2,1,0:T(8,128)(2,1)}, f32[256,128]{1,0:T(8,128)}, f32[8...) custom-call(bf16[32,256]{1,0:T(8,128)(2,1)} %refs_0_.1, bf16[32,256]{1,0:T(8,128)(2,1)} %refs_1_.1, ...), custom_call_target="tpu_custom_call" | custom-call | tf_op jit(solution)/shard_map/block/pallas_call | solution.py:522
  106.7 6.0 %gate_grad.1 = (f32[256,256]{1,0:T(8,128)}, f32[256,1024]{1,0:T(8,128)}, f32[1024,256]{1,0:T(8,128)}, bf16[32,256]{1,0:T(8,128)(2,1)}, bf16[32,256]{1,0:T(8,128)(2,1)}) custom-call(bf16[8192,256]{1,0:T(8,128)(2,1)} %bitcast.7, f32[256,128]{1,0:T(8,128)} %get-tuple-element.18.m_ref, f32[256,128]{1,0:T(8,128)} %bitcast.10, ...), custom_call_target="tpu_custom_call" | custom-call | tf_op jit(solution)/shard_map/gate_grad/pallas_call | solution.py:571

commit v5 on v4

--- a/solution.py
+++ b/solution.py
@@ -127,7 +127,7 @@
     refs = [list(itertools.islice(refs, n)) for n in sizes]
     (tok_hbm, dout_hbm, ids_hbm, wg_hbm, w1_hbm, w2_hbm), outs, held, kept, rows, works, (load_sem, keep_sem, save_sem), sems = refs
     out_ref, gx_ref, x_all, m_all, d_land, g1_ref, g2_ref = held
-    tok, dout, ids, wg, w1, w2, row, m_land, g_all, xs_ref, dys_ref, h_ref, da_ref, hot_ref, d_row = kept
+    tok, dout, ids, wg, w1, w2, row, m_land, g_all, xs_ref, dys_ref, h_ref, da_ref, slope_ref, hot_ref, d_row = kept
     z, y, x, c, dev = coords(dims)
     sent, saves = [], []
 
@@ -137,7 +137,7 @@
         cp.start()
         saves.append(cp)
 
-    links = [Links(send, recv, sent) for send, recv in zip(sems[::2], sems[1::2])]
+    links = iter([Links(send, recv, sent) for send, recv in zip(sems[::2], sems[1::2])])
 
     loads = [pltpu.make_async_copy(s, d, load_sem.at[k]) for k, (s, d) in enumerate(
         [(tok_hbm, x_all.at[z, y, x, c]), (dout_hbm, g_all.at[z, y, x, c]), (tok_hbm, tok), (ids_hbm, ids), (wg_hbm, wg), (dout_hbm, dout), (w1_hbm, w1), (w2_hbm, w2)])]
@@ -147,67 +147,58 @@
     for d in (1, 2, 3):
         peers.append(dev(z, lax.rem(y + d, ny), x, c))
         peers.append(dev(z, y, lax.rem(x + d, nx), c))
-    peers.append(dev(z, y, x, 1 - c))
+    mate = dev(z, y, x, 1 - c)
+    peers.append(mate)
     meet(peers)
 
     full = slice(None)
 
-    def along_z(link, ref):
-        return [link.go(ref.at[z, y, x, c], ref.at[z, y, x, c], dev(lax.rem(z + d, nz), y, x, c)) for d in range(1, nz)]
-
-    def gather(i, held, zcopies):
-        link = links[i]
-        yx = i == 0
-        p0, q0 = (y, x) if yx else (x, y)
+    def step(v, d, m=4):
+        return lax.rem(v + d, m)
+
+    def by_lines(link, ref, rows, x_last):
+        p0, q0 = (y, x) if x_last else (x, y)
         low, high = pl.ds(0, nz // 2), pl.ds(nz // 2, nz // 2)
 
         def at(zs, p, q):
-            return held.at[zs, p, q, c] if yx else held.at[zs, q, p, c]
-
-        def to(p, q):
-            return dev(z, p, q, c) if yx else dev(z, q, p, c)
-
-        def go(ref, to):
-            return link.go(ref, ref, to)
-
-        def step(v, d):
-            return lax.rem(v + d, 4)
+            return ref.at[(zs, p, q, c, rows) if x_last else (zs, q, p, c, rows)]
+
+        def go(part, p, q):
+            return link.go(part, part, dev(z, p, q, c) if x_last else dev(z, q, p, c))
 
         cross = []
 
-        def over(p, q):
-            cross.append(go(at(full, p, q), dev(z, y, x, 1 - c)))
-
-        for cp in zcopies:
-            yield
+        def over(q):
+            part = at(full, full, q)
+            cross.append(link.go(part, part, mate))
+
+        own = at(z, p0, q0)
+        first = [link.go(own, own, dev(step(z, d, nz), y, x, c)) for d in range(1, nz)]
+        yield
+        for cp in first:
             cp.wait_recv()
         pm, pp, po = step(p0, 3), step(p0, 1), step(p0, 2)
         qm, qp, qo = step(q0, 3), step(q0, 1), step(q0, 2)
-        p_up = go(at(full, p0, q0), to(pp, q0))
-        p_dn = go(at(full, p0, q0), to(pm, q0))
         qs, relays = [], []
 
         def spread(p):
-            qs.append((p, go(at(full, p, q0), to(p0, qp)), go(at(full, p, q0), to(p0, qm))))
-            over(p, q0)
+            part = at(full, p, q0)
+            qs.append((p, go(part, p0, qp), go(part, p0, qm)))
 
         def relay(i):
             p, up, dn = qs[i]
             up.wait_recv()
-            r_up = go(at(low, p, qm), to(p0, qp))
-            over(p, qm)
+            relays.append(go(at(low, p, qm), p0, qp))
             dn.wait_recv()
-            r_dn = go(at(high, p, qp), to(p0, qm))
-            over(p, qp)
-            relays.append((p, r_up, r_dn))
-
+            relays.append(go(at(high, p, qp), p0, qm))
+
+        p_up, p_dn = go(at(full, p0, q0), pp, q0), go(at(full, p0, q0), pm, q0)
         spread(p0)
         yield
         p_up.wait_recv()
-        f_up = go(at(low, pm, q0), to(pp, q0))
-        yield
+        f_up = go(at(low, pm, q0), pp, q0)
         p_dn.wait_recv()
-        f_dn = go(at(high, pp, q0), to(pm, q0))
+        f_dn = go(at(high, pp, q0), pm, q0)
         spread(pm)
         spread(pp)
         yield
@@ -216,16 +207,59 @@
         f_up.wait_recv()
         f_dn.wait_recv()
         spread(po)
-        for i in range(1, 5):
+        over(q0)
+        for i in range(1, 4):
             yield
-            if i < 4:
-                relay(i)
-            p, r_up, r_dn = relays[i - 1]
-            r_up.wait_recv()
-            r_dn.wait_recv()
-            over(p, qo)
+            relay(i)
+        over(qm)
+        over(qp)
+        yield
+        for cp in relays:
+            cp.wait_recv()
+        over(qo)
+        yield
         for cp in cross:
+            cp.wait_recv()
+
+    def by_planes(link, ref, rows):
+        go = lambda part, *to: link.go(part, part, dev(*to))
+        at = lambda zz, ys=full: ref.at[zz, ys, full, c, rows]
+        own = ref.at[z, y, x, c, rows]
+        xs = [go(own, z, y, step(x, d), c) for d in range(1, nx)]
+        yield
+        for cp in xs:
+            cp.wait_recv()
+        line = ref.at[z, y, full, c, rows]
+        ys = [go(line, z, step(y, d), x, c) for d in range(1, ny)]
+        yield
+        for cp in ys:
+            cp.wait_recv()
+        cross = []
+
+        def over(*planes):
+            for zz in planes:
+                cross.append(link.go(at(zz), at(zz), mate))
+
+        half = nz // 2
+        lower, upper = pl.ds(0, ny // 2), pl.ds(ny // 2, ny // 2)
+
+        def pair(d):
+            a, b = (full, full) if d + 1 < half else (lower, upper)
+            return go(at(step(z, nz - d, nz), a), step(z, 1, nz), y, x, c), go(at(step(z, d, nz), b), step(z, nz - 1, nz), y, x, c)
+
+        up, dn = pair(0)
+        over(z)
+        for d in range(1, half + 1):
             yield
+            up.wait_recv()
+            dn.wait_recv()
+            if d < half:
+                up, dn = pair(d)
+                over(step(z, d, nz), step(z, nz - d, nz))
+            else:
+                over(step(z, d, nz))
+        yield
+        for cp in cross:
             cp.wait_recv()
 
     def gather_rows(link, held, order):
@@ -239,21 +273,34 @@
                 there[axis] = lax.rem(there[axis] + d, size)
                 copies.append(link.go(part, part, dev(*there)))
             have[axis] = full
+            yield
             for cp in copies:
-                yield
                 cp.wait_recv()
 
+    def advance(plans):
+        for g in plans:
+            next(g, None)
+
+    def streams(ref, cuts):
+        a, b, c, d = cuts
+        return [by_lines(next(links), ref, slice(a, b), True), by_lines(next(links), ref, slice(b, c), False), by_planes(next(links), ref, slice(c, d))]
+
+    tok_plans, grad_plans = streams(x_all, (0, 16, 24, 32)), streams(g_all, (0, 8, 24, 32))
     loads[0].wait()
-    z_tok = along_z(links[0], x_all)
+    advance(tok_plans)
     loads[1].wait()
-    z_dout = along_z(links[1], g_all)
+    advance(grad_plans)
     for ld in loads[2:5]:
         ld.wait()
     row[...] = choice_row(tok[...], ids[...], wg[...])
     place = pltpu.make_async_copy(row, m_land.at[z, y, x, c], keep_sem.at[0])
     place.start()
     place.wait()
-    take_turns([gather(0, x_all, z_tok), gather(1, g_all, z_dout), gather_rows(links[2], m_land, (0, 1, 2, 3))])
+    row_plan = [gather_rows(next(links), m_land, range(4))]
+    for turn in FIRST:
+        advance({'t': tok_plans, 'g': grad_plans, 'm': row_plan}[turn])
+    take_turns(row_plan)
+    take_turns(tok_plans)
 
     def flatten(zz, carry):
         for k in range(ny * nx * nc):
@@ -263,8 +310,6 @@
     lax.fori_loop(0, nz, flatten, 0)
     for ld in loads[5:]:
         ld.wait()
-    save(2)
-    save(3)
 
     me = lax.axis_index('ep').astype(F32)
     code = m_all[...]
@@ -281,7 +326,9 @@
     n_pair = n_quad // 2
     n_slot = n_pair * 8 * CAP
 
-    def run_expert(i, carry):
+    places = [(cc, xx, yy, zz) for cc in range(nc) for xx in range(nx) for yy in range(ny) for zz in range(per)]
+
+    def select(i, ref, with_gate):
         c0, c1, g0, g1 = (pair_rows(token_lanes(m_all, k, pl.multiple_of(4 * n_quad * i, 4 * n_quad), n_quad)) for k in range(4))
         hit0, hit1 = plain_id(c0) == me, plain_id(c1) == me
         hit = (hit0 | hit1).astype(F32)
@@ -292,40 +339,41 @@
         src = (iota((n_pair, 256), 1) // 32).astype(F32)
         key = jnp.where(hit > 0.0, src * CAP + rank, -1.0)
         slot = iota((8 * CAP, 256), 0).astype(F32)
-        xs, dys = [], []
+        parts = []
         for p in range(n_pair):
             sel = (slot == key[p:p + 1]).astype(F32)
-            g = jnp.sum(sel * gate[p:p + 1], axis=1, keepdims=True)
-            sel = sel.astype(BF16)
-            xs.append(dot(sel, x_all[i * per + p // ny, p % ny].reshape(256, 256), 1, 0))
-            dys.append(g * dot(sel, g_all[i * per + p // ny, p % ny].reshape(256, 256), 1, 0))
-        places = [(cc, xx, yy, zz) for cc in range(nc) for xx in range(nx) for yy in range(ny) for zz in range(per)]
-
-        def by_place(parts):
-            return jnp.concatenate([parts[zz * ny + yy][8 * (xx * nc + cc):8 * (xx * nc + cc + 1)] for cc, xx, yy, zz in places], axis=0).astype(BF16)
-
-        xs, dys = by_place(xs), by_place(dys)
+            v = dot(sel.astype(BF16), ref[i * per + p // ny, p % ny].reshape(256, 256), 1, 0)
+            parts.append(v * jnp.sum(sel * gate[p:p + 1], axis=1, keepdims=True) if with_gate else v)
+        return jnp.concatenate([parts[zz * ny + yy][CAP * (xx * nc + cc):CAP * (xx * nc + cc + 1)] for cc, xx, yy, zz in places], axis=0).astype(BF16)
+
+    def put(i, v, to):
+        for k, (cc, xx, yy, zz) in enumerate(places):
+            for half in range(2):
+                to[half][cc, xx, yy, i * per + zz] = v[CAP * k:CAP * (k + 1), 128 * half:128 * (half + 1)].astype(BF16)
+
+    def forward(i):
+        here = pl.ds(i * n_slot, n_slot)
+        xs = select(i, x_all, False)
         h, slope = gelu_parts(dot(xs, w1[...], 1, 0))
         h = h.astype(BF16)
-        here = pl.ds(pl.multiple_of(i * n_slot, n_slot), n_slot)
-        xs_ref[here], dys_ref[here], h_ref[here] = xs, dys, h
-        yv = dot(h, w2[...], 1, 0)
-        da = (dot(dys, w2[...], 1, 1) * slope).astype(BF16)
-        da_ref[here] = da
-        dxv = dot(da, w1[...], 1, 1)
-        for k, (cc, xx, yy, zz) in enumerate(places):
-            for half in range(2):
-                lanes = slice(128 * half, 128 * (half + 1))
-                rows[half][cc, xx, yy, i * per + zz] = yv[8 * k:8 * (k + 1), lanes].astype(BF16)
-                rows[2 + half][cc, xx, yy, i * per + zz] = dxv[8 * k:8 * (k + 1), lanes].astype(BF16)
-        return carry
-
-    lax.fori_loop(0, steps, run_expert, 0)
+        xs_ref[here], h_ref[here], slope_ref[here] = xs, h, slope
+        put(i, dot(h, w2[...], 1, 0), rows[:2])
+
+    def backward(i):
+        here = pl.ds(i * n_slot, n_slot)
+        dys = select(i, g_all, True)
+        da = (dot(dys, w2[...], 1, 1) * slope_ref[here]).astype(BF16)
+        dys_ref[here], da_ref[here] = dys, da
+        put(i, dot(da, w1[...], 1, 1), rows[2:])
+
+    for i in range(steps):
+        forward(i)
+        advance(grad_plans)
 
     def back(i):
         h = rows[i]
         other, near, via, out2, via2, in2, out3, hot_land, cold_land = works[9 * i:9 * i + 9]
-        go = links[3 + i].go
+        go = next(links).go
         x_first = i % 2 == 0
         a, b = (x, y) if x_first else (y, x)
 
@@ -335,12 +383,9 @@
         def index(lead, a, bs):
             return lead + ((a, bs) if x_first else (bs, a))
 
-        def step(v, d):
-            return lax.rem(v + d, 4)
-
         up, dn, far = step(a, 1), step(a, 3), step(a, 2)
         lo, hi = pl.ds(0, 2), pl.ds(2, 2)
-        cross = go(h.at[1 - c], other, dev(z, y, x, 1 - c))
+        cross = go(h.at[1 - c], other, mate)
 
         def spread(ref, lead, e):
             return [go(ref.at[index(lead, far, lo)], via.at[0, e], to(up, b)), go(ref.at[index(lead, far, hi)], via.at[1, e], to(dn, b)),
@@ -425,18 +470,27 @@
             save(5, (full, part))
 
     ys, dxs = [back(0), back(1)], [back(2), back(3)]
-
-    def advance(plans):
-        for g in plans:
-            next(g, None)
-
-    todo = list(range(8))
-
-    for turn in 'y x w y x ww yy w xx y w x y w y w xx w y'.replace(' ', ''):
-        if turn == 'w':
-            weight_grad(todo.pop(0))
-        else:
-            advance(ys if turn == 'y' else dxs)
+    todo = [functools.partial(weight_grad, k) for k in range(8)]
+    undone = [functools.partial(backward, i) for i in range(steps)]
+
+    def turns(text):
+        for turn in text:
+            if turn == 'y':
+                advance(ys)
+            elif turn == 'x':
+                advance(dxs)
+            elif turn == 'd':
+                advance(d_plans)
+            elif turn == 'g':
+                take_turns(grad_plans)
+            elif turn == 'b' and undone:
+                undone.pop(0)()
+            elif turn == 'w':
+                todo.pop(0)()
+
+    turns(SECOND)
+    save(2)
+    save(3)
 
     r0, r1 = ids[0:1].astype(F32), ids[1:2].astype(F32)
     i0, i1 = as_col(r0), as_col(r1)
@@ -480,19 +534,15 @@
     place = pltpu.make_async_copy(d_row, d_land.at[z, y, x, c], keep_sem.at[1])
     place.start()
     place.wait()
-    d_plan = gather_rows(links[7], d_land, (1, 2, 0, 3))
-    next(d_plan)
-    advance(dxs)
+    d_plans = [gather_rows(next(links), d_land, (1, 2, 0, 3))]
     expert = iota((n_tok, n_exp), 1).astype(F32)
     spread = jnp.where(expert == i0, d0, jnp.where(expert == i1, d1, 0.0)).astype(BF16)
     through_gate = dot(spread, wg[...], 1, 1)
-    for _ in range(6):
-        next(d_plan)
-    advance(dxs)
+    turns(THIRD)
     dx0, dx1 = rows_of(2)
     gx_ref[...] = (dx0 + dx1 + through_gate).astype(BF16)
     save(1)
-    take_turns([d_plan])
+    take_turns(d_plans)
     save(4)
     for cp in sent:
         cp.wait_send()
@@ -510,7 +560,8 @@
     hbm = pl.BlockSpec(memory_space=pltpu.HBM)
     out = jax.ShapeDtypeStruct
     work = [(4, 4, nz), (4, 2, 4, nz), (2, 2, 2, nz), (4, 4, nz), (2, 4, nz // 2), (4, 4, nz), (nz, 3), (nz, 3), (nz, 4)]
-    counts = [nz - 1 + 4 + 16 + 16] * 2 + [nz - 1 + 3 + 3 + 1] + [1 + 12 + 6 + 2 * (nz - 1)] * 4 + [nz - 1 + 3 + 3 + 1]
+    lines, planes = nz - 1 + 4 + 16 + 4, 3 + 3 + nz + nz
+    counts = [lines, lines, planes] * 2 + [nz - 1 + 3 + 3 + 1] + [1 + 12 + 6 + 2 * (nz - 1)] * 4 + [nz - 1 + 3 + 3 + 1]
     sems = []
     for k in counts:
         sems += [pltpu.SemaphoreType.DMA((k,))] * 2
@@ -518,7 +569,7 @@
                ((d_model, d_hidden), F32), ((d_hidden, d_model), F32)]
     row, n_dma = (1, 128), 16
     kept = [(tokens.shape, BF16), (tokens.shape, BF16), (ids.shape, jnp.int32), (w_gate.shape, BF16), (w1.shape, BF16), (w2.shape, BF16), (row, F32), (dims + row, F32),
-            (dims + tokens.shape, BF16), ((n_row, d_model), BF16), ((n_row, d_model), BF16), ((n_row, d_hidden), BF16), ((n_row, d_hidden), BF16), (tile, F32), (row, F32)]
+            (dims + tokens.shape, BF16), ((n_row, d_model), BF16), ((n_row, d_model), BF16), ((n_row, d_hidden), BF16), ((n_row, d_hidden), BF16), ((n_row, d_hidden), F32), (tile, F32), (row, F32)]
     return pl.pallas_call(
         functools.partial(block_kernel, dims, (6, len(results), len(results), len(kept), 4, 4 * len(work), 3, len(sems))),
         out_shape=[out(*r) for r in results],
@@ -532,50 +583,56 @@
 
 
 VMEM_LIMIT = 67043328
-
-
-def gate_kernel(x_ref, m_ref, d_ref, g1_ref, g2_ref, out_ref, gx_ref, o_ref, o1_ref, o2_ref, o3_ref, o4_ref, acc):
-    o1_ref[...] = g1_ref[...]
-    o2_ref[...] = g2_ref[...]
-    o3_ref[...] = out_ref[...]
-    o4_ref[...] = gx_ref[...]
-    n_quad = m_ref.shape[0] // 4
-    i0, i1 = (plain_id(pair_rows(token_lanes(m_ref, k, 0, n_quad))) for k in range(2))
-    d0, d1 = (pair_rows(token_lanes(d_ref, k, 0, n_quad)) for k in range(2))
-    expert = iota((acc.shape[0], 256), 0).astype(F32)
-
-    @pl.when(pl.program_id(0) == 0)
-    def _():
-        acc[...] = jnp.zeros_like(acc)
-
-    total = acc[...]
-    for p in range(n_quad // 2):
-        q = slice(p, p + 1)
-        spread = jnp.where(expert == i0[q], d0[q], jnp.where(expert == i1[q], d1[q], 0.0))
-        total += dot(spread.astype(BF16), x_ref[256 * p:256 * (p + 1)], 1, 0)
-    acc[...] = total
-
-    @pl.when(pl.program_id(0) == pl.num_programs(0) - 1)
-    def _():
-        o_ref[...] = total.T
+FIRST = 'tmtgmtmtgmtmtgmtmtg'
+SECOND = 'gybbyybybxyxxwyxwyxwy'
+THIRD = 'dxwdxwdwwdwx'
+
+
+def gate_kernel(n, x_hbm, m_hbm, d_hbm, *refs):
+    refs = iter(refs)
+    through, (o_ref,), passed, (x, m, d), held, (load_sem, save_sem) = [tuple(itertools.islice(refs, k)) for k in (n, 1, n, 3, n, 2)]
+    n_part = x.shape[0]
+    loads = [pltpu.make_async_copy(s, t, load_sem.at[k]) for k, (s, t) in enumerate(zip((m_hbm, d_hbm) + through, (m, d) + held))]
+    chunks = [pltpu.make_async_copy(x_hbm.at[k], x.at[k], load_sem.at[len(loads) + k]) for k in range(n_part)]
+    for cp in loads[:2] + chunks[:1] + loads[2:] + chunks[1:]:
+        cp.start()
+    for cp in loads[:2]:
+        cp.wait()
+    n_quad = m.shape[0] // 4
+    i0, i1 = (plain_id(pair_rows(token_lanes(m, k, 0, n_quad))) for k in range(2))
+    d0, d1 = (pair_rows(token_lanes(d, k, 0, n_quad)) for k in range(2))
+    expert = iota((m.shape[0], 256), 0).astype(F32)
+    total = jnp.zeros(o_ref.shape[::-1], F32)
+    per = n_quad // 2 // n_part
+    saves = []
+    for k in range(n_part):
+        chunks[k].wait()
+        for p in range(per * k, per * (k + 1)):
+            q = slice(p, p + 1)
+            spread = jnp.where(expert == i0[q], d0[q], jnp.where(expert == i1[q], d1[q], 0.0))
+            at = 256 * (p - per * k)
+            total += dot(spread.astype(BF16), x[k, at:at + 256], 1, 0)
+        if k < n:
+            loads[2 + k].wait()
+            saves.append(pltpu.make_async_copy(held[k], passed[k], save_sem.at[k]))
+            saves[k].start()
+    o_ref[...] = total.T
+    for cp in saves:
+        cp.wait()
 
 
 def gate_grad(x_all, m_all, d_all, *through):
-    n_src = m_all.shape[0]
-    steps = 4 if n_src == 256 else 2
-    d_model = x_all.shape[1]
-    part = lambda shape: pl.BlockSpec((shape[0] // steps,) + shape[1:], lambda i: (i, 0))
-    whole = lambda shape: pl.BlockSpec(shape, lambda i: (0, 0))
-    specs = [part(v.shape) if v.shape[0] >= 64 else whole(v.shape) for v in through]
+    n_src, d_model, parts = m_all.shape[0], x_all.shape[1], 4
+    x_all = x_all.reshape(parts, -1, d_model)
+    hbm, vmem = pl.BlockSpec(memory_space=pltpu.HBM), pl.BlockSpec(memory_space=pltpu.VMEM)
     out = jax.ShapeDtypeStruct
     return pl.pallas_call(
-        gate_kernel,
-        grid=(steps,),
+        functools.partial(gate_kernel, len(through)),
         out_shape=[out((d_model, n_src), F32)] + [out(v.shape, v.dtype) for v in through],
-        in_specs=[part(x_all.shape), part(m_all.shape), part(d_all.shape)] + specs,
-        out_specs=[whole((d_model, n_src))] + specs,
-        scratch_shapes=[pltpu.VMEM((n_src, d_model), F32)],
-        compiler_params=pltpu.CompilerParams(dimension_semantics=('arbitrary',), vmem_limit_bytes=VMEM_LIMIT),
+        in_specs=[hbm] * (len(through) + 3),
+        out_specs=[vmem] + [hbm] * len(through),
+        scratch_shapes=[pltpu.VMEM(v.shape, v.dtype) for v in (x_all, m_all, d_all) + through] + [pltpu.SemaphoreType.DMA((16,))] * 2,
+        compiler_params=pltpu.CompilerParams(vmem_limit_bytes=VMEM_LIMIT),
         name='gate_grad',
     )(x_all, m_all, d_all, *through)
 

time: 113 us -> 110 us (0.973)
  Pallas kernels: 112 us -> 109 us
    pallas_call x1, Pallas kernels: 106 us -> 103 us  [block_call(): pl.pallas_call(functools.partial(block_kernel, dims, (6, len(results), le...]
where the time goes in v5:
time: 110 us
  Pallas kernels  109 us (99%)
    pallas_call x1, Pallas kernels, block_call(): pl.pallas_call(functools.partial(block_kernel, dims, (6, len(results), le...  103 us
    pallas_call x1, Pallas kernels, gate_grad(): pl.pallas_call(functools.partial(gate_kernel, len(through)), out_shape=[o...  5.9 us

profile of v5, /device:TPU:1, one launch (start us, length us, event | category | flops | bytes accessed | tf_op | source)
XLA Modules:
  0.0 110.0 jit_solution(1317116632060456909)
XLA Ops:
  0.6 103.3 %block.1 = (bf16[32,256]{1,0:T(8,128)(2,1)}, bf16[32,256]{1,0:T(8,128)(2,1)}, bf16[8,4,4,2,32,256]{5,4,3,2,1,0:T(8,128)(2,1)}, f32[256,128]{1,0:T(8,128)}, f32[8...) custom-call(bf16[32,256]{1,0:T(8,128)(2,1)} %refs_0_.1, bf16[32,256]{1,0:T(8,128)(2,1)} %refs_1_.1, ...), custom_call_target="tpu_custom_call" | custom-call | tf_op jit(solution)/shard_map/block/pallas_call | solution.py:573
  103.9 5.9 %gate_grad.1 = (f32[256,256]{1,0:T(8,128)}, f32[256,1024]{1,0:T(8,128)}, f32[1024,256]{1,0:T(8,128)}, bf16[32,256]{1,0:T(8,128)(2,1)}, bf16[32,256]{1,0:T(8,128)(2,1)}) custom-call(bf16[4,2048,256]{2,1,0:T(8,128)(2,1)} %bitcast.7, f32[256,128]{1,0:T(8,128)} %get-tuple-element.18.m_hbm, f32[256,128]{1,0:T(8,128)} %bitcast.10, ...), custom_call_target="tpu_custom_call" | custom-call | tf_op jit(solution)/shard_map/gate_grad/pallas_call | solution.py:629

commit v6 on v5

--- a/solution.py
+++ b/solution.py
@@ -75,13 +75,21 @@
     return jnp.concatenate([code(i0), code(i1), as_row(g0), as_row(g1)], axis=1)
 
 
-def gelu_parts(a):
+def gelu_tanh(a):
     k = 0.7978845608028654
     sq = a * a
-    t = jnp.tanh(a * (k + (k * 0.044715) * sq))
-    half = 0.5 + 0.5 * t
-    slope = half + (0.5 * a) * (1.0 - t * t) * (k + (3 * k * 0.044715) * sq)
-    return a * half, slope
+    return jnp.tanh(a * (k + (k * 0.044715) * sq)), sq
+
+
+def gelu(a):
+    half = 0.5 * a
+    return half + half * gelu_tanh(a)[0]
+
+
+def gelu_slope(a):
+    k = 0.7978845608028654
+    t, sq = gelu_tanh(a)
+    return (0.5 + 0.5 * t) + (0.5 * a) * (1.0 - t * t) * (k + (3 * k * 0.044715) * sq)
 
 
 def token_lanes(ref, k, start, n):
@@ -126,8 +134,8 @@
     refs = iter(refs)
     refs = [list(itertools.islice(refs, n)) for n in sizes]
     (tok_hbm, dout_hbm, ids_hbm, wg_hbm, w1_hbm, w2_hbm), outs, held, kept, rows, works, (load_sem, keep_sem, save_sem), sems = refs
-    out_ref, gx_ref, x_all, m_all, d_land, g1_ref, g2_ref = held
-    tok, dout, ids, wg, w1, w2, row, m_land, g_all, xs_ref, dys_ref, h_ref, da_ref, slope_ref, hot_ref, d_row = kept
+    out_ref, gx_ref, gate_ref, g1_ref, g2_ref = held
+    tok, dout, ids, wg, w1, w2, row, m_land, x_all, g_all, xs_ref, dys_ref, h_ref, da_ref, a_ref, m_all, hot_ref, d_row, d_land, d_all = kept
     z, y, x, c, dev = coords(dims)
     sent, saves = [], []
 
@@ -152,6 +160,7 @@
     meet(peers)
 
     full = slice(None)
+    by_distance = sorted(range(1, nz), key=lambda d: abs(d - nz // 2))
 
     def step(v, d, m=4):
         return lax.rem(v + d, m)
@@ -173,7 +182,7 @@
             cross.append(link.go(part, part, mate))
 
         own = at(z, p0, q0)
-        first = [link.go(own, own, dev(step(z, d, nz), y, x, c)) for d in range(1, nz)]
+        first = [link.go(own, own, dev(step(z, d, nz), y, x, c)) for d in by_distance]
         yield
         for cp in first:
             cp.wait_recv()
@@ -268,7 +277,7 @@
             size = (nz, ny, nx, nc)[axis]
             part = held.at[tuple(have)]
             copies = []
-            for d in range(1, size):
+            for d in sorted(range(1, size), key=lambda d: abs(d - size // 2)):
                 there = [z, y, x, c]
                 there[axis] = lax.rem(there[axis] + d, size)
                 copies.append(link.go(part, part, dev(*there)))
@@ -281,14 +290,13 @@
         for g in plans:
             next(g, None)
 
-    def streams(ref, cuts):
-        a, b, c, d = cuts
-        return [by_lines(next(links), ref, slice(a, b), True), by_lines(next(links), ref, slice(b, c), False), by_planes(next(links), ref, slice(c, d))]
-
-    tok_plans, grad_plans = streams(x_all, (0, 16, 24, 32)), streams(g_all, (0, 8, 24, 32))
+    tok_plans = [by_lines(next(links), x_all, slice(0, 16), True), by_lines(next(links), x_all, slice(16, 32), False)]
+    grad_plans = [by_lines(next(links), g_all, slice(0, 8), True), by_lines(next(links), g_all, slice(8, 16), False)]
+    plane_plan = [by_planes(next(links), g_all, slice(16, 32))]
     loads[0].wait()
     advance(tok_plans)
     loads[1].wait()
+    advance(plane_plan)
     advance(grad_plans)
     for ld in loads[2:5]:
         ld.wait()
@@ -298,16 +306,19 @@
     place.wait()
     row_plan = [gather_rows(next(links), m_land, range(4))]
     for turn in FIRST:
-        advance({'t': tok_plans, 'g': grad_plans, 'm': row_plan}[turn])
+        advance({'t': tok_plans, 'g': grad_plans, 'c': plane_plan, 'm': row_plan}[turn])
     take_turns(row_plan)
     take_turns(tok_plans)
 
-    def flatten(zz, carry):
-        for k in range(ny * nx * nc):
-            m_all[pl.ds(zz * (ny * nx * nc) + k, 1), :] = m_land[zz, k // (nx * nc), k // nc % nx, k % nc]
-        return carry
-
-    lax.fori_loop(0, nz, flatten, 0)
+    def flatten(land, flat):
+        def lines(zz, carry):
+            for k in range(ny * nx * nc):
+                flat[pl.ds(zz * (ny * nx * nc) + k, 1), :] = land[zz, k // (nx * nc), k // nc % nx, k % nc]
+            return carry
+
+        lax.fori_loop(0, nz, lines, 0)
+
+    flatten(m_land, m_all)
     for ld in loads[5:]:
         ld.wait()
 
@@ -354,21 +365,21 @@
     def forward(i):
         here = pl.ds(i * n_slot, n_slot)
         xs = select(i, x_all, False)
-        h, slope = gelu_parts(dot(xs, w1[...], 1, 0))
-        h = h.astype(BF16)
-        xs_ref[here], h_ref[here], slope_ref[here] = xs, h, slope
+        a = dot(xs, w1[...], 1, 0)
+        h = gelu(a).astype(BF16)
+        xs_ref[here], h_ref[here], a_ref[here] = xs, h, a
         put(i, dot(h, w2[...], 1, 0), rows[:2])
 
     def backward(i):
         here = pl.ds(i * n_slot, n_slot)
         dys = select(i, g_all, True)
-        da = (dot(dys, w2[...], 1, 1) * slope_ref[here]).astype(BF16)
+        da = (dot(dys, w2[...], 1, 1) * gelu_slope(a_ref[here])).astype(BF16)
         dys_ref[here], da_ref[here] = dys, da
         put(i, dot(da, w1[...], 1, 1), rows[2:])
 
     for i in range(steps):
         forward(i)
-        advance(grad_plans)
+        advance(grad_plans + plane_plan)
 
     def back(i):
         h = rows[i]
@@ -447,10 +458,10 @@
         for j in range(3):
             out3[:, j] = (in2[0, j] + in2[1, j]) + (in2[2, j] + in2[3, j])
         last = []
-        for d in range(1, nz):
+        for d in by_distance:
             zz = lax.rem(z + d, nz)
             last.append(go(in2.at[:, 3, zz], cold_land.at[z], dev(zz, y, x, c)))
-        for d in range(1, nz):
+        for d in by_distance:
             zz = lax.rem(z + d, nz)
             last.append(go(out3.at[zz], hot_land.at[z], dev(zz, y, x, c)))
         cold_land[z] = in2[:, 3, z]
@@ -463,11 +474,11 @@
         if k % 2 == 0:
             part = slice(w2.shape[0] // 4 * (k // 2), w2.shape[0] // 4 * (k // 2 + 1))
             g2_ref[part, :] = dot(h_ref[:, part], dys_ref[...], 0, 0)
-            save(6, (part, full))
+            save(4, (part, full))
         else:
             part = slice(w1.shape[1] // 4 * (k // 2), w1.shape[1] // 4 * (k // 2 + 1))
             g1_ref[:, part] = dot(xs_ref[...], da_ref[:, part], 0, 0)
-            save(5, (full, part))
+            save(3, (full, part))
 
     ys, dxs = [back(0), back(1)], [back(2), back(3)]
     todo = [functools.partial(weight_grad, k) for k in range(8)]
@@ -482,15 +493,13 @@
             elif turn == 'd':
                 advance(d_plans)
             elif turn == 'g':
-                take_turns(grad_plans)
+                take_turns(grad_plans + plane_plan)
             elif turn == 'b' and undone:
                 undone.pop(0)()
             elif turn == 'w':
                 todo.pop(0)()
 
     turns(SECOND)
-    save(2)
-    save(3)
 
     r0, r1 = ids[0:1].astype(F32), ids[1:2].astype(F32)
     i0, i1 = as_col(r0), as_col(r1)
@@ -534,7 +543,7 @@
     place = pltpu.make_async_copy(d_row, d_land.at[z, y, x, c], keep_sem.at[1])
     place.start()
     place.wait()
-    d_plans = [gather_rows(next(links), d_land, (1, 2, 0, 3))]
+    d_plans = [gather_rows(next(links), d_land, range(4))]
     expert = iota((n_tok, n_exp), 1).astype(F32)
     spread = jnp.where(expert == i0, d0, jnp.where(expert == i1, d1, 0.0)).astype(BF16)
     through_gate = dot(spread, wg[...], 1, 1)
@@ -543,7 +552,18 @@
     gx_ref[...] = (dx0 + dx1 + through_gate).astype(BF16)
     save(1)
     take_turns(d_plans)
-    save(4)
+    flatten(d_land, d_all)
+    expert = iota((n_exp, 256), 0).astype(F32)
+    n_tok_z = ny * nx * nc * n_tok
+    def gate_part(zz, carry):
+        start = pl.multiple_of(zz * (ny * nx * nc), ny * nx * nc)
+        c0, c1 = (plain_id(pair_rows(token_lanes(m_all, k, start, n_tok_z // 128))) for k in range(2))
+        e0, e1 = (pair_rows(token_lanes(d_all, k, start, n_tok_z // 128)) for k in range(2))
+        spread = [jnp.where(expert == c0[p:p + 1], e0[p:p + 1], jnp.where(expert == c1[p:p + 1], e1[p:p + 1], 0.0)).astype(BF16) for p in range(n_tok_z // 256)]
+        return carry + dot(jnp.concatenate(spread, axis=1), x_all[zz].reshape(n_tok_z, x_all.shape[-1]), 1, 0)
+
+    gate_ref[...] = lax.fori_loop(0, nz, gate_part, jnp.zeros((n_exp, x_all.shape[-1]), F32)).T
+    save(2)
     for cp in sent:
         cp.wait_send()
     for cp in saves:
@@ -561,20 +581,20 @@
     out = jax.ShapeDtypeStruct
     work = [(4, 4, nz), (4, 2, 4, nz), (2, 2, 2, nz), (4, 4, nz), (2, 4, nz // 2), (4, 4, nz), (nz, 3), (nz, 3), (nz, 4)]
     lines, planes = nz - 1 + 4 + 16 + 4, 3 + 3 + nz + nz
-    counts = [lines, lines, planes] * 2 + [nz - 1 + 3 + 3 + 1] + [1 + 12 + 6 + 2 * (nz - 1)] * 4 + [nz - 1 + 3 + 3 + 1]
+    counts = [lines] * 4 + [planes] + [nz - 1 + 3 + 3 + 1] + [1 + 12 + 6 + 2 * (nz - 1)] * 4 + [nz - 1 + 3 + 3 + 1]
     sems = []
     for k in counts:
         sems += [pltpu.SemaphoreType.DMA((k,))] * 2
-    results = [(tokens.shape, BF16), (tokens.shape, BF16), (dims + tokens.shape, BF16), ((n_dev, 128), F32), (dims + (1, 128), F32),
-               ((d_model, d_hidden), F32), ((d_hidden, d_model), F32)]
+    results = [(tokens.shape, BF16), (tokens.shape, BF16), ((d_model, n_dev), F32), ((d_model, d_hidden), F32), ((d_hidden, d_model), F32)]
     row, n_dma = (1, 128), 16
     kept = [(tokens.shape, BF16), (tokens.shape, BF16), (ids.shape, jnp.int32), (w_gate.shape, BF16), (w1.shape, BF16), (w2.shape, BF16), (row, F32), (dims + row, F32),
-            (dims + tokens.shape, BF16), ((n_row, d_model), BF16), ((n_row, d_model), BF16), ((n_row, d_hidden), BF16), ((n_row, d_hidden), BF16), ((n_row, d_hidden), F32), (tile, F32), (row, F32)]
+            (dims + tokens.shape, BF16), (dims + tokens.shape, BF16), ((n_row, d_model), BF16), ((n_row, d_model), BF16), ((n_row, d_hidden), BF16), ((n_row, d_hidden), BF16), ((n_row, d_hidden), F32), ((n_dev, 128), F32), (tile, F32), (row, F32),
+            (dims + row, F32), ((n_dev, 128), F32)]
     return pl.pallas_call(
         functools.partial(block_kernel, dims, (6, len(results), len(results), len(kept), 4, 4 * len(work), 3, len(sems))),
         out_shape=[out(*r) for r in results],
         in_specs=[hbm] * 6,
-        out_specs=[hbm] * 7,
+        out_specs=[hbm] * len(results),
         scratch_shapes=[pltpu.VMEM(*r) for r in results + kept] + [pltpu.VMEM((nc, nx, ny, nz) + tile, BF16)] * 4 + [pltpu.VMEM(w + tile, BF16) for w in work] * 4
         + [pltpu.SemaphoreType.DMA((n_dma,))] * 3 + sems,
         compiler_params=pltpu.CompilerParams(collective_id=0, has_side_effects=True, vmem_limit_bytes=VMEM_LIMIT),
@@ -583,64 +603,40 @@
 
 
 VMEM_LIMIT = 67043328
-FIRST = 'tmtgmtmtgmtmtgmtmtg'
-SECOND = 'gybbyybybxyxxwyxwyxwy'
-THIRD = 'dxwdxwdwwdwx'
-
-
-def gate_kernel(n, x_hbm, m_hbm, d_hbm, *refs):
+FIRST = 'ctcgmttcgtmtcgtgmtcgt'
+SECOND = 'gybybyybybyxwwyxxwxwy'
+THIRD = 'dxwdxwdxwdwx'
+
+
+def pass_kernel(n, *refs):
     refs = iter(refs)
-    through, (o_ref,), passed, (x, m, d), held, (load_sem, save_sem) = [tuple(itertools.islice(refs, k)) for k in (n, 1, n, 3, n, 2)]
-    n_part = x.shape[0]
-    loads = [pltpu.make_async_copy(s, t, load_sem.at[k]) for k, (s, t) in enumerate(zip((m_hbm, d_hbm) + through, (m, d) + held))]
-    chunks = [pltpu.make_async_copy(x_hbm.at[k], x.at[k], load_sem.at[len(loads) + k]) for k in range(n_part)]
-    for cp in loads[:2] + chunks[:1] + loads[2:] + chunks[1:]:
+    given, passed, held, (load_sem, save_sem) = [list(itertools.islice(refs, k)) for k in (n, n, n, 2)]
+    loads = [pltpu.make_async_copy(given[k], held[k], load_sem.at[k]) for k in range(n)]
+    saves = [pltpu.make_async_copy(held[k], passed[k], save_sem.at[k]) for k in range(n)]
+    for cp in loads:
         cp.start()
-    for cp in loads[:2]:
-        cp.wait()
-    n_quad = m.shape[0] // 4
-    i0, i1 = (plain_id(pair_rows(token_lanes(m, k, 0, n_quad))) for k in range(2))
-    d0, d1 = (pair_rows(token_lanes(d, k, 0, n_quad)) for k in range(2))
-    expert = iota((m.shape[0], 256), 0).astype(F32)
-    total = jnp.zeros(o_ref.shape[::-1], F32)
-    per = n_quad // 2 // n_part
-    saves = []
-    for k in range(n_part):
-        chunks[k].wait()
-        for p in range(per * k, per * (k + 1)):
-            q = slice(p, p + 1)
-            spread = jnp.where(expert == i0[q], d0[q], jnp.where(expert == i1[q], d1[q], 0.0))
-            at = 256 * (p - per * k)
-            total += dot(spread.astype(BF16), x[k, at:at + 256], 1, 0)
-        if k < n:
-            loads[2 + k].wait()
-            saves.append(pltpu.make_async_copy(held[k], passed[k], save_sem.at[k]))
-            saves[k].start()
-    o_ref[...] = total.T
+    for load, save in zip(loads, saves):
+        load.wait()
+        save.start()
     for cp in saves:
         cp.wait()
 
 
-def gate_grad(x_all, m_all, d_all, *through):
-    n_src, d_model, parts = m_all.shape[0], x_all.shape[1], 4
-    x_all = x_all.reshape(parts, -1, d_model)
-    hbm, vmem = pl.BlockSpec(memory_space=pltpu.HBM), pl.BlockSpec(memory_space=pltpu.VMEM)
-    out = jax.ShapeDtypeStruct
+def pass_on(*arrays):
+    n = len(arrays)
     return pl.pallas_call(
-        functools.partial(gate_kernel, len(through)),
-        out_shape=[out((d_model, n_src), F32)] + [out(v.shape, v.dtype) for v in through],
-        in_specs=[hbm] * (len(through) + 3),
-        out_specs=[vmem] + [hbm] * len(through),
-        scratch_shapes=[pltpu.VMEM(v.shape, v.dtype) for v in (x_all, m_all, d_all) + through] + [pltpu.SemaphoreType.DMA((16,))] * 2,
+        functools.partial(pass_kernel, n),
+        out_shape=[jax.ShapeDtypeStruct(v.shape, v.dtype) for v in arrays],
+        in_specs=[pl.BlockSpec(memory_space=pltpu.HBM)] * n,
+        out_specs=[pl.BlockSpec(memory_space=pltpu.HBM)] * n,
+        scratch_shapes=[pltpu.VMEM(v.shape, v.dtype) for v in arrays] + [pltpu.SemaphoreType.DMA((n,))] * 2,
         compiler_params=pltpu.CompilerParams(vmem_limit_bytes=VMEM_LIMIT),
-        name='gate_grad',
-    )(x_all, m_all, d_all, *through)
+        name='pass_on',
+    )(*arrays)
 
 
 def local_block(dims, tokens, grad_out, expert_ids, w_gate, w_in, w_out):
-    n_exp = w_gate.shape[1]
-    y_out, grad_x, x_all, m_all, d_all, g1, g2 = block_call(dims, tokens, grad_out, expert_ids.T, w_gate, w_in[0], w_out[0])
-    grad_w_gate, g1, g2, y_out, grad_x = gate_grad(x_all.reshape(-1, tokens.shape[1]), m_all, d_all.reshape(n_exp, 128), g1, g2, y_out, grad_x)
+    y_out, grad_x, grad_w_gate, g1, g2 = pass_on(*block_call(dims, tokens, grad_out, expert_ids.T, w_gate, w_in[0], w_out[0]))
     return y_out, grad_x, g1[None], g2[None], grad_w_gate
 
 

time: 110 us -> 96.1 us (0.87)
  Pallas kernels: 109 us -> 94.5 us
    pallas_call x1, Pallas kernels: 103 us -> 91.8 us  [block_call(): pl.pallas_call(functools.partial(block_kernel, dims, (6, len(results), le...]
    pallas_call x1, Pallas kernels: 5.9 us -> 2.74 us  [pass_on(): pl.pallas_call(functools.partial(pass_kernel, n), out_shape=[jax.ShapeDty...]
where the time goes in v6:
time: 96.1 us; the launch traced here: 95.3 us
  Pallas kernels  94.5 us (98%)
    pallas_call x1, Pallas kernels, block_call(): pl.pallas_call(functools.partial(block_kernel, dims, (6, len(results), le...  91.8 us
    pallas_call x1, Pallas kernels, pass_on(): pl.pallas_call(functools.partial(pass_kernel, n), out_shape=[jax.ShapeDty...  2.74 us

profile of v6, /device:TPU:1, one launch (start us, length us, event | category | flops | bytes accessed | tf_op | source)
XLA Modules:
  0.0 95.3 jit_solution(5163319420759667854)
XLA Ops:
  0.6 91.8 %block.1 = (bf16[32,256]{1,0:T(8,128)(2,1)}, bf16[32,256]{1,0:T(8,128)(2,1)}, f32[256,256]{1,0:T(8,128)}, f32[256,1024]{1,0:T(8,128)}, f32[1024,256]{1,0:T(8,128)}) custom-call(bf16[32,256]{1,0:T(8,128)(2,1)} %refs_0_.1, bf16[32,256]{1,0:T(8,128)(2,1)} %refs_1_.1, s32[2,32]{1,0:T(2,128)} %bitcast.7, bf16[256,256]{1,0:T(8,128)(2,1)} %refs_3_.1, ...), custom_call_target="tpu_custom_call" | custom-call | tf_op jit(solution)/shard_map/block/pallas_call | solution.py:593
  92.4 2.7 %pass_on.1 = (bf16[32,256]{1,0:T(8,128)(2,1)}, bf16[32,256]{1,0:T(8,128)(2,1)}, f32[256,256]{1,0:T(8,128)}, f32[256,1024]{1,0:T(8,128)}, f32[1024,256]{1,0:T(8,128)}) custom-call(bf16[32,256]{1,0:T(8,128)(2,1)} %get-tuple-element.15.refs_0_, bf16[32,256]{1,0:T(8,128)(2,1)} %get-tuple-element.16.refs_1_, f32[256,256]{1,0:T(8,128)} %get-tuple-element.17.refs_2_, ...), custom_call_target="tpu_custom_call" | custom-call | tf_op jit(solution)/shard_map/pass_on/pallas_call | solution.py:627

commit v7 on v6

--- a/solution.py
+++ b/solution.py
@@ -1,5 +1,6 @@
 import functools
 import itertools
+import math
 
 import jax
 import jax.numpy as jnp
@@ -110,15 +111,25 @@
 
 
 class Links:
-    def __init__(self, send, recv, sent):
-        self.send, self.recv, self.sent, self.k = send, recv, sent, 0
-
-    def go(self, src, dst, to):
-        cp = pltpu.make_async_remote_copy(src_ref=src, dst_ref=dst, send_sem=self.send.at[self.k], recv_sem=self.recv.at[self.k], device_id=to, device_id_type=MESH)
-        self.k += 1
-        cp.start()
-        self.sent.append(cp)
-        return cp
+    def __init__(self, send, recv, pool):
+        self.send, self.recv, self.pool, self.bytes = send, recv, pool, 0
+
+    def group(self):
+        return self.recv.at[next(self.pool)]
+
+    def go(self, src, dst, to, group):
+        pltpu.make_async_remote_copy(src_ref=src, dst_ref=dst, send_sem=self.send, recv_sem=group, device_id=to, device_id_type=MESH).start()
+        self.bytes += math.prod(src.shape) * jnp.dtype(src.dtype).itemsize
+
+    def wait(self, group, ref):
+        pltpu.make_async_copy(ref, ref, group).wait()
+
+    def finish(self, *pads):
+        for pad in pads:
+            unit = math.prod(pad.shape[1:]) * jnp.dtype(pad.dtype).itemsize
+            if self.bytes % unit == 0:
+                return self.wait(self.send, pad.at[pl.ds(0, self.bytes // unit)])
+        raise ValueError(self.bytes)
 
 
 def take_turns(plans):
@@ -135,9 +146,9 @@
     refs = [list(itertools.islice(refs, n)) for n in sizes]
     (tok_hbm, dout_hbm, ids_hbm, wg_hbm, w1_hbm, w2_hbm), outs, held, kept, rows, works, (load_sem, keep_sem, save_sem), sems = refs
     out_ref, gx_ref, gate_ref, g1_ref, g2_ref = held
-    tok, dout, ids, wg, w1, w2, row, m_land, x_all, g_all, xs_ref, dys_ref, h_ref, da_ref, a_ref, m_all, hot_ref, d_row, d_land, d_all = kept
+    tok, dout, ids, wg, w1, w2, row, m_land, x_all, g_all, xs_ref, dys_ref, h_ref, da_ref, a_ref, m_all, hot_ref, d_row, d_land, d_all, pad, pad_row = kept
     z, y, x, c, dev = coords(dims)
-    sent, saves = [], []
+    saves = []
 
     def save(k, part=None):
         src, dst = (held[k], outs[k]) if part is None else (held[k].at[part], outs[k].at[part])
@@ -145,7 +156,10 @@
         cp.start()
         saves.append(cp)
 
-    links = iter([Links(send, recv, sent) for send, recv in zip(sems[::2], sems[1::2])])
+    send_sem, recv_sem = sems
+    pool = itertools.count()
+    all_links = [Links(send_sem.at[k], recv_sem, pool) for k in range(send_sem.shape[0])]
+    links = iter(all_links)
 
     loads = [pltpu.make_async_copy(s, d, load_sem.at[k]) for k, (s, d) in enumerate(
         [(tok_hbm, x_all.at[z, y, x, c]), (dout_hbm, g_all.at[z, y, x, c]), (tok_hbm, tok), (ids_hbm, ids), (wg_hbm, wg), (dout_hbm, dout), (w1_hbm, w1), (w2_hbm, w2)])]
@@ -172,49 +186,52 @@
         def at(zs, p, q):
             return ref.at[(zs, p, q, c, rows) if x_last else (zs, q, p, c, rows)]
 
-        def go(part, p, q):
-            return link.go(part, part, dev(z, p, q, c) if x_last else dev(z, q, p, c))
-
-        cross = []
+        def go(part, p, q, group):
+            link.go(part, part, dev(z, p, q, c) if x_last else dev(z, q, p, c), group)
+
+        in_z, in_p, in_m, in_f, in_r, in_c = [link.group() for _ in range(6)]
+        line = at(full, p0, q0)
 
         def over(q):
             part = at(full, full, q)
-            cross.append(link.go(part, part, mate))
+            link.go(part, part, mate, in_c)
 
         own = at(z, p0, q0)
-        first = [link.go(own, own, dev(step(z, d, nz), y, x, c)) for d in by_distance]
-        yield
-        for cp in first:
-            cp.wait_recv()
+        for d in by_distance:
+            link.go(own, own, dev(step(z, d, nz), y, x, c), in_z)
+        yield
+        link.wait(in_z, at(pl.ds(0, nz - 1), p0, q0))
         pm, pp, po = step(p0, 3), step(p0, 1), step(p0, 2)
         qm, qp, qo = step(q0, 3), step(q0, 1), step(q0, 2)
-        qs, relays = [], []
+        qs = []
 
         def spread(p):
             part = at(full, p, q0)
-            qs.append((p, go(part, p0, qp), go(part, p0, qm)))
+            qs.append((p, link.group(), link.group()))
+            go(part, p0, qp, qs[-1][1])
+            go(part, p0, qm, qs[-1][2])
 
         def relay(i):
             p, up, dn = qs[i]
-            up.wait_recv()
-            relays.append(go(at(low, p, qm), p0, qp))
-            dn.wait_recv()
-            relays.append(go(at(high, p, qp), p0, qm))
-
-        p_up, p_dn = go(at(full, p0, q0), pp, q0), go(at(full, p0, q0), pm, q0)
+            link.wait(up, line)
+            go(at(low, p, qm), p0, qp, in_r)
+            link.wait(dn, line)
+            go(at(high, p, qp), p0, qm, in_r)
+
+        go(line, pp, q0, in_p)
+        go(line, pm, q0, in_m)
         spread(p0)
         yield
-        p_up.wait_recv()
-        f_up = go(at(low, pm, q0), pp, q0)
-        p_dn.wait_recv()
-        f_dn = go(at(high, pp, q0), pm, q0)
+        link.wait(in_p, line)
+        go(at(low, pm, q0), pp, q0, in_f)
+        link.wait(in_m, line)
+        go(at(high, pp, q0), pm, q0, in_f)
         spread(pm)
         spread(pp)
         yield
         relay(0)
         yield
-        f_up.wait_recv()
-        f_dn.wait_recv()
+        link.wait(in_f, line)
         spread(po)
         over(q0)
         for i in range(1, 4):
@@ -223,68 +240,67 @@
         over(qm)
         over(qp)
         yield
-        for cp in relays:
-            cp.wait_recv()
+        link.wait(in_r, at(full, full, q0))
         over(qo)
         yield
-        for cp in cross:
-            cp.wait_recv()
+        link.wait(in_c, ref.at[full, full, full, c, rows])
 
     def by_planes(link, ref, rows):
-        go = lambda part, *to: link.go(part, part, dev(*to))
+        go = lambda part, group, *to: link.go(part, part, dev(*to), group)
         at = lambda zz, ys=full: ref.at[zz, ys, full, c, rows]
+        in_x, in_y, in_c = [link.group() for _ in range(3)]
         own = ref.at[z, y, x, c, rows]
-        xs = [go(own, z, y, step(x, d), c) for d in range(1, nx)]
-        yield
-        for cp in xs:
-            cp.wait_recv()
+        for d in range(1, nx):
+            go(own, in_x, z, y, step(x, d), c)
+        yield
+        link.wait(in_x, ref.at[z, y, pl.ds(0, nx - 1), c, rows])
         line = ref.at[z, y, full, c, rows]
-        ys = [go(line, z, step(y, d), x, c) for d in range(1, ny)]
-        yield
-        for cp in ys:
-            cp.wait_recv()
-        cross = []
+        for d in range(1, ny):
+            go(line, in_y, z, step(y, d), x, c)
+        yield
+        link.wait(in_y, ref.at[z, pl.ds(0, ny - 1), full, c, rows])
 
         def over(*planes):
             for zz in planes:
-                cross.append(link.go(at(zz), at(zz), mate))
+                link.go(at(zz), at(zz), mate, in_c)
 
         half = nz // 2
         lower, upper = pl.ds(0, ny // 2), pl.ds(ny // 2, ny // 2)
 
         def pair(d):
             a, b = (full, full) if d + 1 < half else (lower, upper)
-            return go(at(step(z, nz - d, nz), a), step(z, 1, nz), y, x, c), go(at(step(z, d, nz), b), step(z, nz - 1, nz), y, x, c)
-
-        up, dn = pair(0)
+            group = link.group()
+            go(at(step(z, nz - d, nz), a), group, step(z, 1, nz), y, x, c)
+            go(at(step(z, d, nz), b), group, step(z, nz - 1, nz), y, x, c)
+            return group
+
+        group = pair(0)
         over(z)
         for d in range(1, half + 1):
             yield
-            up.wait_recv()
-            dn.wait_recv()
+            link.wait(group, at(pl.ds(0, 2) if d < half else z))
             if d < half:
-                up, dn = pair(d)
+                group = pair(d)
                 over(step(z, d, nz), step(z, nz - d, nz))
             else:
                 over(step(z, d, nz))
         yield
-        for cp in cross:
-            cp.wait_recv()
+        link.wait(in_c, ref.at[full, full, full, c, rows])
 
     def gather_rows(link, held, order):
         have = [z, y, x, c]
         for axis in order:
             size = (nz, ny, nx, nc)[axis]
             part = held.at[tuple(have)]
-            copies = []
+            group = link.group()
             for d in sorted(range(1, size), key=lambda d: abs(d - size // 2)):
                 there = [z, y, x, c]
                 there[axis] = lax.rem(there[axis] + d, size)
-                copies.append(link.go(part, part, dev(*there)))
+                link.go(part, part, dev(*there), group)
+            have[axis] = pl.ds(0, size - 1)
+            yield
+            link.wait(group, held.at[tuple(have)])
             have[axis] = full
-            yield
-            for cp in copies:
-                cp.wait_recv()
 
     def advance(plans):
         for g in plans:
@@ -295,9 +311,6 @@
     plane_plan = [by_planes(next(links), g_all, slice(16, 32))]
     loads[0].wait()
     advance(tok_plans)
-    loads[1].wait()
-    advance(plane_plan)
-    advance(grad_plans)
     for ld in loads[2:5]:
         ld.wait()
     row[...] = choice_row(tok[...], ids[...], wg[...])
@@ -305,6 +318,8 @@
     place.start()
     place.wait()
     row_plan = [gather_rows(next(links), m_land, range(4))]
+    loads[1].wait()
+    advance(row_plan + plane_plan + grad_plans)
     for turn in FIRST:
         advance({'t': tok_plans, 'g': grad_plans, 'c': plane_plan, 'm': row_plan}[turn])
     take_turns(row_plan)
@@ -373,18 +388,22 @@
     def backward(i):
         here = pl.ds(i * n_slot, n_slot)
         dys = select(i, g_all, True)
-        da = (dot(dys, w2[...], 1, 1) * gelu_slope(a_ref[here])).astype(BF16)
-        dys_ref[here], da_ref[here] = dys, da
-        put(i, dot(da, w1[...], 1, 1), rows[2:])
+        dys_ref[here] = dys
+        da_ref[here] = (dot(dys, w2[...], 1, 1) * gelu_slope(a_ref[here])).astype(BF16)
+
+    def backward_rows(i):
+        put(i, dot(da_ref[pl.ds(i * n_slot, n_slot)], w1[...], 1, 1), rows[2:])
 
     for i in range(steps):
         forward(i)
-        advance(grad_plans + plane_plan)
+        advance(grad_plans + plane_plan if i else grad_plans)
 
     def back(i):
         h = rows[i]
         other, near, via, out2, via2, in2, out3, hot_land, cold_land = works[9 * i:9 * i + 9]
-        go = next(links).go
+        link = next(links)
+        go = link.go
+        in_c, in_e, in_h, in_n, in_v, in_2, in_l, in_s = [link.group() for _ in range(8)]
         x_first = i % 2 == 0
         a, b = (x, y) if x_first else (y, x)
 
@@ -396,30 +415,29 @@
 
         up, dn, far = step(a, 1), step(a, 3), step(a, 2)
         lo, hi = pl.ds(0, 2), pl.ds(2, 2)
-        cross = go(h.at[1 - c], other, mate)
-
-        def spread(ref, lead, e):
-            return [go(ref.at[index(lead, far, lo)], via.at[0, e], to(up, b)), go(ref.at[index(lead, far, hi)], via.at[1, e], to(dn, b)),
-                    go(ref.at[index(lead, up, full)], near.at[a, e], to(up, b)), go(ref.at[index(lead, dn, full)], near.at[a, e], to(dn, b))]
-
-        def relay(cps, e):
-            cps[0].wait_recv()
-            r_up = go(via.at[0, e], near.at[dn, e, lo], to(up, b))
-            cps[1].wait_recv()
-            r_dn = go(via.at[1, e], near.at[up, e, hi], to(dn, b))
-            return [cps[2], cps[3], r_up, r_dn]
-
-        own = spread(h, (c,), c)
-        yield
-        cross.wait_recv()
-        his = spread(other, (), 1 - c)
-        yield
-        waits = relay(own, c)
-        yield
-        waits += relay(his, 1 - c)
-        yield
-        for cp in waits:
-            cp.wait_recv()
+        go(h.at[1 - c], other, mate, in_c)
+
+        def spread(ref, lead, e, group):
+            go(ref.at[index(lead, far, lo)], via.at[0, e], to(up, b), group)
+            go(ref.at[index(lead, far, hi)], via.at[1, e], to(dn, b), group)
+            go(ref.at[index(lead, up, full)], near.at[a, e], to(up, b), in_n)
+            go(ref.at[index(lead, dn, full)], near.at[a, e], to(dn, b), in_n)
+
+        def relay(e, group):
+            link.wait(group, via.at[:, e])
+            go(via.at[0, e], near.at[dn, e, lo], to(up, b), in_n)
+            go(via.at[1, e], near.at[up, e, hi], to(dn, b), in_n)
+
+        spread(h, (c,), c, in_e)
+        yield
+        link.wait(in_c, other)
+        spread(other, (), 1 - c, in_h)
+        yield
+        relay(c, in_e)
+        yield
+        relay(1 - c, in_h)
+        yield
+        link.wait(in_n, near.at[pl.ds(0, 3)])
 
         def expert(s, e):
             return ((z * ny + y) * nx + s) * nc + e if x_first else ((z * ny + s) * nx + x) * nc + e
@@ -444,31 +462,28 @@
         lax.fori_loop(0, 4, squeeze, 0)
         up, dn, far = step(b, 1), step(b, 3), step(b, 2)
         lo, hi = pl.ds(0, nz // 2), pl.ds(nz // 2, nz // 2)
-        f_up, f_dn = go(out2.at[far, :, lo], via2.at[0], to(a, up)), go(out2.at[far, :, hi], via2.at[1], to(a, dn))
-        n_up, n_dn = go(out2.at[up], in2.at[b], to(a, up)), go(out2.at[dn], in2.at[b], to(a, dn))
+        go(out2.at[far, :, lo], via2.at[0], to(a, up), in_v)
+        go(out2.at[far, :, hi], via2.at[1], to(a, dn), in_v)
+        go(out2.at[up], in2.at[b], to(a, up), in_2)
+        go(out2.at[dn], in2.at[b], to(a, dn), in_2)
         in2[b] = out2[b]
         yield
-        f_up.wait_recv()
-        r_up = go(via2.at[0], in2.at[dn, :, lo], to(a, up))
-        f_dn.wait_recv()
-        r_dn = go(via2.at[1], in2.at[up, :, hi], to(a, dn))
-        yield
-        for cp in (n_up, n_dn, r_up, r_dn):
-            cp.wait_recv()
+        link.wait(in_v, via2)
+        go(via2.at[0], in2.at[dn, :, lo], to(a, up), in_2)
+        go(via2.at[1], in2.at[up, :, hi], to(a, dn), in_2)
+        yield
+        link.wait(in_2, in2.at[pl.ds(0, 3)])
         for j in range(3):
             out3[:, j] = (in2[0, j] + in2[1, j]) + (in2[2, j] + in2[3, j])
-        last = []
         for d in by_distance:
             zz = lax.rem(z + d, nz)
-            last.append(go(in2.at[:, 3, zz], cold_land.at[z], dev(zz, y, x, c)))
-        for d in by_distance:
-            zz = lax.rem(z + d, nz)
-            last.append(go(out3.at[zz], hot_land.at[z], dev(zz, y, x, c)))
+            go(in2.at[:, 3, zz], cold_land.at[z], dev(zz, y, x, c), in_s)
+            go(out3.at[zz], hot_land.at[z], dev(zz, y, x, c), in_l)
         cold_land[z] = in2[:, 3, z]
         hot_land[z] = out3[z]
         yield
-        for cp in last:
-            cp.wait_recv()
+        link.wait(in_s, cold_land.at[pl.ds(0, nz - 1)])
+        link.wait(in_l, hot_land.at[pl.ds(0, nz - 1)])
 
     def weight_grad(k):
         if k % 2 == 0:
@@ -483,6 +498,7 @@
     ys, dxs = [back(0), back(1)], [back(2), back(3)]
     todo = [functools.partial(weight_grad, k) for k in range(8)]
     undone = [functools.partial(backward, i) for i in range(steps)]
+    unsent = [functools.partial(backward_rows, i) for i in range(steps)]
 
     def turns(text):
         for turn in text:
@@ -496,6 +512,8 @@
                 take_turns(grad_plans + plane_plan)
             elif turn == 'b' and undone:
                 undone.pop(0)()
+            elif turn == 'B' and unsent:
+                unsent.pop(0)()
             elif turn == 'w':
                 todo.pop(0)()
 
@@ -552,20 +570,24 @@
     gx_ref[...] = (dx0 + dx1 + through_gate).astype(BF16)
     save(1)
     take_turns(d_plans)
+    n_dev = nz * ny * nx * nc
     flatten(d_land, d_all)
     expert = iota((n_exp, 256), 0).astype(F32)
-    n_tok_z = ny * nx * nc * n_tok
-    def gate_part(zz, carry):
-        start = pl.multiple_of(zz * (ny * nx * nc), ny * nx * nc)
-        c0, c1 = (plain_id(pair_rows(token_lanes(m_all, k, start, n_tok_z // 128))) for k in range(2))
-        e0, e1 = (pair_rows(token_lanes(d_all, k, start, n_tok_z // 128)) for k in range(2))
-        spread = [jnp.where(expert == c0[p:p + 1], e0[p:p + 1], jnp.where(expert == c1[p:p + 1], e1[p:p + 1], 0.0)).astype(BF16) for p in range(n_tok_z // 256)]
-        return carry + dot(jnp.concatenate(spread, axis=1), x_all[zz].reshape(n_tok_z, x_all.shape[-1]), 1, 0)
-
-    gate_ref[...] = lax.fori_loop(0, nz, gate_part, jnp.zeros((n_exp, x_all.shape[-1]), F32)).T
+    some = n_dev // 4
+    codes = [plain_id(pair_rows(token_lanes(m_all, k, 0, some))) for k in range(2)]
+    grads = [pair_rows(token_lanes(d_all, k, 0, some)) for k in range(2)]
+    total = jnp.zeros((n_exp, x_all.shape[-1]), F32)
+    zs = nz // 4 or 1
+    for z0 in range(0, nz, zs):
+        spread = []
+        for p in range(z0 * ny, (z0 + zs) * ny):
+            q = slice(p, p + 1)
+            spread.append(jnp.where(expert == codes[0][q], grads[0][q], jnp.where(expert == codes[1][q], grads[1][q], 0.0)).astype(BF16))
+        total += dot(jnp.concatenate(spread, axis=1), x_all[z0:z0 + zs].reshape(zs * ny * 256, x_all.shape[-1]), 1, 0)
+    gate_ref[...] = total.T
     save(2)
-    for cp in sent:
-        cp.wait_send()
+    for link in all_links:
+        link.finish(pad, pad_row)
     for cp in saves:
         cp.wait()
 
@@ -580,32 +602,29 @@
     hbm = pl.BlockSpec(memory_space=pltpu.HBM)
     out = jax.ShapeDtypeStruct
     work = [(4, 4, nz), (4, 2, 4, nz), (2, 2, 2, nz), (4, 4, nz), (2, 4, nz // 2), (4, 4, nz), (nz, 3), (nz, 3), (nz, 4)]
-    lines, planes = nz - 1 + 4 + 16 + 4, 3 + 3 + nz + nz
-    counts = [lines] * 4 + [planes] + [nz - 1 + 3 + 3 + 1] + [1 + 12 + 6 + 2 * (nz - 1)] * 4 + [nz - 1 + 3 + 3 + 1]
-    sems = []
-    for k in counts:
-        sems += [pltpu.SemaphoreType.DMA((k,))] * 2
+    n_group = 4 * 14 + 3 + nz // 2 + 4 + 4 * 8 + 4
+    sems = [pltpu.SemaphoreType.DMA((11,)), pltpu.SemaphoreType.DMA((n_group,))]
     results = [(tokens.shape, BF16), (tokens.shape, BF16), ((d_model, n_dev), F32), ((d_model, d_hidden), F32), ((d_hidden, d_model), F32)]
-    row, n_dma = (1, 128), 16
+    row = (1, 128)
     kept = [(tokens.shape, BF16), (tokens.shape, BF16), (ids.shape, jnp.int32), (w_gate.shape, BF16), (w1.shape, BF16), (w2.shape, BF16), (row, F32), (dims + row, F32),
             (dims + tokens.shape, BF16), (dims + tokens.shape, BF16), ((n_row, d_model), BF16), ((n_row, d_model), BF16), ((n_row, d_hidden), BF16), ((n_row, d_hidden), BF16), ((n_row, d_hidden), F32), ((n_dev, 128), F32), (tile, F32), (row, F32),
-            (dims + row, F32), ((n_dev, 128), F32)]
+            (dims + row, F32), ((n_dev, 128), F32), ((1024,) + tile, BF16), ((n_dev,) + row, F32)]
     return pl.pallas_call(
         functools.partial(block_kernel, dims, (6, len(results), len(results), len(kept), 4, 4 * len(work), 3, len(sems))),
         out_shape=[out(*r) for r in results],
         in_specs=[hbm] * 6,
         out_specs=[hbm] * len(results),
         scratch_shapes=[pltpu.VMEM(*r) for r in results + kept] + [pltpu.VMEM((nc, nx, ny, nz) + tile, BF16)] * 4 + [pltpu.VMEM(w + tile, BF16) for w in work] * 4
-        + [pltpu.SemaphoreType.DMA((n_dma,))] * 3 + sems,
+        + [pltpu.SemaphoreType.DMA((k,)) for k in (8, 2, 11)] + sems,
         compiler_params=pltpu.CompilerParams(collective_id=0, has_side_effects=True, vmem_limit_bytes=VMEM_LIMIT),
         name='block',
     )(tokens, grad_out, ids, w_gate, w1, w2)
 
 
 VMEM_LIMIT = 67043328
-FIRST = 'ctcgmttcgtmtcgtgmtcgt'
-SECOND = 'gybybyybybyxwwyxxwxwy'
-THIRD = 'dxwdxwdxwdwx'
+FIRST = 'tmcgttmctgtmtgtcmgt'
+SECOND = 'ygbybyBybBybByBxwwyxwxxwy'
+THIRD = 'dxwwdxdxwdwx'
 
 
 def pass_kernel(n, *refs):

time: 96.1 us -> 96.2 us (level)
  the two profiles are of different devices: /device:TPU:1 before, /device:TPU:8 now
where the time goes in v7:
time: 96.2 us; the launch traced here: 96 us
  Pallas kernels  95.2 us (99%)
    pallas_call x1, Pallas kernels, block_call(): pl.pallas_call(functools.partial(block_kernel, dims, (6, len(results), le...  92.5 us
    pallas_call x1, Pallas kernels, pass_on(): pl.pallas_call(functools.partial(pass_kernel, n), out_shape=[jax.ShapeDty...  2.74 us

profile of v7, /device:TPU:8, one launch (start us, length us, event | category | flops | bytes accessed | tf_op | source)
XLA Modules:
  0.0 96.0 jit_solution(13693807982235413303)
XLA Ops:
  0.6 92.5 %block.1 = (bf16[32,256]{1,0:T(8,128)(2,1)}, bf16[32,256]{1,0:T(8,128)(2,1)}, f32[256,256]{1,0:T(8,128)}, f32[256,1024]{1,0:T(8,128)}, f32[1024,256]{1,0:T(8,128)}) custom-call(bf16[32,256]{1,0:T(8,128)(2,1)} %refs_0_.1, bf16[32,256]{1,0:T(8,128)(2,1)} %refs_1_.1, s32[2,32]{1,0:T(2,128)} %bitcast.7, bf16[256,256]{1,0:T(8,128)(2,1)} %refs_3_.1, ...), custom_call_target="tpu_custom_call" | custom-call | tf_op jit(solution)/shard_map/block/pallas_call | solution.py:612
  93.1 2.7 %pass_on.1 = (bf16[32,256]{1,0:T(8,128)(2,1)}, bf16[32,256]{1,0:T(8,128)(2,1)}, f32[256,256]{1,0:T(8,128)}, f32[256,1024]{1,0:T(8,128)}, f32[1024,256]{1,0:T(8,128)}) custom-call(bf16[32,256]{1,0:T(8,128)(2,1)} %get-tuple-element.15.refs_0_, bf16[32,256]{1,0:T(8,128)(2,1)} %get-tuple-element.16.refs_1_, f32[256,256]{1,0:T(8,128)} %get-tuple-element.17.refs_2_, ...), custom_call_target="tpu_custom_call" | custom-call | tf_op jit(solution)/shard_map/pass_on/pallas_call | solution.py:646

commit v8 on v7

--- a/solution.py
+++ b/solution.py
@@ -132,19 +132,11 @@
         raise ValueError(self.bytes)
 
 
-def take_turns(plans):
-    live = list(plans)
-    while live:
-        for g in list(live):
-            if next(g, 'end') == 'end':
-                live.remove(g)
-
-
 def block_kernel(dims, sizes, *refs):
     nz, ny, nx, nc = dims
     refs = iter(refs)
     refs = [list(itertools.islice(refs, n)) for n in sizes]
-    (tok_hbm, dout_hbm, ids_hbm, wg_hbm, w1_hbm, w2_hbm), outs, held, kept, rows, works, (load_sem, keep_sem, save_sem), sems = refs
+    (tok_hbm, dout_hbm, ids_hbm, wg_hbm, w1_hbm, w2_hbm), outs, held, kept, rows, areas, (load_sem, keep_sem, save_sem), sems = refs
     out_ref, gx_ref, gate_ref, g1_ref, g2_ref = held
     tok, dout, ids, wg, w1, w2, row, m_land, x_all, g_all, xs_ref, dys_ref, h_ref, da_ref, a_ref, m_all, hot_ref, d_row, d_land, d_all, pad, pad_row = kept
     z, y, x, c, dev = coords(dims)
@@ -242,48 +234,6 @@
         yield
         link.wait(in_r, at(full, full, q0))
         over(qo)
-        yield
-        link.wait(in_c, ref.at[full, full, full, c, rows])
-
-    def by_planes(link, ref, rows):
-        go = lambda part, group, *to: link.go(part, part, dev(*to), group)
-        at = lambda zz, ys=full: ref.at[zz, ys, full, c, rows]
-        in_x, in_y, in_c = [link.group() for _ in range(3)]
-        own = ref.at[z, y, x, c, rows]
-        for d in range(1, nx):
-            go(own, in_x, z, y, step(x, d), c)
-        yield
-        link.wait(in_x, ref.at[z, y, pl.ds(0, nx - 1), c, rows])
-        line = ref.at[z, y, full, c, rows]
-        for d in range(1, ny):
-            go(line, in_y, z, step(y, d), x, c)
-        yield
-        link.wait(in_y, ref.at[z, pl.ds(0, ny - 1), full, c, rows])
-
-        def over(*planes):
-            for zz in planes:
-                link.go(at(zz), at(zz), mate, in_c)
-
-        half = nz // 2
-        lower, upper = pl.ds(0, ny // 2), pl.ds(ny // 2, ny // 2)
-
-        def pair(d):
-            a, b = (full, full) if d + 1 < half else (lower, upper)
-            group = link.group()
-            go(at(step(z, nz - d, nz), a), group, step(z, 1, nz), y, x, c)
-            go(at(step(z, d, nz), b), group, step(z, nz - 1, nz), y, x, c)
-            return group
-
-        group = pair(0)
-        over(z)
-        for d in range(1, half + 1):
-            yield
-            link.wait(group, at(pl.ds(0, 2) if d < half else z))
-            if d < half:
-                group = pair(d)
-                over(step(z, d, nz), step(z, nz - d, nz))
-            else:
-                over(step(z, d, nz))
         yield
         link.wait(in_c, ref.at[full, full, full, c, rows])
 
@@ -306,9 +256,8 @@
         for g in plans:
             next(g, None)
 
-    tok_plans = [by_lines(next(links), x_all, slice(0, 16), True), by_lines(next(links), x_all, slice(16, 32), False)]
-    grad_plans = [by_lines(next(links), g_all, slice(0, 8), True), by_lines(next(links), g_all, slice(8, 16), False)]
-    plane_plan = [by_planes(next(links), g_all, slice(16, 32))]
+    halves = [slice(0, 16), slice(16, 32)]
+    tok_plans, grad_plans = [[by_lines(next(links), ref, half, half.start == 0) for half in halves] for ref in (x_all, g_all)]
     loads[0].wait()
     advance(tok_plans)
     for ld in loads[2:5]:
@@ -319,12 +268,7 @@
     place.wait()
     row_plan = [gather_rows(next(links), m_land, range(4))]
     loads[1].wait()
-    advance(row_plan + plane_plan + grad_plans)
-    for turn in FIRST:
-        advance({'t': tok_plans, 'g': grad_plans, 'c': plane_plan, 'm': row_plan}[turn])
-    take_turns(row_plan)
-    take_turns(tok_plans)
-
+    advance(row_plan + grad_plans)
     def flatten(land, flat):
         def lines(zz, carry):
             for k in range(ny * nx * nc):
@@ -333,19 +277,21 @@
 
         lax.fori_loop(0, nz, lines, 0)
 
-    flatten(m_land, m_all)
-    for ld in loads[5:]:
-        ld.wait()
 
     me = lax.axis_index('ep').astype(F32)
-    code = m_all[...]
-    left = jnp.where((iota(code.shape, 1) < 64) & (code >= 256.0), code - 256.0, 999.0)
-    found = []
-    for _ in range(3):
-        best = jnp.min(jnp.min(left, axis=0, keepdims=True), axis=1, keepdims=True)
-        left = jnp.where(left == best, 999.0, left)
-        found.append(jnp.broadcast_to(best, (1, 128)))
-    hot_ref[...] = jnp.concatenate(found + [jnp.full((5, 128), 999.0, F32)], axis=0)
+    def read_rows():
+        flatten(m_land, m_all)
+        for ld in loads[5:]:
+            ld.wait()
+        code = m_all[...]
+        left = jnp.where((iota(code.shape, 1) < 64) & (code >= 256.0), code - 256.0, 999.0)
+        found = []
+        for _ in range(3):
+            best = jnp.min(jnp.min(left, axis=0, keepdims=True), axis=1, keepdims=True)
+            left = jnp.where(left == best, 999.0, left)
+            found.append(jnp.broadcast_to(best, (1, 128)))
+        hot_ref[...] = jnp.concatenate(found + [jnp.full((5, 128), 999.0, F32)], axis=0)
+
     steps = 4 if nz == 8 else 1
     per = nz // steps
     n_quad = per * ny * nx * nc // 4
@@ -394,16 +340,13 @@
     def backward_rows(i):
         put(i, dot(da_ref[pl.ds(i * n_slot, n_slot)], w1[...], 1, 1), rows[2:])
 
-    for i in range(steps):
-        forward(i)
-        advance(grad_plans + plane_plan if i else grad_plans)
-
     def back(i):
         h = rows[i]
-        other, near, via, out2, via2, in2, out3, hot_land, cold_land = works[9 * i:9 * i + 9]
+        other, near, via, out2, via2, in2, out3, hot_land, cold_land = areas[9 * i:9 * i + 9]
         link = next(links)
         go = link.go
-        in_c, in_e, in_h, in_n, in_v, in_2, in_l, in_s = [link.group() for _ in range(8)]
+        in_c, in_e, in_h = [[link.group(), link.group()] for _ in range(3)]
+        in_n, in_v, in_2, in_l, in_s = [link.group() for _ in range(5)]
         x_first = i % 2 == 0
         a, b = (x, y) if x_first else (y, x)
 
@@ -415,27 +358,42 @@
 
         up, dn, far = step(a, 1), step(a, 3), step(a, 2)
         lo, hi = pl.ds(0, 2), pl.ds(2, 2)
-        go(h.at[1 - c], other, mate, in_c)
-
-        def spread(ref, lead, e, group):
-            go(ref.at[index(lead, far, lo)], via.at[0, e], to(up, b), group)
-            go(ref.at[index(lead, far, hi)], via.at[1, e], to(dn, b), group)
-            go(ref.at[index(lead, up, full)], near.at[a, e], to(up, b), in_n)
-            go(ref.at[index(lead, dn, full)], near.at[a, e], to(dn, b), in_n)
-
-        def relay(e, group):
-            link.wait(group, via.at[:, e])
-            go(via.at[0, e], near.at[dn, e, lo], to(up, b), in_n)
-            go(via.at[1, e], near.at[up, e, hi], to(dn, b), in_n)
-
-        spread(h, (c,), c, in_e)
-        yield
-        link.wait(in_c, other)
-        spread(other, (), 1 - c, in_h)
-        yield
-        relay(c, in_e)
-        yield
-        relay(1 - c, in_h)
+        parts = [pl.ds(0, nz // 2), pl.ds(nz // 2, nz // 2)]
+
+        def start(k):
+            zs = parts[k]
+            go(h.at[1 - c, :, :, zs], other.at[:, :, zs], mate, in_c[k])
+            spread(h, (c,), c, zs, in_e[k])
+
+        def follow(k):
+            link.wait(in_c[k], other.at[:, :, parts[k]])
+            spread(other, (), 1 - c, parts[k], in_h[k])
+
+        def spread(ref, lead, e, zs, group):
+            go(ref.at[index(lead, far, lo) + (zs,)], via.at[0, e, :, zs], to(up, b), group)
+            go(ref.at[index(lead, far, hi) + (zs,)], via.at[1, e, :, zs], to(dn, b), group)
+            go(ref.at[index(lead, up, full) + (zs,)], near.at[a, e, :, zs], to(up, b), in_n)
+            go(ref.at[index(lead, dn, full) + (zs,)], near.at[a, e, :, zs], to(dn, b), in_n)
+
+        def relay(e, zs, group):
+            link.wait(group, via.at[:, e, :, zs])
+            go(via.at[0, e, :, zs], near.at[dn, e, lo, zs], to(up, b), in_n)
+            go(via.at[1, e, :, zs], near.at[up, e, hi, zs], to(dn, b), in_n)
+
+        start(0)
+        yield
+        follow(0)
+        yield
+        start(1)
+        yield
+        relay(c, parts[0], in_e[0])
+        relay(1 - c, parts[0], in_h[0])
+        yield
+        follow(1)
+        yield
+        relay(c, parts[1], in_e[1])
+        yield
+        relay(1 - c, parts[1], in_h[1])
         yield
         link.wait(in_n, near.at[pl.ds(0, 3)])
 
@@ -450,12 +408,12 @@
         mine = [(wide(is_hot[0][k] + is_hot[1][k] + is_hot[2][k]) < 0.5) & (line == s * nc + e) for k, (s, e) in enumerate(places)]
 
         def squeeze(bb, carry):
-            parts = [h[index((c,), a, bb)], other[index((), a, bb)]] + [near[s, e, bb] for s, e in places[2:]]
+            given = [h[index((c,), a, bb)], other[index((), a, bb)]] + [near[s, e, bb] for s, e in places[2:]]
             for j in range(3):
-                out2[bb, j] = sum(parts[k] * weight[j][k] for k in range(8))
+                out2[bb, j] = sum(given[k] * weight[j][k] for k in range(8))
             singles = jnp.zeros((nz, 8, 128), F32)
             for k in range(8):
-                singles = jnp.where(mine[k], jnp.sum(parts[k].astype(F32), axis=1, keepdims=True), singles)
+                singles = jnp.where(mine[k], jnp.sum(given[k].astype(F32), axis=1, keepdims=True), singles)
             out2[bb, 3] = singles.astype(BF16)
             return carry
 
@@ -496,38 +454,12 @@
             save(3, (full, part))
 
     ys, dxs = [back(0), back(1)], [back(2), back(3)]
-    todo = [functools.partial(weight_grad, k) for k in range(8)]
-    undone = [functools.partial(backward, i) for i in range(steps)]
-    unsent = [functools.partial(backward_rows, i) for i in range(steps)]
-
-    def turns(text):
-        for turn in text:
-            if turn == 'y':
-                advance(ys)
-            elif turn == 'x':
-                advance(dxs)
-            elif turn == 'd':
-                advance(d_plans)
-            elif turn == 'g':
-                take_turns(grad_plans + plane_plan)
-            elif turn == 'b' and undone:
-                undone.pop(0)()
-            elif turn == 'B' and unsent:
-                unsent.pop(0)()
-            elif turn == 'w':
-                todo.pop(0)()
-
-    turns(SECOND)
-
-    r0, r1 = ids[0:1].astype(F32), ids[1:2].astype(F32)
-    i0, i1 = as_col(r0), as_col(r1)
-    tokens = tok[...]
-    g0, g1 = gates(tokens, i0, i1, wg[...])
     n_tok = tok.shape[0]
+    memo = {}
     earlier = iota((n_tok, n_tok), 1) < iota((n_tok, n_tok), 0)
     n_exp = wg.shape[1]
 
-    def where_from(i):
+    def where_from(i, r0, r1):
         rank = jnp.sum(jnp.where(earlier & ((i == r0) | (i == r1)), 1.0, 0.0), axis=1, keepdims=True)
         slot = jnp.full((n_tok, 1), -1.0, F32)
         for j in range(3):
@@ -538,54 +470,71 @@
         pick = lambda m: m.astype(F32).astype(BF16)
         return pick(iota((n_tok, 32), 1).astype(F32) == slot), (pick((lane == e) & single), pick((lane == ((zz * nx + xx) * ny + yy) * nc + core) & single))
 
-    chosen = [where_from(i0), where_from(i1)]
-
-    def rows_of(kind):
+    def rows_of(kind, chosen):
         parts = []
         for half in range(2):
-            hot_land, cold_land = works[9 * (kind + half) + 7:9 * (kind + half) + 9]
+            hot_land, cold_land = areas[9 * (kind + half) + 7:9 * (kind + half) + 9]
             hot = jnp.sum(hot_land[...].astype(F32), axis=0).reshape(24, 128)
             hot = jnp.concatenate([hot, jnp.zeros((8, 128), F32)], axis=0).astype(BF16)
             cold = cold_land[...].astype(F32).reshape(n_exp, 128).astype(BF16)
             parts.append([dot(by_slot, hot, 1, 0) + dot(by_place[half], cold, 1, 0) for by_slot, by_place in chosen])
         return [jnp.concatenate([parts[0][k], parts[1][k]], axis=1) for k in range(2)]
 
-    y0, y1 = rows_of(0)
-    out_ref[...] = (g0 * y0 + g1 * y1).astype(BF16)
-    save(0)
-    grad = dout[...].astype(F32)
-    dg0, dg1 = (jnp.sum(grad * v, axis=1, keepdims=True) for v in (y0, y1))
-    mean = g0 * dg0 + g1 * dg1
-    d0, d1 = ((g * (dg - mean)).astype(BF16).astype(F32) for g, dg in ((g0, dg0), (g1, dg1)))
-    d_row[...] = jnp.concatenate([as_row(d0), as_row(d1), jnp.zeros((1, 2 * n_tok), F32)], axis=1)
-    place = pltpu.make_async_copy(d_row, d_land.at[z, y, x, c], keep_sem.at[1])
-    place.start()
-    place.wait()
-    d_plans = [gather_rows(next(links), d_land, range(4))]
-    expert = iota((n_tok, n_exp), 1).astype(F32)
-    spread = jnp.where(expert == i0, d0, jnp.where(expert == i1, d1, 0.0)).astype(BF16)
-    through_gate = dot(spread, wg[...], 1, 1)
-    turns(THIRD)
-    dx0, dx1 = rows_of(2)
-    gx_ref[...] = (dx0 + dx1 + through_gate).astype(BF16)
-    save(1)
-    take_turns(d_plans)
+    def combine():
+        r0, r1 = ids[0:1].astype(F32), ids[1:2].astype(F32)
+        i0, i1 = as_col(r0), as_col(r1)
+        g0, g1 = gates(tok[...], i0, i1, wg[...])
+        chosen = [where_from(i, r0, r1) for i in (i0, i1)]
+        y0, y1 = rows_of(0, chosen)
+        grad = dout[...].astype(F32)
+        dg0, dg1 = (jnp.sum(grad * v, axis=1, keepdims=True) for v in (y0, y1))
+        mean = g0 * dg0 + g1 * dg1
+        d0, d1 = ((g * (dg - mean)).astype(BF16).astype(F32) for g, dg in ((g0, dg0), (g1, dg1)))
+        d_row[...] = jnp.concatenate([as_row(d0), as_row(d1), jnp.zeros((1, 2 * n_tok), F32)], axis=1)
+        place = pltpu.make_async_copy(d_row, d_land.at[z, y, x, c], keep_sem.at[1])
+        place.start()
+        out_ref[...] = (g0 * y0 + g1 * y1).astype(BF16)
+        save(0)
+        place.wait()
+        d_plans.append(gather_rows(next(links), d_land, range(4)))
+        advance(d_plans)
+        expert = iota((n_tok, n_exp), 1).astype(F32)
+        spread = jnp.where(expert == i0, d0, jnp.where(expert == i1, d1, 0.0)).astype(BF16)
+        memo.update(chosen=chosen, through=dot(spread, wg[...], 1, 1))
+
+    def finish():
+        dx0, dx1 = rows_of(2, memo['chosen'])
+        gx_ref[...] = (dx0 + dx1 + memo['through']).astype(BF16)
+        save(1)
+
     n_dev = nz * ny * nx * nc
-    flatten(d_land, d_all)
-    expert = iota((n_exp, 256), 0).astype(F32)
-    some = n_dev // 4
-    codes = [plain_id(pair_rows(token_lanes(m_all, k, 0, some))) for k in range(2)]
-    grads = [pair_rows(token_lanes(d_all, k, 0, some)) for k in range(2)]
-    total = jnp.zeros((n_exp, x_all.shape[-1]), F32)
-    zs = nz // 4 or 1
-    for z0 in range(0, nz, zs):
-        spread = []
-        for p in range(z0 * ny, (z0 + zs) * ny):
-            q = slice(p, p + 1)
-            spread.append(jnp.where(expert == codes[0][q], grads[0][q], jnp.where(expert == codes[1][q], grads[1][q], 0.0)).astype(BF16))
-        total += dot(jnp.concatenate(spread, axis=1), x_all[z0:z0 + zs].reshape(zs * ny * 256, x_all.shape[-1]), 1, 0)
-    gate_ref[...] = total.T
-    save(2)
+
+    def gate_grad():
+        flatten(d_land, d_all)
+        expert = iota((n_exp, 256), 0).astype(F32)
+        codes = [plain_id(pair_rows(token_lanes(m_all, k, 0, n_dev // 4))) for k in range(2)]
+        grads = [pair_rows(token_lanes(d_all, k, 0, n_dev // 4)) for k in range(2)]
+        total = jnp.zeros((n_exp, x_all.shape[-1]), F32)
+        zs = nz // 4 or 1
+        for z0 in range(0, nz, zs):
+            spread = []
+            for p in range(z0 * ny, (z0 + zs) * ny):
+                q = slice(p, p + 1)
+                spread.append(jnp.where(expert == codes[0][q], grads[0][q], jnp.where(expert == codes[1][q], grads[1][q], 0.0)).astype(BF16))
+            total += dot(jnp.concatenate(spread, axis=1), x_all[z0:z0 + zs].reshape(zs * ny * 256, x_all.shape[-1]), 1, 0)
+        gate_ref[...] = total.T
+        save(2)
+
+    d_plans = []
+    moves = {'t': tok_plans, 'g': grad_plans, 'm': row_plan, 'y': ys, 'x': dxs, 'd': d_plans}
+    works = {'f': [functools.partial(forward, i) for i in range(steps)], 'b': [functools.partial(backward, i) for i in range(steps)],
+             'B': [functools.partial(backward_rows, i) for i in range(steps)], 'w': [functools.partial(weight_grad, k) for k in range(8)],
+             'h': [read_rows], 'c': [combine], 'k': [gate_grad], 'e': [finish]}
+    for turn in SCHEDULE:
+        if turn in moves:
+            advance(moves[turn])
+        elif works[turn]:
+            works[turn].pop(0)()
     for link in all_links:
         link.finish(pad, pad_row)
     for cp in saves:
@@ -602,8 +551,8 @@
     hbm = pl.BlockSpec(memory_space=pltpu.HBM)
     out = jax.ShapeDtypeStruct
     work = [(4, 4, nz), (4, 2, 4, nz), (2, 2, 2, nz), (4, 4, nz), (2, 4, nz // 2), (4, 4, nz), (nz, 3), (nz, 3), (nz, 4)]
-    n_group = 4 * 14 + 3 + nz // 2 + 4 + 4 * 8 + 4
-    sems = [pltpu.SemaphoreType.DMA((11,)), pltpu.SemaphoreType.DMA((n_group,))]
+    n_group = 4 * 14 + 4 + 4 * 11 + 4
+    sems = [pltpu.SemaphoreType.DMA((10,)), pltpu.SemaphoreType.DMA((n_group,))]
     results = [(tokens.shape, BF16), (tokens.shape, BF16), ((d_model, n_dev), F32), ((d_model, d_hidden), F32), ((d_hidden, d_model), F32)]
     row = (1, 128)
     kept = [(tokens.shape, BF16), (tokens.shape, BF16), (ids.shape, jnp.int32), (w_gate.shape, BF16), (w1.shape, BF16), (w2.shape, BF16), (row, F32), (dims + row, F32),
@@ -622,9 +571,7 @@
 
 
 VMEM_LIMIT = 67043328
-FIRST = 'tmcgttmctgtmtgtcmgt'
-SECOND = 'ygbybyBybBybByBxwwyxwxxwy'
-THIRD = 'dxwwdxdxwdwx'
+SCHEDULE = 'tmttmgttmgttgmtgth' + 'fgfgyfgyf' + 'ygygybyybyBBxbybBBxxyx' + 'wxwwxwxyc' + 'wxwwdxdwxddkx' + 'e'
 
 
 def pass_kernel(n, *refs):

time: 96.2 us -> 92.4 us (0.960)
  the two profiles are of different devices: /device:TPU:8 before, /device:TPU:32 now
where the time goes in v8:
time: 92.4 us; the launch traced here: 92.2 us
  Pallas kernels  91.4 us (99%)
    pallas_call x1, Pallas kernels, block_call(): pl.pallas_call(functools.partial(block_kernel, dims, (6, len(results), le...  88.6 us
    pallas_call x1, Pallas kernels, pass_on(): pl.pallas_call(functools.partial(pass_kernel, n), out_shape=[jax.ShapeDty...  2.74 us

profile of v8, /device:TPU:32, one launch (start us, length us, event | category | flops | bytes accessed | tf_op | source)
XLA Modules:
  0.0 92.2 jit_solution(16858371034860478172)
XLA Ops:
  0.6 88.6 %block.1 = (bf16[32,256]{1,0:T(8,128)(2,1)}, bf16[32,256]{1,0:T(8,128)(2,1)}, f32[256,256]{1,0:T(8,128)}, f32[256,1024]{1,0:T(8,128)}, f32[1024,256]{1,0:T(8,128)}) custom-call(bf16[32,256]{1,0:T(8,128)(2,1)} %refs_0_.1, bf16[32,256]{1,0:T(8,128)(2,1)} %refs_1_.1, s32[2,32]{1,0:T(2,128)} %bitcast.7, bf16[256,256]{1,0:T(8,128)(2,1)} %refs_3_.1, ...), custom_call_target="tpu_custom_call" | custom-call | tf_op jit(solution)/shard_map/block/pallas_call | solution.py:561
  89.3 2.7 %pass_on.1 = (bf16[32,256]{1,0:T(8,128)(2,1)}, bf16[32,256]{1,0:T(8,128)(2,1)}, f32[256,256]{1,0:T(8,128)}, f32[256,1024]{1,0:T(8,128)}, f32[1024,256]{1,0:T(8,128)}) custom-call(bf16[32,256]{1,0:T(8,128)(2,1)} %get-tuple-element.15.refs_0_, bf16[32,256]{1,0:T(8,128)(2,1)} %get-tuple-element.16.refs_1_, f32[256,256]{1,0:T(8,128)} %get-tuple-element.17.refs_2_, ...), custom_call_target="tpu_custom_call" | custom-call | tf_op jit(solution)/shard_map/pass_on/pallas_call | solution.py:593

commit v9 on v8

--- a/solution.py
+++ b/solution.py
@@ -27,13 +27,6 @@
         return (((z * ny + y) * nx + x) * nc + c,)
 
     return z, y, x, c, dev
-
-
-def meet(peers):
-    barrier = pltpu.get_barrier_semaphore()
-    for peer in peers:
-        pl.semaphore_signal(barrier, inc=1, device_id=peer, device_id_type=MESH)
-    pl.semaphore_wait(barrier, len(peers))
 
 
 def dot(a, b, ca, cb):
@@ -163,7 +156,18 @@
         peers.append(dev(z, y, lax.rem(x + d, nx), c))
     mate = dev(z, y, x, 1 - c)
     peers.append(mate)
-    meet(peers)
+    barrier = pltpu.get_barrier_semaphore()
+    for peer in peers:
+        pl.semaphore_signal(barrier, inc=1, device_id=peer, device_id_type=MESH)
+    for ld in loads[2:5]:
+        ld.wait()
+    row[...] = choice_row(tok[...], ids[...], wg[...])
+    place = pltpu.make_async_copy(row, m_land.at[z, y, x, c], keep_sem.at[0])
+    place.start()
+    loads[0].wait()
+    loads[1].wait()
+    place.wait()
+    pl.semaphore_wait(barrier, len(peers))
 
     full = slice(None)
     by_distance = sorted(range(1, nz), key=lambda d: abs(d - nz // 2))
@@ -258,16 +262,8 @@
 
     halves = [slice(0, 16), slice(16, 32)]
     tok_plans, grad_plans = [[by_lines(next(links), ref, half, half.start == 0) for half in halves] for ref in (x_all, g_all)]
-    loads[0].wait()
+    row_plan = [gather_rows(next(links), m_land, range(4))]
     advance(tok_plans)
-    for ld in loads[2:5]:
-        ld.wait()
-    row[...] = choice_row(tok[...], ids[...], wg[...])
-    place = pltpu.make_async_copy(row, m_land.at[z, y, x, c], keep_sem.at[0])
-    place.start()
-    place.wait()
-    row_plan = [gather_rows(next(links), m_land, range(4))]
-    loads[1].wait()
     advance(row_plan + grad_plans)
     def flatten(land, flat):
         def lines(zz, carry):
@@ -571,7 +567,7 @@
 
 
 VMEM_LIMIT = 67043328
-SCHEDULE = 'tmttmgttmgttgmtgth' + 'fgfgyfgyf' + 'ygygybyybyBBxbybBBxxyx' + 'wxwwxwxyc' + 'wxwwdxdwxddkx' + 'e'
+SCHEDULE = 'ttmttmttmtgtmgtgh' + 'fgfgyfgyf' + 'ygygygbyybyBBxbyxbBBxyx' + 'wxwwxxwxyc' + 'wwxdwxdwddkx' + 'e'
 
 
 def pass_kernel(n, *refs):

time: 92.4 us -> 96.6 us (1.045)
  the two profiles are of different devices: /device:TPU:32 before, /device:TPU:1 now
where the time goes in v9:
time: 96.6 us; the launch traced here: 96.4 us
  Pallas kernels  95.6 us (99%)
    pallas_call x1, Pallas kernels, block_call(): pl.pallas_call(functools.partial(block_kernel, dims, (6, len(results), le...  92.8 us
    pallas_call x1, Pallas kernels, pass_on(): pl.pallas_call(functools.partial(pass_kernel, n), out_shape=[jax.ShapeDty...  2.74 us

profile of v9, /device:TPU:1, one launch (start us, length us, event | category | flops | bytes accessed | tf_op | source)
XLA Modules:
  0.0 96.4 jit_solution(9547316923051290119)
XLA Ops:
  0.6 92.8 %block.1 = (bf16[32,256]{1,0:T(8,128)(2,1)}, bf16[32,256]{1,0:T(8,128)(2,1)}, f32[256,256]{1,0:T(8,128)}, f32[256,1024]{1,0:T(8,128)}, f32[1024,256]{1,0:T(8,128)}) custom-call(bf16[32,256]{1,0:T(8,128)(2,1)} %refs_0_.1, bf16[32,256]{1,0:T(8,128)(2,1)} %refs_1_.1, s32[2,32]{1,0:T(2,128)} %bitcast.7, bf16[256,256]{1,0:T(8,128)(2,1)} %refs_3_.1, ...), custom_call_target="tpu_custom_call" | custom-call | tf_op jit(solution)/shard_map/block/pallas_call | solution.py:557
  93.5 2.7 %pass_on.1 = (bf16[32,256]{1,0:T(8,128)(2,1)}, bf16[32,256]{1,0:T(8,128)(2,1)}, f32[256,256]{1,0:T(8,128)}, f32[256,1024]{1,0:T(8,128)}, f32[1024,256]{1,0:T(8,128)}) custom-call(bf16[32,256]{1,0:T(8,128)(2,1)} %get-tuple-element.15.refs_0_, bf16[32,256]{1,0:T(8,128)(2,1)} %get-tuple-element.16.refs_1_, f32[256,256]{1,0:T(8,128)} %get-tuple-element.17.refs_2_, ...), custom_call_target="tpu_custom_call" | custom-call | tf_op jit(solution)/shard_map/pass_on/pallas_call | solution.py:589

commit v10 on v9

--- a/solution.py
+++ b/solution.py
@@ -263,8 +263,7 @@
     halves = [slice(0, 16), slice(16, 32)]
     tok_plans, grad_plans = [[by_lines(next(links), ref, half, half.start == 0) for half in halves] for ref in (x_all, g_all)]
     row_plan = [gather_rows(next(links), m_land, range(4))]
-    advance(tok_plans)
-    advance(row_plan + grad_plans)
+    advance(row_plan + tok_plans + grad_plans)
     def flatten(land, flat):
         def lines(zz, carry):
             for k in range(ny * nx * nc):
@@ -567,7 +566,7 @@
 
 
 VMEM_LIMIT = 67043328
-SCHEDULE = 'ttmttmttmtgtmgtgh' + 'fgfgyfgyf' + 'ygygygbyybyBBxbyxbBBxyx' + 'wxwwxxwxyc' + 'wwxdwxdwddkx' + 'e'
+SCHEDULE = 'mttmttmtmttgtth' + 'fggfgyfgyf' + 'yggygyg' + 'bybybyBBxbyxBBxy' + 'wwxxwwxwxyc' + 'xwwdxdxwddkxe'
 
 
 def pass_kernel(n, *refs):

time: 96.6 us -> 95.2 us (0.986)
  Pallas kernels: 95.6 us -> 94.3 us
    pallas_call x1, Pallas kernels: 92.8 us -> 91.5 us  [block_call(): pl.pallas_call(functools.partial(block_kernel, dims, (6, len(results), le...]
where the time goes in v10:
time: 95.2 us; the launch traced here: 95.1 us
  Pallas kernels  94.3 us (99%)
    pallas_call x1, Pallas kernels, block_call(): pl.pallas_call(functools.partial(block_kernel, dims, (6, len(results), le...  91.5 us
    pallas_call x1, Pallas kernels, pass_on(): pl.pallas_call(functools.partial(pass_kernel, n), out_shape=[jax.ShapeDty...  2.74 us

profile of v10, /device:TPU:1, one launch (start us, length us, event | category | flops | bytes accessed | tf_op | source)
XLA Modules:
  0.0 95.1 jit_solution(7844687136500266327)
XLA Ops:
  0.6 91.5 %block.1 = (bf16[32,256]{1,0:T(8,128)(2,1)}, bf16[32,256]{1,0:T(8,128)(2,1)}, f32[256,256]{1,0:T(8,128)}, f32[256,1024]{1,0:T(8,128)}, f32[1024,256]{1,0:T(8,128)}) custom-call(bf16[32,256]{1,0:T(8,128)(2,1)} %refs_0_.1, bf16[32,256]{1,0:T(8,128)(2,1)} %refs_1_.1, s32[2,32]{1,0:T(2,128)} %bitcast.7, bf16[256,256]{1,0:T(8,128)(2,1)} %refs_3_.1, ...), custom_call_target="tpu_custom_call" | custom-call | tf_op jit(solution)/shard_map/block/pallas_call | solution.py:556
  92.1 2.7 %pass_on.1 = (bf16[32,256]{1,0:T(8,128)(2,1)}, bf16[32,256]{1,0:T(8,128)(2,1)}, f32[256,256]{1,0:T(8,128)}, f32[256,1024]{1,0:T(8,128)}, f32[1024,256]{1,0:T(8,128)}) custom-call(bf16[32,256]{1,0:T(8,128)(2,1)} %get-tuple-element.15.refs_0_, bf16[32,256]{1,0:T(8,128)(2,1)} %get-tuple-element.16.refs_1_, f32[256,256]{1,0:T(8,128)} %get-tuple-element.17.refs_2_, ...), custom_call_target="tpu_custom_call" | custom-call | tf_op jit(solution)/shard_map/pass_on/pallas_call | solution.py:588

commit v11 on v10

--- a/solution.py
+++ b/solution.py
@@ -175,7 +175,7 @@
     def step(v, d, m=4):
         return lax.rem(v + d, m)
 
-    def by_lines(link, ref, rows, x_last):
+    def by_lines(link, ref, rows, x_last, late):
         p0, q0 = (y, x) if x_last else (x, y)
         low, high = pl.ds(0, nz // 2), pl.ds(nz // 2, nz // 2)
 
@@ -214,22 +214,36 @@
             link.wait(dn, line)
             go(at(high, p, qp), p0, qm, in_r)
 
+        def pass_one():
+            link.wait(in_p, line)
+            go(at(low, pm, q0), pp, q0, in_f)
+            link.wait(in_m, line)
+            go(at(high, pp, q0), pm, q0, in_f)
+
         go(line, pp, q0, in_p)
         go(line, pm, q0, in_m)
-        spread(p0)
-        yield
-        link.wait(in_p, line)
-        go(at(low, pm, q0), pp, q0, in_f)
-        link.wait(in_m, line)
-        go(at(high, pp, q0), pm, q0, in_f)
-        spread(pm)
-        spread(pp)
-        yield
-        relay(0)
-        yield
-        link.wait(in_f, line)
-        spread(po)
-        over(q0)
+        if late:
+            yield
+            pass_one()
+            yield
+            link.wait(in_f, line)
+            for p in (p0, pm, pp, po):
+                spread(p)
+            over(q0)
+            yield
+            relay(0)
+        else:
+            spread(p0)
+            yield
+            pass_one()
+            spread(pm)
+            spread(pp)
+            yield
+            relay(0)
+            yield
+            link.wait(in_f, line)
+            spread(po)
+            over(q0)
         for i in range(1, 4):
             yield
             relay(i)
@@ -261,7 +275,7 @@
             next(g, None)
 
     halves = [slice(0, 16), slice(16, 32)]
-    tok_plans, grad_plans = [[by_lines(next(links), ref, half, half.start == 0) for half in halves] for ref in (x_all, g_all)]
+    tok_plans, grad_plans = [[by_lines(next(links), ref, half, half.start == 0, ref is g_all) for half in halves] for ref in (x_all, g_all)]
     row_plan = [gather_rows(next(links), m_land, range(4))]
     advance(row_plan + tok_plans + grad_plans)
     def flatten(land, flat):
@@ -566,7 +580,7 @@
 
 
 VMEM_LIMIT = 67043328
-SCHEDULE = 'mttmttmtmttgtth' + 'fggfgyfgyf' + 'yggygyg' + 'bybybyBBxbyxBBxy' + 'wwxxwwxwxyc' + 'xwwdxdxwddkxe'
+SCHEDULE = 'mttgmttmgtmttgtth' + 'fgfgyfgyfgy' + 'yygg' + 'bybybyBBxbyxBBxy' + 'wwxxwwxwxyc' + 'xwwdxdxwddkxe'
 
 
 def pass_kernel(n, *refs):

time: 95.2 us -> 90.4 us (0.950)
  Pallas kernels: 94.3 us -> 89.4 us
    pallas_call x1, Pallas kernels: 91.5 us -> 86.6 us  [block_call(): pl.pallas_call(functools.partial(block_kernel, dims, (6, len(results), le...]
where the time goes in v11:
time: 90.4 us; the launch traced here: 90.2 us
  Pallas kernels  89.4 us (99%)
    pallas_call x1, Pallas kernels, block_call(): pl.pallas_call(functools.partial(block_kernel, dims, (6, len(results), le...  86.6 us
    pallas_call x1, Pallas kernels, pass_on(): pl.pallas_call(functools.partial(pass_kernel, n), out_shape=[jax.ShapeDty...  2.74 us

profile of v11, /device:TPU:1, one launch (start us, length us, event | category | flops | bytes accessed | tf_op | source)
XLA Modules:
  0.0 90.2 jit_solution(10266604716012364439)
XLA Ops:
  0.6 86.6 %block.1 = (bf16[32,256]{1,0:T(8,128)(2,1)}, bf16[32,256]{1,0:T(8,128)(2,1)}, f32[256,256]{1,0:T(8,128)}, f32[256,1024]{1,0:T(8,128)}, f32[1024,256]{1,0:T(8,128)}) custom-call(bf16[32,256]{1,0:T(8,128)(2,1)} %refs_0_.1, bf16[32,256]{1,0:T(8,128)(2,1)} %refs_1_.1, s32[2,32]{1,0:T(2,128)} %bitcast.7, bf16[256,256]{1,0:T(8,128)(2,1)} %refs_3_.1, ...), custom_call_target="tpu_custom_call" | custom-call | tf_op jit(solution)/shard_map/block/pallas_call | solution.py:570
  87.3 2.7 %pass_on.1 = (bf16[32,256]{1,0:T(8,128)(2,1)}, bf16[32,256]{1,0:T(8,128)(2,1)}, f32[256,256]{1,0:T(8,128)}, f32[256,1024]{1,0:T(8,128)}, f32[1024,256]{1,0:T(8,128)}) custom-call(bf16[32,256]{1,0:T(8,128)(2,1)} %get-tuple-element.15.refs_0_, bf16[32,256]{1,0:T(8,128)(2,1)} %get-tuple-element.16.refs_1_, f32[256,256]{1,0:T(8,128)} %get-tuple-element.17.refs_2_, ...), custom_call_target="tpu_custom_call" | custom-call | tf_op jit(solution)/shard_map/pass_on/pallas_call | solution.py:602

commit v12 on v11

--- a/solution.py
+++ b/solution.py
@@ -233,9 +233,11 @@
             yield
             relay(0)
         else:
+            yield
             spread(p0)
             yield
             pass_one()
+            yield
             spread(pm)
             spread(pp)
             yield
@@ -395,10 +397,10 @@
         yield
         start(1)
         yield
+        follow(1)
+        yield
         relay(c, parts[0], in_e[0])
         relay(1 - c, parts[0], in_h[0])
-        yield
-        follow(1)
         yield
         relay(c, parts[1], in_e[1])
         yield
@@ -580,7 +582,7 @@
 
 
 VMEM_LIMIT = 67043328
-SCHEDULE = 'mttgmttmgtmttgtth' + 'fgfgyfgyfgy' + 'yygg' + 'bybybyBBxbyxBBxy' + 'wwxxwwxwxyc' + 'xwwdxdxwddkxe'
+SCHEDULE = 'mttttmgttmgtttgtmth' + 'fgfgyfgyfgy' + 'gygy' + 'bybybyBBxbyxBBxy' + 'wwxxwxwwxxyc' + 'wwxdxwdddkxe'
 
 
 def pass_kernel(n, *refs):

time: 90.4 us -> 93.7 us (1.037)
  Pallas kernels: 89.4 us -> 92.8 us
    pallas_call x1, Pallas kernels: 86.6 us -> 90 us  [block_call(): pl.pallas_call(functools.partial(block_kernel, dims, (6, len(results), le...]
where the time goes in v12:
time: 93.7 us; the launch traced here: 93.6 us
  Pallas kernels  92.8 us (99%)
    pallas_call x1, Pallas kernels, block_call(): pl.pallas_call(functools.partial(block_kernel, dims, (6, len(results), le...  90 us
    pallas_call x1, Pallas kernels, pass_on(): pl.pallas_call(functools.partial(pass_kernel, n), out_shape=[jax.ShapeDty...  2.74 us

profile of v12, /device:TPU:1, one launch (start us, length us, event | category | flops | bytes accessed | tf_op | source)
XLA Modules:
  0.0 93.6 jit_solution(14419451491167195717)
XLA Ops:
  0.6 90.0 %block.1 = (bf16[32,256]{1,0:T(8,128)(2,1)}, bf16[32,256]{1,0:T(8,128)(2,1)}, f32[256,256]{1,0:T(8,128)}, f32[256,1024]{1,0:T(8,128)}, f32[1024,256]{1,0:T(8,128)}) custom-call(bf16[32,256]{1,0:T(8,128)(2,1)} %refs_0_.1, bf16[32,256]{1,0:T(8,128)(2,1)} %refs_1_.1, s32[2,32]{1,0:T(2,128)} %bitcast.7, bf16[256,256]{1,0:T(8,128)(2,1)} %refs_3_.1, ...), custom_call_target="tpu_custom_call" | custom-call | tf_op jit(solution)/shard_map/block/pallas_call | solution.py:572
  90.6 2.7 %pass_on.1 = (bf16[32,256]{1,0:T(8,128)(2,1)}, bf16[32,256]{1,0:T(8,128)(2,1)}, f32[256,256]{1,0:T(8,128)}, f32[256,1024]{1,0:T(8,128)}, f32[1024,256]{1,0:T(8,128)}) custom-call(bf16[32,256]{1,0:T(8,128)(2,1)} %get-tuple-element.15.refs_0_, bf16[32,256]{1,0:T(8,128)(2,1)} %get-tuple-element.16.refs_1_, f32[256,256]{1,0:T(8,128)} %get-tuple-element.17.refs_2_, ...), custom_call_target="tpu_custom_call" | custom-call | tf_op jit(solution)/shard_map/pass_on/pallas_call | solution.py:604

commit v13 on v12

--- a/solution.py
+++ b/solution.py
@@ -582,7 +582,7 @@
 
 
 VMEM_LIMIT = 67043328
-SCHEDULE = 'mttttmgttmgtttgtmth' + 'fgfgyfgyfgy' + 'gygy' + 'bybybyBBxbyxBBxy' + 'wwxxwxwwxxyc' + 'wwxdxwdddkxe'
+SCHEDULE = 'mttmttmgttgtttgtmth' + 'fgfgyfgyfgy' + 'gygy' + 'bybybyBBxbyxBBxy' + 'wwxxwxwwxyc' + 'xwwdxdxwddkxe'
 
 
 def pass_kernel(n, *refs):

time: 93.7 us -> 90.8 us (0.969)
  Pallas kernels: 92.8 us -> 89.8 us
    pallas_call x1, Pallas kernels: 90 us -> 87.1 us  [block_call(): pl.pallas_call(functools.partial(block_kernel, dims, (6, len(results), le...]
where the time goes in v13:
time: 90.8 us; the launch traced here: 90.6 us
  Pallas kernels  89.8 us (99%)
    pallas_call x1, Pallas kernels, block_call(): pl.pallas_call(functools.partial(block_kernel, dims, (6, len(results), le...  87.1 us
    pallas_call x1, Pallas kernels, pass_on(): pl.pallas_call(functools.partial(pass_kernel, n), out_shape=[jax.ShapeDty...  2.74 us

profile of v13, /device:TPU:1, one launch (start us, length us, event | category | flops | bytes accessed | tf_op | source)
XLA Modules:
  0.0 90.6 jit_solution(4503575771839330487)
XLA Ops:
  0.6 87.1 %block.1 = (bf16[32,256]{1,0:T(8,128)(2,1)}, bf16[32,256]{1,0:T(8,128)(2,1)}, f32[256,256]{1,0:T(8,128)}, f32[256,1024]{1,0:T(8,128)}, f32[1024,256]{1,0:T(8,128)}) custom-call(bf16[32,256]{1,0:T(8,128)(2,1)} %refs_0_.1, bf16[32,256]{1,0:T(8,128)(2,1)} %refs_1_.1, s32[2,32]{1,0:T(2,128)} %bitcast.7, bf16[256,256]{1,0:T(8,128)(2,1)} %refs_3_.1, ...), custom_call_target="tpu_custom_call" | custom-call | tf_op jit(solution)/shard_map/block/pallas_call | solution.py:572
  87.7 2.7 %pass_on.1 = (bf16[32,256]{1,0:T(8,128)(2,1)}, bf16[32,256]{1,0:T(8,128)(2,1)}, f32[256,256]{1,0:T(8,128)}, f32[256,1024]{1,0:T(8,128)}, f32[1024,256]{1,0:T(8,128)}) custom-call(bf16[32,256]{1,0:T(8,128)(2,1)} %get-tuple-element.15.refs_0_, bf16[32,256]{1,0:T(8,128)(2,1)} %get-tuple-element.16.refs_1_, f32[256,256]{1,0:T(8,128)} %get-tuple-element.17.refs_2_, ...), custom_call_target="tpu_custom_call" | custom-call | tf_op jit(solution)/shard_map/pass_on/pallas_call | solution.py:604

commit v14 on v13

--- a/solution.py
+++ b/solution.py
@@ -133,13 +133,10 @@
     out_ref, gx_ref, gate_ref, g1_ref, g2_ref = held
     tok, dout, ids, wg, w1, w2, row, m_land, x_all, g_all, xs_ref, dys_ref, h_ref, da_ref, a_ref, m_all, hot_ref, d_row, d_land, d_all, pad, pad_row = kept
     z, y, x, c, dev = coords(dims)
-    saves = []
-
-    def save(k, part=None):
-        src, dst = (held[k], outs[k]) if part is None else (held[k].at[part], outs[k].at[part])
-        cp = pltpu.make_async_copy(src, dst, save_sem.at[len(saves)])
-        cp.start()
-        saves.append(cp)
+    saves = [pltpu.make_async_copy(held[k], outs[k], save_sem.at[k]) for k in range(len(held))]
+
+    def save(k, part):
+        pltpu.make_async_copy(held[k].at[part], outs[k].at[part], save_sem.at[k]).start()
 
     send_sem, recv_sem = sems
     pool = itertools.count()
@@ -203,15 +200,14 @@
 
         def spread(p):
             part = at(full, p, q0)
-            qs.append((p, link.group(), link.group()))
+            qs.append((p, link.group()))
             go(part, p0, qp, qs[-1][1])
-            go(part, p0, qm, qs[-1][2])
+            go(part, p0, qm, qs[-1][1])
 
         def relay(i):
-            p, up, dn = qs[i]
-            link.wait(up, line)
+            p, group = qs[i]
+            link.wait(group, at(full, pl.ds(0, 2), q0))
             go(at(low, p, qm), p0, qp, in_r)
-            link.wait(dn, line)
             go(at(high, p, qp), p0, qm, in_r)
 
         def pass_one():
@@ -505,7 +501,7 @@
         place = pltpu.make_async_copy(d_row, d_land.at[z, y, x, c], keep_sem.at[1])
         place.start()
         out_ref[...] = (g0 * y0 + g1 * y1).astype(BF16)
-        save(0)
+        saves[0].start()
         place.wait()
         d_plans.append(gather_rows(next(links), d_land, range(4)))
         advance(d_plans)
@@ -516,7 +512,7 @@
     def finish():
         dx0, dx1 = rows_of(2, memo['chosen'])
         gx_ref[...] = (dx0 + dx1 + memo['through']).astype(BF16)
-        save(1)
+        saves[1].start()
 
     n_dev = nz * ny * nx * nc
 
@@ -534,7 +530,7 @@
                 spread.append(jnp.where(expert == codes[0][q], grads[0][q], jnp.where(expert == codes[1][q], grads[1][q], 0.0)).astype(BF16))
             total += dot(jnp.concatenate(spread, axis=1), x_all[z0:z0 + zs].reshape(zs * ny * 256, x_all.shape[-1]), 1, 0)
         gate_ref[...] = total.T
-        save(2)
+        saves[2].start()
 
     d_plans = []
     moves = {'t': tok_plans, 'g': grad_plans, 'm': row_plan, 'y': ys, 'x': dxs, 'd': d_plans}
@@ -562,7 +558,7 @@
     hbm = pl.BlockSpec(memory_space=pltpu.HBM)
     out = jax.ShapeDtypeStruct
     work = [(4, 4, nz), (4, 2, 4, nz), (2, 2, 2, nz), (4, 4, nz), (2, 4, nz // 2), (4, 4, nz), (nz, 3), (nz, 3), (nz, 4)]
-    n_group = 4 * 14 + 4 + 4 * 11 + 4
+    n_group = 4 * 10 + 4 + 4 * 11 + 4
     sems = [pltpu.SemaphoreType.DMA((10,)), pltpu.SemaphoreType.DMA((n_group,))]
     results = [(tokens.shape, BF16), (tokens.shape, BF16), ((d_model, n_dev), F32), ((d_model, d_hidden), F32), ((d_hidden, d_model), F32)]
     row = (1, 128)
@@ -575,14 +571,14 @@
         in_specs=[hbm] * 6,
         out_specs=[hbm] * len(results),
         scratch_shapes=[pltpu.VMEM(*r) for r in results + kept] + [pltpu.VMEM((nc, nx, ny, nz) + tile, BF16)] * 4 + [pltpu.VMEM(w + tile, BF16) for w in work] * 4
-        + [pltpu.SemaphoreType.DMA((k,)) for k in (8, 2, 11)] + sems,
+        + [pltpu.SemaphoreType.DMA((k,)) for k in (8, 2, len(results))] + sems,
         compiler_params=pltpu.CompilerParams(collective_id=0, has_side_effects=True, vmem_limit_bytes=VMEM_LIMIT),
         name='block',
     )(tokens, grad_out, ids, w_gate, w1, w2)
 
 
 VMEM_LIMIT = 67043328
-SCHEDULE = 'mttmttmgttgtttgtmth' + 'fgfgyfgyfgy' + 'gygy' + 'bybybyBBxbyxBBxy' + 'wwxxwxwwxyc' + 'xwwdxdxwddkxe'
+SCHEDULE = 'mttmttmgttttgttgmth' + 'fggfgyfgyfy' + 'gygy' + 'bybybyBBxbyxBBxy' + 'wwxxwxwwxyc' + 'xwwdxdxwddkxe'
 
 
 def pass_kernel(n, *refs):

time: 90.8 us -> 88.8 us (0.978)
  Pallas kernels: 89.8 us -> 87.8 us
    pallas_call x1, Pallas kernels: 87.1 us -> 85.1 us  [block_call(): pl.pallas_call(functools.partial(block_kernel, dims, (6, len(results), le...]
where the time goes in v14:
time: 88.8 us; the launch traced here: 88.6 us
  Pallas kernels  87.8 us (99%)
    pallas_call x1, Pallas kernels, block_call(): pl.pallas_call(functools.partial(block_kernel, dims, (6, len(results), le...  85.1 us
    pallas_call x1, Pallas kernels, pass_on(): pl.pallas_call(functools.partial(pass_kernel, n), out_shape=[jax.ShapeDty...  2.74 us

profile of v14, /device:TPU:1, one launch (start us, length us, event | category | flops | bytes accessed | tf_op | source)
XLA Modules:
  0.0 88.6 jit_solution(1012226800653779455)
XLA Ops:
  0.6 85.1 %block.1 = (bf16[32,256]{1,0:T(8,128)(2,1)}, bf16[32,256]{1,0:T(8,128)(2,1)}, f32[256,256]{1,0:T(8,128)}, f32[256,1024]{1,0:T(8,128)}, f32[1024,256]{1,0:T(8,128)}) custom-call(bf16[32,256]{1,0:T(8,128)(2,1)} %refs_0_.1, bf16[32,256]{1,0:T(8,128)(2,1)} %refs_1_.1, s32[2,32]{1,0:T(2,128)} %bitcast.7, bf16[256,256]{1,0:T(8,128)(2,1)} %refs_3_.1, ...), custom_call_target="tpu_custom_call" | custom-call | tf_op jit(solution)/shard_map/block/pallas_call | solution.py:568
  85.7 2.7 %pass_on.1 = (bf16[32,256]{1,0:T(8,128)(2,1)}, bf16[32,256]{1,0:T(8,128)(2,1)}, f32[256,256]{1,0:T(8,128)}, f32[256,1024]{1,0:T(8,128)}, f32[1024,256]{1,0:T(8,128)}) custom-call(bf16[32,256]{1,0:T(8,128)(2,1)} %get-tuple-element.15.refs_0_, bf16[32,256]{1,0:T(8,128)(2,1)} %get-tuple-element.16.refs_1_, f32[256,256]{1,0:T(8,128)} %get-tuple-element.17.refs_2_, ...), custom_call_target="tpu_custom_call" | custom-call | tf_op jit(solution)/shard_map/pass_on/pallas_call | solution.py:600

commit v15 on v14

--- a/solution.py
+++ b/solution.py
@@ -578,7 +578,7 @@
 
 
 VMEM_LIMIT = 67043328
-SCHEDULE = 'mttmttmgttttgttgmth' + 'fggfgyfgyfy' + 'gygy' + 'bybybyBBxbyxBBxy' + 'wwxxwxwwxyc' + 'xwwdxdxwddkxe'
+SCHEDULE = 'mttmttmgttttgttgmth' + 'ffggyfggyfy' + 'gygy' + 'bybyBBxbybyBBxxwwxwyxwxxwwxyc' + 'xwxddwddkxe'
 
 
 def pass_kernel(n, *refs):

time: 88.8 us -> 91.3 us (1.028)
  Pallas kernels: 87.8 us -> 90.4 us
    pallas_call x1, Pallas kernels: 85.1 us -> 87.6 us  [block_call(): pl.pallas_call(functools.partial(block_kernel, dims, (6, len(results), le...]
where the time goes in v15:
time: 91.3 us; the launch traced here: 91.2 us
  Pallas kernels  90.4 us (99%)
    pallas_call x1, Pallas kernels, block_call(): pl.pallas_call(functools.partial(block_kernel, dims, (6, len(results), le...  87.6 us
    pallas_call x1, Pallas kernels, pass_on(): pl.pallas_call(functools.partial(pass_kernel, n), out_shape=[jax.ShapeDty...  2.74 us

profile of v15, /device:TPU:1, one launch (start us, length us, event | category | flops | bytes accessed | tf_op | source)
XLA Modules:
  0.0 91.2 jit_solution(14818348190285190524)
XLA Ops:
  0.6 87.6 %block.1 = (bf16[32,256]{1,0:T(8,128)(2,1)}, bf16[32,256]{1,0:T(8,128)(2,1)}, f32[256,256]{1,0:T(8,128)}, f32[256,1024]{1,0:T(8,128)}, f32[1024,256]{1,0:T(8,128)}) custom-call(bf16[32,256]{1,0:T(8,128)(2,1)} %refs_0_.1, bf16[32,256]{1,0:T(8,128)(2,1)} %refs_1_.1, s32[2,32]{1,0:T(2,128)} %bitcast.7, bf16[256,256]{1,0:T(8,128)(2,1)} %refs_3_.1, ...), custom_call_target="tpu_custom_call" | custom-call | tf_op jit(solution)/shard_map/block/pallas_call | solution.py:568
  88.3 2.7 %pass_on.1 = (bf16[32,256]{1,0:T(8,128)(2,1)}, bf16[32,256]{1,0:T(8,128)(2,1)}, f32[256,256]{1,0:T(8,128)}, f32[256,1024]{1,0:T(8,128)}, f32[1024,256]{1,0:T(8,128)}) custom-call(bf16[32,256]{1,0:T(8,128)(2,1)} %get-tuple-element.15.refs_0_, bf16[32,256]{1,0:T(8,128)(2,1)} %get-tuple-element.16.refs_1_, f32[256,256]{1,0:T(8,128)} %get-tuple-element.17.refs_2_, ...), custom_call_target="tpu_custom_call" | custom-call | tf_op jit(solution)/shard_map/pass_on/pallas_call | solution.py:600

commit v16 on v14

--- a/solution.py
+++ b/solution.py
@@ -131,7 +131,7 @@
     refs = [list(itertools.islice(refs, n)) for n in sizes]
     (tok_hbm, dout_hbm, ids_hbm, wg_hbm, w1_hbm, w2_hbm), outs, held, kept, rows, areas, (load_sem, keep_sem, save_sem), sems = refs
     out_ref, gx_ref, gate_ref, g1_ref, g2_ref = held
-    tok, dout, ids, wg, w1, w2, row, m_land, x_all, g_all, xs_ref, dys_ref, h_ref, da_ref, a_ref, m_all, hot_ref, d_row, d_land, d_all, pad, pad_row = kept
+    tok, dout, ids, wg, w1, w2, row, m_land, x_all, g_all, xs_ref, dys_ref, h_ref, da_ref, a_ref, m_all, hot_ref, d_land, d_all, pad, pad_row = kept
     z, y, x, c, dev = coords(dims)
     saves = [pltpu.make_async_copy(held[k], outs[k], save_sem.at[k]) for k in range(len(held))]
 
@@ -414,7 +414,7 @@
         line = iota((8, 128), 0)
         mine = [(wide(is_hot[0][k] + is_hot[1][k] + is_hot[2][k]) < 0.5) & (line == s * nc + e) for k, (s, e) in enumerate(places)]
 
-        def squeeze(bb, carry):
+        def squeeze(bb):
             given = [h[index((c,), a, bb)], other[index((), a, bb)]] + [near[s, e, bb] for s, e in places[2:]]
             for j in range(3):
                 out2[bb, j] = sum(given[k] * weight[j][k] for k in range(8))
@@ -422,14 +422,16 @@
             for k in range(8):
                 singles = jnp.where(mine[k], jnp.sum(given[k].astype(F32), axis=1, keepdims=True), singles)
             out2[bb, 3] = singles.astype(BF16)
-            return carry
-
-        lax.fori_loop(0, 4, squeeze, 0)
+
         up, dn, far = step(b, 1), step(b, 3), step(b, 2)
         lo, hi = pl.ds(0, nz // 2), pl.ds(nz // 2, nz // 2)
+        squeeze(far)
+        squeeze(up)
         go(out2.at[far, :, lo], via2.at[0], to(a, up), in_v)
         go(out2.at[far, :, hi], via2.at[1], to(a, dn), in_v)
+        squeeze(dn)
         go(out2.at[up], in2.at[b], to(a, up), in_2)
+        squeeze(b)
         go(out2.at[dn], in2.at[b], to(a, dn), in_2)
         in2[b] = out2[b]
         yield
@@ -438,11 +440,13 @@
         go(via2.at[1], in2.at[up, :, hi], to(a, dn), in_2)
         yield
         link.wait(in_2, in2.at[pl.ds(0, 3)])
+        for d in by_distance:
+            zz = lax.rem(z + d, nz)
+            go(in2.at[:, 3, zz], cold_land.at[z], dev(zz, y, x, c), in_s)
         for j in range(3):
             out3[:, j] = (in2[0, j] + in2[1, j]) + (in2[2, j] + in2[3, j])
         for d in by_distance:
             zz = lax.rem(z + d, nz)
-            go(in2.at[:, 3, zz], cold_land.at[z], dev(zz, y, x, c), in_s)
             go(out3.at[zz], hot_land.at[z], dev(zz, y, x, c), in_l)
         cold_land[z] = in2[:, 3, z]
         hot_land[z] = out3[z]
@@ -497,12 +501,9 @@
         dg0, dg1 = (jnp.sum(grad * v, axis=1, keepdims=True) for v in (y0, y1))
         mean = g0 * dg0 + g1 * dg1
         d0, d1 = ((g * (dg - mean)).astype(BF16).astype(F32) for g, dg in ((g0, dg0), (g1, dg1)))
-        d_row[...] = jnp.concatenate([as_row(d0), as_row(d1), jnp.zeros((1, 2 * n_tok), F32)], axis=1)
-        place = pltpu.make_async_copy(d_row, d_land.at[z, y, x, c], keep_sem.at[1])
-        place.start()
+        d_land[z, y, x, c] = jnp.concatenate([as_row(d0), as_row(d1), jnp.zeros((1, 2 * n_tok), F32)], axis=1)
         out_ref[...] = (g0 * y0 + g1 * y1).astype(BF16)
         saves[0].start()
-        place.wait()
         d_plans.append(gather_rows(next(links), d_land, range(4)))
         advance(d_plans)
         expert = iota((n_tok, n_exp), 1).astype(F32)
@@ -563,7 +564,7 @@
     results = [(tokens.shape, BF16), (tokens.shape, BF16), ((d_model, n_dev), F32), ((d_model, d_hidden), F32), ((d_hidden, d_model), F32)]
     row = (1, 128)
     kept = [(tokens.shape, BF16), (tokens.shape, BF16), (ids.shape, jnp.int32), (w_gate.shape, BF16), (w1.shape, BF16), (w2.shape, BF16), (row, F32), (dims + row, F32),
-            (dims + tokens.shape, BF16), (dims + tokens.shape, BF16), ((n_row, d_model), BF16), ((n_row, d_model), BF16), ((n_row, d_hidden), BF16), ((n_row, d_hidden), BF16), ((n_row, d_hidden), F32), ((n_dev, 128), F32), (tile, F32), (row, F32),
+            (dims + tokens.shape, BF16), (dims + tokens.shape, BF16), ((n_row, d_model), BF16), ((n_row, d_model), BF16), ((n_row, d_hidden), BF16), ((n_row, d_hidden), BF16), ((n_row, d_hidden), F32), ((n_dev, 128), F32), (tile, F32),
             (dims + row, F32), ((n_dev, 128), F32), ((1024,) + tile, BF16), ((n_dev,) + row, F32)]
     return pl.pallas_call(
         functools.partial(block_kernel, dims, (6, len(results), len(results), len(kept), 4, 4 * len(work), 3, len(sems))),
@@ -571,7 +572,7 @@
         in_specs=[hbm] * 6,
         out_specs=[hbm] * len(results),
         scratch_shapes=[pltpu.VMEM(*r) for r in results + kept] + [pltpu.VMEM((nc, nx, ny, nz) + tile, BF16)] * 4 + [pltpu.VMEM(w + tile, BF16) for w in work] * 4
-        + [pltpu.SemaphoreType.DMA((k,)) for k in (8, 2, len(results))] + sems,
+        + [pltpu.SemaphoreType.DMA((k,)) for k in (8, 1, len(results))] + sems,
         compiler_params=pltpu.CompilerParams(collective_id=0, has_side_effects=True, vmem_limit_bytes=VMEM_LIMIT),
         name='block',
     )(tokens, grad_out, ids, w_gate, w1, w2)

time: 88.8 us -> 87.8 us (0.989)
  Pallas kernels: 87.8 us -> 86.8 us
    pallas_call x1, Pallas kernels: 85.1 us -> 84 us  [block_call(): pl.pallas_call(functools.partial(block_kernel, dims, (6, len(results), le...]
where the time goes in v16:
time: 87.8 us; the launch traced here: 87.6 us
  Pallas kernels  86.8 us (99%)
    pallas_call x1, Pallas kernels, block_call(): pl.pallas_call(functools.partial(block_kernel, dims, (6, len(results), le...  84 us
    pallas_call x1, Pallas kernels, pass_on(): pl.pallas_call(functools.partial(pass_kernel, n), out_shape=[jax.ShapeDty...  2.74 us

profile of v16, /device:TPU:1, one launch (start us, length us, event | category | flops | bytes accessed | tf_op | source)
XLA Modules:
  0.0 87.6 jit_solution(14484773158572372025)
XLA Ops:
  0.6 84.0 %block.1 = (bf16[32,256]{1,0:T(8,128)(2,1)}, bf16[32,256]{1,0:T(8,128)(2,1)}, f32[256,256]{1,0:T(8,128)}, f32[256,1024]{1,0:T(8,128)}, f32[1024,256]{1,0:T(8,128)}) custom-call(bf16[32,256]{1,0:T(8,128)(2,1)} %refs_0_.1, bf16[32,256]{1,0:T(8,128)(2,1)} %refs_1_.1, s32[2,32]{1,0:T(2,128)} %bitcast.7, bf16[256,256]{1,0:T(8,128)(2,1)} %refs_3_.1, ...), custom_call_target="tpu_custom_call" | custom-call | tf_op jit(solution)/shard_map/block/pallas_call | solution.py:569
  84.7 2.7 %pass_on.1 = (bf16[32,256]{1,0:T(8,128)(2,1)}, bf16[32,256]{1,0:T(8,128)(2,1)}, f32[256,256]{1,0:T(8,128)}, f32[256,1024]{1,0:T(8,128)}, f32[1024,256]{1,0:T(8,128)}) custom-call(bf16[32,256]{1,0:T(8,128)(2,1)} %get-tuple-element.15.refs_0_, bf16[32,256]{1,0:T(8,128)(2,1)} %get-tuple-element.16.refs_1_, f32[256,256]{1,0:T(8,128)} %get-tuple-element.17.refs_2_, ...), custom_call_target="tpu_custom_call" | custom-call | tf_op jit(solution)/shard_map/pass_on/pallas_call | solution.py:601

commit v17 on v16

--- a/solution.py
+++ b/solution.py
@@ -318,9 +318,10 @@
         src = (iota((n_pair, 256), 1) // 32).astype(F32)
         key = jnp.where(hit > 0.0, src * CAP + rank, -1.0)
         slot = iota((8 * CAP, 256), 0).astype(F32)
+        short, key_short, one = slot.astype(BF16), key.astype(BF16), jnp.ones((), BF16)
         parts = []
         for p in range(n_pair):
-            sel = (slot == key[p:p + 1]).astype(F32)
+            sel = (slot == key[p:p + 1]).astype(F32) if with_gate else jnp.where(short == key_short[p:p + 1], one, one - one)
             v = dot(sel.astype(BF16), ref[i * per + p // ny, p % ny].reshape(256, 256), 1, 0)
             parts.append(v * jnp.sum(sel * gate[p:p + 1], axis=1, keepdims=True) if with_gate else v)
         return jnp.concatenate([parts[zz * ny + yy][CAP * (xx * nc + cc):CAP * (xx * nc + cc + 1)] for cc, xx, yy, zz in places], axis=0).astype(BF16)
@@ -519,16 +520,17 @@
 
     def gate_grad():
         flatten(d_land, d_all)
-        expert = iota((n_exp, 256), 0).astype(F32)
-        codes = [plain_id(pair_rows(token_lanes(m_all, k, 0, n_dev // 4))) for k in range(2)]
-        grads = [pair_rows(token_lanes(d_all, k, 0, n_dev // 4)) for k in range(2)]
+        expert = iota((n_exp, 256), 0).astype(F32).astype(BF16)
+        codes = [plain_id(pair_rows(token_lanes(m_all, k, 0, n_dev // 4))).astype(BF16) for k in range(2)]
+        grads = [pair_rows(token_lanes(d_all, k, 0, n_dev // 4)).astype(BF16) for k in range(2)]
+        none = jnp.zeros((), BF16)
         total = jnp.zeros((n_exp, x_all.shape[-1]), F32)
         zs = nz // 4 or 1
         for z0 in range(0, nz, zs):
             spread = []
             for p in range(z0 * ny, (z0 + zs) * ny):
                 q = slice(p, p + 1)
-                spread.append(jnp.where(expert == codes[0][q], grads[0][q], jnp.where(expert == codes[1][q], grads[1][q], 0.0)).astype(BF16))
+                spread.append(jnp.where(expert == codes[0][q], grads[0][q], jnp.where(expert == codes[1][q], grads[1][q], none)))
             total += dot(jnp.concatenate(spread, axis=1), x_all[z0:z0 + zs].reshape(zs * ny * 256, x_all.shape[-1]), 1, 0)
         gate_ref[...] = total.T
         saves[2].start()

time: 87.8 us -> 87.8 us (level)
  no operation moved by 1% of the time
where the time goes in v17:
time: 87.8 us; the launch traced here: 87.6 us
  Pallas kernels  86.8 us (99%)
    pallas_call x1, Pallas kernels, block_call(): pl.pallas_call(functools.partial(block_kernel, dims, (6, len(results), le...  84.1 us
    pallas_call x1, Pallas kernels, pass_on(): pl.pallas_call(functools.partial(pass_kernel, n), out_shape=[jax.ShapeDty...  2.74 us

profile of v17, /device:TPU:1, one launch (start us, length us, event | category | flops | bytes accessed | tf_op | source)
XLA Modules:
  0.0 87.6 jit_solution(14291478422466255574)
XLA Ops:
  0.6 84.1 %block.1 = (bf16[32,256]{1,0:T(8,128)(2,1)}, bf16[32,256]{1,0:T(8,128)(2,1)}, f32[256,256]{1,0:T(8,128)}, f32[256,1024]{1,0:T(8,128)}, f32[1024,256]{1,0:T(8,128)}) custom-call(bf16[32,256]{1,0:T(8,128)(2,1)} %refs_0_.1, bf16[32,256]{1,0:T(8,128)(2,1)} %refs_1_.1, s32[2,32]{1,0:T(2,128)} %bitcast.7, bf16[256,256]{1,0:T(8,128)(2,1)} %refs_3_.1, ...), custom_call_target="tpu_custom_call" | custom-call | tf_op jit(solution)/shard_map/block/pallas_call | solution.py:571
  84.7 2.7 %pass_on.1 = (bf16[32,256]{1,0:T(8,128)(2,1)}, bf16[32,256]{1,0:T(8,128)(2,1)}, f32[256,256]{1,0:T(8,128)}, f32[256,1024]{1,0:T(8,128)}, f32[1024,256]{1,0:T(8,128)}) custom-call(bf16[32,256]{1,0:T(8,128)(2,1)} %get-tuple-element.15.refs_0_, bf16[32,256]{1,0:T(8,128)(2,1)} %get-tuple-element.16.refs_1_, f32[256,256]{1,0:T(8,128)} %get-tuple-element.17.refs_2_, ...), custom_call_target="tpu_custom_call" | custom-call | tf_op jit(solution)/shard_map/pass_on/pallas_call | solution.py:603

commit v18 on v17

--- a/solution.py
+++ b/solution.py
@@ -581,7 +581,7 @@
 
 
 VMEM_LIMIT = 67043328
-SCHEDULE = 'mttmttmgttttgttgmth' + 'fggfgyfgyfy' + 'gygy' + 'bybybyBBxbyxBBxy' + 'wwxxwxwwxyc' + 'xwwdxdxwddkxe'
+SCHEDULE = 'mttmttmgttttgttgmth' + 'ffggyfggyfy' + 'gygy' + 'bybybyBBxbyxBBxy' + 'wwxxwxwwxyc' + 'xwwdxdxwddkxe'
 
 
 def pass_kernel(n, *refs):

time: 87.8 us -> 87.6 us (level)
  no operation moved by 1% of the time
where the time goes in v18:
time: 87.6 us; the launch traced here: 87.4 us
  Pallas kernels  86.6 us (99%)
    pallas_call x1, Pallas kernels, block_call(): pl.pallas_call(functools.partial(block_kernel, dims, (6, len(results), le...  83.9 us
    pallas_call x1, Pallas kernels, pass_on(): pl.pallas_call(functools.partial(pass_kernel, n), out_shape=[jax.ShapeDty...  2.74 us

profile of v18, /device:TPU:1, one launch (start us, length us, event | category | flops | bytes accessed | tf_op | source)
XLA Modules:
  0.0 87.4 jit_solution(220874742819454462)
XLA Ops:
  0.6 83.9 %block.1 = (bf16[32,256]{1,0:T(8,128)(2,1)}, bf16[32,256]{1,0:T(8,128)(2,1)}, f32[256,256]{1,0:T(8,128)}, f32[256,1024]{1,0:T(8,128)}, f32[1024,256]{1,0:T(8,128)}) custom-call(bf16[32,256]{1,0:T(8,128)(2,1)} %refs_0_.1, bf16[32,256]{1,0:T(8,128)(2,1)} %refs_1_.1, s32[2,32]{1,0:T(2,128)} %bitcast.7, bf16[256,256]{1,0:T(8,128)(2,1)} %refs_3_.1, ...), custom_call_target="tpu_custom_call" | custom-call | tf_op jit(solution)/shard_map/block/pallas_call | solution.py:571
  84.5 2.7 %pass_on.1 = (bf16[32,256]{1,0:T(8,128)(2,1)}, bf16[32,256]{1,0:T(8,128)(2,1)}, f32[256,256]{1,0:T(8,128)}, f32[256,1024]{1,0:T(8,128)}, f32[1024,256]{1,0:T(8,128)}) custom-call(bf16[32,256]{1,0:T(8,128)(2,1)} %get-tuple-element.15.refs_0_, bf16[32,256]{1,0:T(8,128)(2,1)} %get-tuple-element.16.refs_1_, f32[256,256]{1,0:T(8,128)} %get-tuple-element.17.refs_2_, ...), custom_call_target="tpu_custom_call" | custom-call | tf_op jit(solution)/shard_map/pass_on/pallas_call | solution.py:603

commit v19 on v18

--- a/solution.py
+++ b/solution.py
@@ -275,7 +275,7 @@
     halves = [slice(0, 16), slice(16, 32)]
     tok_plans, grad_plans = [[by_lines(next(links), ref, half, half.start == 0, ref is g_all) for half in halves] for ref in (x_all, g_all)]
     row_plan = [gather_rows(next(links), m_land, range(4))]
-    advance(row_plan + tok_plans + grad_plans)
+    advance(row_plan + tok_plans)
     def flatten(land, flat):
         def lines(zz, carry):
             for k in range(ny * nx * nc):
@@ -581,7 +581,7 @@
 
 
 VMEM_LIMIT = 67043328
-SCHEDULE = 'mttmttmgttttgttgmth' + 'ffggyfggyfy' + 'gygy' + 'bybybyBBxbyxBBxy' + 'wwxxwxwwxyc' + 'xwwdxdxwddkxe'
+SCHEDULE = 'mtgtmttmgttttgttgmth' + 'ffggyfggyfy' + 'gygy' + 'bybybyBBxbyxBBxy' + 'wwxxwxwwxyc' + 'xwwdxdxwddkxe'
 
 
 def pass_kernel(n, *refs):

time: 87.6 us -> 86.7 us (0.990)
  Pallas kernels: 86.6 us -> 85.7 us
where the time goes in v19:
time: 86.7 us; the launch traced here: 86.5 us
  Pallas kernels  85.7 us (99%)
    pallas_call x1, Pallas kernels, block_call(): pl.pallas_call(functools.partial(block_kernel, dims, (6, len(results), le...  83 us
    pallas_call x1, Pallas kernels, pass_on(): pl.pallas_call(functools.partial(pass_kernel, n), out_shape=[jax.ShapeDty...  2.74 us

profile of v19, /device:TPU:1, one launch (start us, length us, event | category | flops | bytes accessed | tf_op | source)
XLA Modules:
  0.0 86.5 jit_solution(11089723739632513369)
XLA Ops:
  0.6 83.0 %block.1 = (bf16[32,256]{1,0:T(8,128)(2,1)}, bf16[32,256]{1,0:T(8,128)(2,1)}, f32[256,256]{1,0:T(8,128)}, f32[256,1024]{1,0:T(8,128)}, f32[1024,256]{1,0:T(8,128)}) custom-call(bf16[32,256]{1,0:T(8,128)(2,1)} %refs_0_.1, bf16[32,256]{1,0:T(8,128)(2,1)} %refs_1_.1, s32[2,32]{1,0:T(2,128)} %bitcast.7, bf16[256,256]{1,0:T(8,128)(2,1)} %refs_3_.1, ...), custom_call_target="tpu_custom_call" | custom-call | tf_op jit(solution)/shard_map/block/pallas_call | solution.py:571
  83.6 2.7 %pass_on.1 = (bf16[32,256]{1,0:T(8,128)(2,1)}, bf16[32,256]{1,0:T(8,128)(2,1)}, f32[256,256]{1,0:T(8,128)}, f32[256,1024]{1,0:T(8,128)}, f32[1024,256]{1,0:T(8,128)}) custom-call(bf16[32,256]{1,0:T(8,128)(2,1)} %get-tuple-element.15.refs_0_, bf16[32,256]{1,0:T(8,128)(2,1)} %get-tuple-element.16.refs_1_, f32[256,256]{1,0:T(8,128)} %get-tuple-element.17.refs_2_, ...), custom_call_target="tpu_custom_call" | custom-call | tf_op jit(solution)/shard_map/pass_on/pallas_call | solution.py:603

commit v20 on v19

--- a/solution.py
+++ b/solution.py
@@ -581,7 +581,7 @@
 
 
 VMEM_LIMIT = 67043328
-SCHEDULE = 'mtgtmttmgttttgttgmth' + 'ffggyfggyfy' + 'gygy' + 'bybybyBBxbyxBBxy' + 'wwxxwxwwxyc' + 'xwwdxdxwddkxe'
+SCHEDULE = 'mtgtmttmtgtttgttgmth' + 'ffggyfggyfy' + 'gygy' + 'bybybyBBxbyxBBxy' + 'wwxxwxwwxyc' + 'xwwdxdxwddkxe'
 
 
 def pass_kernel(n, *refs):

time: 86.7 us -> 86.7 us (level)
  no operation moved by 1% of the time
where the time goes in v20:
time: 86.7 us; the launch traced here: 86.6 us
  Pallas kernels  85.8 us (99%)
    pallas_call x1, Pallas kernels, block_call(): pl.pallas_call(functools.partial(block_kernel, dims, (6, len(results), le...  83 us
    pallas_call x1, Pallas kernels, pass_on(): pl.pallas_call(functools.partial(pass_kernel, n), out_shape=[jax.ShapeDty...  2.74 us

profile of v20, /device:TPU:1, one launch (start us, length us, event | category | flops | bytes accessed | tf_op | source)
XLA Modules:
  0.0 86.6 jit_solution(128366131468102409)
XLA Ops:
  0.6 83.0 %block.1 = (bf16[32,256]{1,0:T(8,128)(2,1)}, bf16[32,256]{1,0:T(8,128)(2,1)}, f32[256,256]{1,0:T(8,128)}, f32[256,1024]{1,0:T(8,128)}, f32[1024,256]{1,0:T(8,128)}) custom-call(bf16[32,256]{1,0:T(8,128)(2,1)} %refs_0_.1, bf16[32,256]{1,0:T(8,128)(2,1)} %refs_1_.1, s32[2,32]{1,0:T(2,128)} %bitcast.7, bf16[256,256]{1,0:T(8,128)(2,1)} %refs_3_.1, ...), custom_call_target="tpu_custom_call" | custom-call | tf_op jit(solution)/shard_map/block/pallas_call | solution.py:571
  83.6 2.7 %pass_on.1 = (bf16[32,256]{1,0:T(8,128)(2,1)}, bf16[32,256]{1,0:T(8,128)(2,1)}, f32[256,256]{1,0:T(8,128)}, f32[256,1024]{1,0:T(8,128)}, f32[1024,256]{1,0:T(8,128)}) custom-call(bf16[32,256]{1,0:T(8,128)(2,1)} %get-tuple-element.15.refs_0_, bf16[32,256]{1,0:T(8,128)(2,1)} %get-tuple-element.16.refs_1_, f32[256,256]{1,0:T(8,128)} %get-tuple-element.17.refs_2_, ...), custom_call_target="tpu_custom_call" | custom-call | tf_op jit(solution)/shard_map/pass_on/pallas_call | solution.py:603

commit v21 on v20

--- a/solution.py
+++ b/solution.py
@@ -581,7 +581,7 @@
 
 
 VMEM_LIMIT = 67043328
-SCHEDULE = 'mtgtmttmtgtttgttgmth' + 'ffggyfggyfy' + 'gygy' + 'bybybyBBxbyxBBxy' + 'wwxxwxwwxyc' + 'xwwdxdxwddkxe'
+SCHEDULE = 'mtgtmtttmgtttgttgmth' + 'ffggyfggyfy' + 'gygy' + 'bybybyBBxbyxBBxy' + 'wwxxwxwwxyc' + 'xwwdxdxwddkxe'
 
 
 def pass_kernel(n, *refs):

time: 86.7 us -> 86.8 us (level)
  no operation moved by 1% of the time
where the time goes in v21:
time: 86.8 us; the launch traced here: 86.6 us
  Pallas kernels  85.8 us (99%)
    pallas_call x1, Pallas kernels, block_call(): pl.pallas_call(functools.partial(block_kernel, dims, (6, len(results), le...  83.1 us
    pallas_call x1, Pallas kernels, pass_on(): pl.pallas_call(functools.partial(pass_kernel, n), out_shape=[jax.ShapeDty...  2.74 us

profile of v21, /device:TPU:1, one launch (start us, length us, event | category | flops | bytes accessed | tf_op | source)
XLA Modules:
  0.0 86.6 jit_solution(6538256423611362982)
XLA Ops:
  0.6 83.1 %block.1 = (bf16[32,256]{1,0:T(8,128)(2,1)}, bf16[32,256]{1,0:T(8,128)(2,1)}, f32[256,256]{1,0:T(8,128)}, f32[256,1024]{1,0:T(8,128)}, f32[1024,256]{1,0:T(8,128)}) custom-call(bf16[32,256]{1,0:T(8,128)(2,1)} %refs_0_.1, bf16[32,256]{1,0:T(8,128)(2,1)} %refs_1_.1, s32[2,32]{1,0:T(2,128)} %bitcast.7, bf16[256,256]{1,0:T(8,128)(2,1)} %refs_3_.1, ...), custom_call_target="tpu_custom_call" | custom-call | tf_op jit(solution)/shard_map/block/pallas_call | solution.py:571
  83.7 2.7 %pass_on.1 = (bf16[32,256]{1,0:T(8,128)(2,1)}, bf16[32,256]{1,0:T(8,128)(2,1)}, f32[256,256]{1,0:T(8,128)}, f32[256,1024]{1,0:T(8,128)}, f32[1024,256]{1,0:T(8,128)}) custom-call(bf16[32,256]{1,0:T(8,128)(2,1)} %get-tuple-element.15.refs_0_, bf16[32,256]{1,0:T(8,128)(2,1)} %get-tuple-element.16.refs_1_, f32[256,256]{1,0:T(8,128)} %get-tuple-element.17.refs_2_, ...), custom_call_target="tpu_custom_call" | custom-call | tf_op jit(solution)/shard_map/pass_on/pallas_call | solution.py:603
